TPU v7x, 32 devices: a whole 2x2x4 slice. The times are simulated.
32 devices in a mesh: dp: 4 (over z), seq: 4 (over y, x), tensor: 2 (over core).
Axes of the slice: x: 2, y: 2, z: 4, core: 2. Of those that a mesh axis runs over, the one named last changes fastest.
Arguments:
- tokens: bfloat16 [1088, 12, 384], P(('seq', 'tensor'), 'dp'), may hold values from -16 to 16
- out_grad: float32 [1088, 12, 384], P('seq', 'dp'), may hold values from -6 to 6
- keep_mask: int32 [1088, 12], P(None, 'dp'), may hold values from 0 to 1, as said below
- w_qkv: float32 [3, 384, 384], P(None, None, 'tensor'), may hold values from -0.3125 to 0.3125
- w_out: float32 [384, 384], P('tensor'), may hold values from -6 to 6
- w_gate_up: float32 [2, 384, 1024], P(None, None, 'tensor'), may hold values from -0.3125 to 0.3125
- w_down: float32 [1024, 384], P('tensor'), may hold values from -0.1875 to 0.1875
- norm_pack: float32 [4, 384], replicated, may hold values from -1.5 to 1.75
- inner_pack: float32 [2, 1024], P(None, 'tensor'), may hold values from -1.5 to 1.75
- moment_qkv: float32 [3, 384, 384], P(None, None, 'tensor'), may hold values from -0.6 to 0.6
- moment_out: float32 [384, 384], P('tensor'), may hold values from -0.6 to 0.6
- moment_gate_up: float32 [2, 384, 1024], P(None, None, 'tensor'), may hold values from -0.6 to 0.6
- moment_down: float32 [1024, 384], P('tensor'), may hold values from -0.6 to 0.6
- moment_norm: float32 [4, 384], replicated, may hold values from -0.6 to 0.6
- moment_inner: float32 [2, 1024], P(None, 'tensor'), may hold values from -0.6 to 0.6
- error_qkv: float32 [16, 3, 384, 384], P(('dp', 'seq'), None, None, 'tensor'), may hold values from -5 to 5
- error_out: float32 [16, 384, 384], P(('dp', 'seq'), 'tensor'), may hold values from -5 to 5
- error_gate_up: float32 [16, 2, 384, 1024], P(('dp', 'seq'), None, None, 'tensor'), may hold values from -5 to 5
- error_down: float32 [16, 1024, 384], P(('dp', 'seq'), 'tensor'), may hold values from -5 to 5
- basis_qkv: float32 [3, 384, 8], P(None, 'tensor'), may hold values from -6 to 6
- basis_out: float32 [384, 8], P('tensor'), may hold values from -6 to 6
- basis_gate_up: float32 [2, 1024, 8], P(None, 'tensor'), may hold values from -6 to 6
- basis_down: float32 [1024, 8], P('tensor'), may hold values from -6 to 6
Outputs:
- residual: float32 [1088, 12, 384], P(('seq', 'tensor'), 'dp')
- input_grad: float32 [1088, 12, 384], P(('seq', 'tensor'), 'dp')
- factor_left: float32 [5, 384, 8], replicated
- factor_qkv: float32 [3, 384, 8], P(None, 'tensor')
- factor_out: float32 [384, 8], P('tensor')
- factor_gate_up: float32 [2, 1024, 8], P(None, 'tensor')
- factor_down: float32 [1024, 8], P('tensor')
- new_error_qkv: float32 [16, 3, 384, 384], P(('dp', 'seq'), None, None, 'tensor')
- new_error_out: float32 [16, 384, 384], P(('dp', 'seq'), 'tensor')
- new_error_gate_up: float32 [16, 2, 384, 1024], P(('dp', 'seq'), None, None, 'tensor')
- new_error_down: float32 [16, 1024, 384], P(('dp', 'seq'), 'tensor')
- new_moment_qkv: float32 [3, 384, 384], P(None, None, 'tensor')
- new_moment_out: float32 [384, 384], P('tensor')
- new_moment_gate_up: float32 [2, 384, 1024], P(None, None, 'tensor')
- new_moment_down: float32 [1024, 384], P('tensor')
- new_moment_norm: float32 [4, 384], replicated
- new_moment_inner: float32 [2, 1024], P(None, 'tensor')
- new_w_qkv: float32 [3, 384, 384], P(None, None, 'tensor')
- new_w_out: float32 [384, 384], P('tensor')
- new_w_gate_up: float32 [2, 384, 1024], P(None, None, 'tensor')
- new_w_down: float32 [1024, 384], P('tensor')
- new_norm_pack: float32 [4, 384], replicated
- new_inner_pack: float32 [2, 1024], P(None, 'tensor')
- branch_rms: float32 [2], replicated
Inputs may be any that keep to these rules, and one draw needn't show every extreme that they name: keep_mask is 1 at slot 0 of every image and 0 at every slot after 32 * 32.
All inputs are finite; a program needn't handle non-finite values.
Results may differ from a plain program's by a relative error of at most 0.014.
The roundings to bfloat16 on the way count: a program that leaves them out, or rounds other values in their place, can miss the bound.
Values may be sent and summed in bfloat16 or wider, within the bound.
A program may use at most 192 MiB of HBM per device.

v0:
```python
import functools

import jax
import jax.numpy as jnp
from jax import lax
from jax.experimental import pallas as pl
from jax.experimental.pallas import tpu as pltpu
from jax.sharding import PartitionSpec as P

DH = 64
FF = 1024
GRID = 32
RANK = 8
QUARTER = DH // 4
CHUNK = 16


EPSILON = 1e-06
MOMENTUM = 0.9
STEP_RATE = 0.5
MESH = pl.DeviceIdType.MESH
BF = jnp.bfloat16
F32 = jnp.float32


def split(value):
    high = value.astype(BF)
    return high, (value - high.astype(F32)).astype(BF)


def dot(left, right, dims):
    return lax.dot_general(left, right, (dims, ((), ())), preferred_element_type=F32)


NN = ((1,), (0,))
NT = ((1,), (1,))
TN = ((0,), (0,))


def fine_dot(left, right, dims):
    left_high, left_low = split(left)
    right_high, right_low = split(right)
    return (
        dot(left_high, right_high, dims)
        + dot(left_high, right_low, dims)
        + dot(left_low, right_high, dims)
    )


def gram_schmidt(stack):
    rows = lax.broadcasted_iota(jnp.int32, (1, RANK, 1), 1)
    for index in range(RANK):
        column = stack[:, index : index + 1, :]
        products = jnp.sum(stack * column, -1, keepdims=True)
        scale = lax.rsqrt(products[:, index : index + 1, :] + EPSILON)
        done = column * scale
        rest = stack - (products * scale) * done
        stack = jnp.where(rows < index, stack, jnp.where(rows == index, done, rest))
    return stack


def exchange(axis, size, buffers, sends, receives):
    me = lax.axis_index(axis)
    copies = []
    for step in range(1, size):
        peer = lax.rem(me + step, size)
        for number, buffer in enumerate(buffers):
            copy = pltpu.make_async_remote_copy(
                src_ref=buffer.at[me],
                dst_ref=buffer.at[me],
                send_sem=sends.at[number, step],
                recv_sem=receives.at[number, step],
                device_id={axis: peer},
                device_id_type=MESH,
            )
            copy.start()
            copies.append(copy)
    for copy in copies:
        copy.wait()


def total(buffer, size):
    value = buffer[0]
    for index in range(1, size):
        value = value + buffer[index]
    return value


def greet(axes, barrier):
    count = 0
    for axis, size in axes:
        me = lax.axis_index(axis)
        for step in range(1, size):
            pl.semaphore_signal(
                barrier, inc=1, device_id={axis: lax.rem(me + step, size)}, device_id_type=MESH
            )
            count += 1
    pl.semaphore_wait(barrier, count)


def factor_kernel(sizes, *refs):
    (
        full_qkv, full_out, full_gate_up, full_down,
        basis_qkv, basis_out, basis_gate_up, basis_down, extra, inner,
        left_rows, left_rows_fine, left_cols_fine, extra_sum,
        narrow_rows, narrow_cols_fine, wide_rows, wide_rows_fine, down_cols_fine, inner_sum,
        sum_t, sum_s, sum_d, narrow_s, narrow_d, wide_s, wide_d,
        send_t, recv_t, send_s, recv_s, send_d, recv_d, send_ns, recv_ns, send_nd, recv_nd,
    ) = refs
    nd, ns, nt = sizes
    greet((("tensor", nt), ("seq", ns), ("dp", nd)), pltpu.get_barrier_semaphore())
    me_t, me_s, me_d = (lax.axis_index(axis) for axis in ("tensor", "seq", "dp"))
    own = sum_t.at[me_t]
    own[0:8] = sum(fine_dot(basis_qkv[index], full_qkv[index], NN) for index in range(3))
    own[8:16] = fine_dot(basis_out[...], full_out[...], NN)
    for index in range(2):
        own[16 + 8 * index : 24 + 8 * index] = fine_dot(
            basis_gate_up[index], full_gate_up[index], NT
        )
    own[32:40] = fine_dot(basis_down[...], full_down[...], NN)
    own[40:48] = extra[...]
    exchange("tensor", nt, (sum_t,), send_t, recv_t)
    sum_s[me_s] = total(sum_t, nt)
    exchange("seq", ns, (sum_s,), send_s, recv_s)
    sum_d[me_d] = total(sum_s, ns)
    exchange("dp", nd, (sum_d,), send_d, recv_d)
    summed = total(sum_d, nd)
    share = 1.0 / (ns * nd)
    extra_sum[0:4] = summed[40:44] * share
    extra_sum[4:8] = summed[44:48]
    left = gram_schmidt(summed[0:40].reshape(5, RANK, summed.shape[-1]))
    for index in range(5):
        left_rows[index] = left[index]
        high, low = split(left[index])
        triple = jnp.concatenate([high.astype(F32), high.astype(F32), low.astype(F32)], 0)
        left_rows_fine[index] = triple.astype(BF)
        if index in (2, 3):
            left_cols_fine[index - 2] = jnp.transpose(triple).astype(BF)
    for index in range(3):
        narrow_s[me_s, 8 * index : 8 * index + 8] = fine_dot(left[0], full_qkv[index], NT)
    narrow_s[me_s, 24:32] = fine_dot(left[1], full_out[...], NT)
    for index in range(2):
        wide_s[me_s, 8 * index : 8 * index + 8] = fine_dot(left[2 + index], full_gate_up[index], NN)
    wide_s[me_s, 16:24] = fine_dot(left[4], full_down[...], NT)
    wide_s[me_s, 24:32] = inner[...]
    exchange("seq", ns, (narrow_s, wide_s), send_ns, recv_ns)
    narrow_d[me_d] = total(narrow_s, ns)
    wide_d[me_d] = total(wide_s, ns)
    exchange("dp", nd, (narrow_d, wide_d), send_nd, recv_nd)
    narrow = total(narrow_d, nd) * share
    wide = total(wide_d, nd) * share
    inner_sum[...] = wide[24:32]

    def triple_of(rows):
        high, low = split(rows)
        return jnp.concatenate([high.astype(F32), low.astype(F32), high.astype(F32)], 0)

    for index in range(4):
        part = narrow[8 * index : 8 * index + 8]
        narrow_rows[index] = part
        narrow_cols_fine[index] = jnp.transpose(triple_of(part)).astype(BF)
    for index in range(3):
        part = wide[8 * index : 8 * index + 8]
        wide_rows[index] = part
        if index < 2:
            wide_rows_fine[index] = triple_of(part).astype(BF)
        else:
            down_cols_fine[...] = jnp.transpose(triple_of(part)).astype(BF)


def factors(mesh_sizes, fulls, bases, extra, inner):
    nd, ns, nt = mesh_sizes
    _, narrow, width = fulls[0].shape
    wide = fulls[2].shape[-1]
    shape = jax.ShapeDtypeStruct
    outs = (
        shape((5, RANK, width), F32),
        shape((5, 3 * RANK, width), BF),
        shape((2, width, 3 * RANK), BF),
        shape((8, width), F32),
        shape((4, RANK, narrow), F32),
        shape((4, narrow, 3 * RANK), BF),
        shape((3, RANK, wide), F32),
        shape((2, 3 * RANK, wide), BF),
        shape((wide, 3 * RANK), BF),
        shape((8, wide), F32),
    )
    sems = []
    for count, size in ((1, nt), (1, ns), (1, nd), (2, ns), (2, nd)):
        sems += [pltpu.SemaphoreType.DMA((count, size))] * 2
    vmem = pl.BlockSpec(memory_space=pltpu.VMEM)
    return pl.pallas_call(
        functools.partial(factor_kernel, mesh_sizes),
        out_shape=outs,
        in_specs=[vmem] * 10,
        out_specs=[vmem] * len(outs),
        scratch_shapes=[
            pltpu.VMEM((nt, 48, width), F32),
            pltpu.VMEM((ns, 48, width), F32),
            pltpu.VMEM((nd, 48, width), F32),
            pltpu.VMEM((ns, 32, narrow), F32),
            pltpu.VMEM((nd, 32, narrow), F32),
            pltpu.VMEM((ns, 32, wide), F32),
            pltpu.VMEM((nd, 32, wide), F32),
            *sems,
        ],
        compiler_params=pltpu.CompilerParams(
            collective_id=0, has_side_effects=True, vmem_limit_bytes=24 * 2**20
        ),
        name="factors",
    )(*fulls, *bases, extra, inner)


def update_kernel(*refs):
    (
        full_qkv, full_out, full_gate_up, full_down,
        moment_qkv, moment_out, moment_gate_up, moment_down,
        w_qkv, w_out, w_gate_up, w_down,
        left_rows, left_rows_fine, left_cols_fine, extra_sum,
        narrow_rows, narrow_cols_fine, wide_rows, wide_rows_fine, down_cols_fine, inner_sum,
        norm_pack, moment_norm, inner_pack, moment_inner,
        factor_left, factor_qkv, factor_out, factor_gate_up, factor_down,
        error_qkv, error_out, error_gate_up, error_down,
        new_moment_qkv, new_moment_out, new_moment_gate_up, new_moment_down, new_moment_norm, new_moment_inner,
        new_w_qkv, new_w_out, new_w_gate_up, new_w_down, new_norm_pack, new_inner_pack,
    ) = refs

    def put(approx, full, moment, weight, error, new_moment, new_weight):
        error[...] = full[...] - approx
        fresh = MOMENTUM * moment[...] + approx
        new_moment[...] = fresh
        new_weight[...] = weight[...] - STEP_RATE * fresh

    for index in range(3):
        put(
            dot(narrow_cols_fine[index], left_rows_fine[0], NN),
            *(ref.at[index] for ref in (full_qkv, moment_qkv, w_qkv, error_qkv, new_moment_qkv, new_w_qkv)),
        )
    put(
        dot(narrow_cols_fine[3], left_rows_fine[1], NN),
        full_out, moment_out, w_out, error_out, new_moment_out, new_w_out,
    )
    for index in range(2):
        put(
            dot(left_cols_fine[index], wide_rows_fine[index], NN),
            *(ref.at[index] for ref in (full_gate_up, moment_gate_up, w_gate_up, error_gate_up, new_moment_gate_up, new_w_gate_up)),
        )
    put(
        dot(down_cols_fine[...], left_rows_fine[4], NN),
        full_down, moment_down, w_down, error_down, new_moment_down, new_w_down,
    )

    @pl.when(pl.program_id(0) == 0)
    def _():
        factor_left[...] = left_rows[...]
        factor_qkv[...] = narrow_rows[0:3]
        factor_out[...] = narrow_rows[3]
        factor_gate_up[...] = wide_rows[0:2]
        factor_down[...] = wide_rows[2]
        fresh = MOMENTUM * moment_norm[...] + extra_sum[0:4]
        new_moment_norm[...] = fresh
        new_norm_pack[...] = norm_pack[...] - STEP_RATE * fresh
        fresh = MOMENTUM * moment_inner[...] + inner_sum[0:2]
        new_moment_inner[...] = fresh
        new_inner_pack[...] = inner_pack[...] - STEP_RATE * fresh


def update(fulls, moments, weights, parts, norms):
    steps = 4
    _, narrow, width = fulls[0].shape
    wide = fulls[2].shape[-1]
    part = width // steps

    def whole(array):
        zeros = (0,) * array.ndim
        return pl.BlockSpec(array.shape, lambda step, zeros=zeros: zeros)

    matrices = [
        pl.BlockSpec((3, narrow // steps, width), lambda step: (0, step, 0)),
        pl.BlockSpec((narrow // steps, width), lambda step: (step, 0)),
        pl.BlockSpec((2, part, wide), lambda step: (0, step, 0)),
        pl.BlockSpec((wide // steps, width), lambda step: (step, 0)),
    ]
    specs = [whole(array) for array in parts]
    specs[2] = pl.BlockSpec((2, part, 3 * RANK), lambda step: (0, step, 0))
    specs[5] = pl.BlockSpec((4, narrow // steps, 3 * RANK), lambda step: (0, step, 0))
    specs[8] = pl.BlockSpec((wide // steps, 3 * RANK), lambda step: (step, 0))
    shape = jax.ShapeDtypeStruct
    small = [
        shape((5, RANK, width), F32),
        shape((3, RANK, narrow), F32),
        shape((RANK, narrow), F32),
        shape((2, RANK, wide), F32),
        shape((RANK, wide), F32),
    ]
    like = [shape(array.shape, F32) for array in fulls]
    norm, inner = shape((4, width), F32), shape((2, wide), F32)
    return pl.pallas_call(
        update_kernel,
        grid=(steps,),
        out_shape=[*small, *like, *like, norm, inner, *like, norm, inner],
        in_specs=[*matrices * 3, *specs, *(whole(array) for array in norms)],
        out_specs=[
            *(whole(array) for array in small),
            *matrices * 2,
            whole(norm),
            whole(inner),
            *matrices,
            whole(norm),
            whole(inner),
        ],
        compiler_params=pltpu.CompilerParams(vmem_limit_bytes=48 * 2**20),
        name="update",
    )(*fulls, *moments, *weights, *parts, *norms)


def swap_quarters(value):
    lane = lax.broadcasted_iota(jnp.int32, (1, 128), 1)
    low = lax.rem(lax.div(lane, QUARTER), 2) == 0
    tiles = []
    for start in range(0, value.shape[-1], 128):
        tile = value[:, start : start + 128]
        tiles.append(
            jnp.where(low, pltpu.roll(tile, 128 - QUARTER, 1), pltpu.roll(tile, QUARTER, 1))
        )
    return jnp.concatenate(tiles, -1)


def norm_parts(values, gain, bias):
    centre = values - jnp.mean(values, -1, keepdims=True)
    spread = jnp.mean(centre * centre, -1, keepdims=True)
    inverse = lax.rsqrt(spread + EPSILON)
    normed = centre * inverse
    return (normed * gain + bias, normed, inverse)


def norm_back(grad, normed, inverse, gain):
    scaled = grad * gain
    return inverse * (
        scaled
        - jnp.mean(scaled, -1, keepdims=True)
        - normed * jnp.mean(scaled * normed, -1, keepdims=True)
    )


def column_sums(value):
    return jnp.sum(value, 0, keepdims=True)


def block_kernel(sizes, images, *refs):
    (
        tokens, keep, mask, cosine, sine, norm_pack, inner_pack, w_qkv,
        w_out_hbm, w_gate_up_hbm, w_down_hbm, out_grad_hbm,
        error_qkv_hbm, error_out_hbm, error_gate_up_hbm, error_down_hbm,
        residual, input_grad, full_qkv, full_out, full_gate_up, full_down, extra, inner,
        normed_one, normed_one_all, keys_values, queries, probs, scores, grad_scores,
        attended, attended_low, attended_in, attended_send,
        out_low, gate_up_low, down_low, inner_all, query_low, key_value_low,
        normed_two, grad_middle_low, grad_middle, normed_three, grad_gate, grad_up,
        normed_three_send, grad_gate_send, grad_up_send,
        grad_attended, grad_attended_send, grad_attended_all, grad_query, grad_query_low, grad_pairs,
        pairs_send, pairs_recv, grad_one, grad_one_recv, sum_query, sum_pairs, inner_sums, inner_recv,
        w_out, w_gate_up, w_down, out_grad, error_qkv, error_out, error_gate_up, error_down,
        local_sems, one_send, one_recv, weight_send, weight_recv, pair_send, pair_recv,
        att_send, att_recv, datt_send, datt_recv, rows_send, rows_recv, back_send, back_recv,
        final_send, final_recv,
    ) = refs
    nd, ns, nt = sizes
    me_t, me_s = lax.axis_index("tensor"), lax.axis_index("seq")
    other = 1 - me_t
    own, width = tokens.shape[1], tokens.shape[2]
    seq_rows = 2 * own
    slots = ns * seq_rows
    heads = w_qkv.shape[1] // DH
    hidden_all = 2 * w_down.shape[0]
    scale = (images * seq_rows) ** (-0.5)
    own_rows = pl.ds(pl.multiple_of(me_t * own, 8), own)
    other_rows = pl.ds(pl.multiple_of(other * own, 8), own)

    loads = [
        pltpu.make_async_copy(source, target, local_sems.at[number])
        for number, (source, target) in enumerate(
            (
                (w_out_hbm, w_out), (w_gate_up_hbm, w_gate_up), (w_down_hbm, w_down), (out_grad_hbm, out_grad),
                (error_qkv_hbm, error_qkv), (error_out_hbm, error_out),
                (error_gate_up_hbm, error_gate_up), (error_down_hbm, error_down),
            )
        )
    ]
    for load in loads:
        load.start()

    def to_partner(source, target, send, receive):
        return pltpu.make_async_remote_copy(
            src_ref=source, dst_ref=target, send_sem=send, recv_sem=receive,
            device_id={"tensor": other}, device_id_type=MESH,
        )

    def to_seq(source, target, send, receive, step):
        return pltpu.make_async_remote_copy(
            src_ref=source, dst_ref=target, send_sem=send, recv_sem=receive,
            device_id={"seq": lax.rem(me_s + step, ns)}, device_id_type=MESH,
        )

    def one_copy(image):
        block = normed_one.at[me_t, image]
        return to_partner(block, block, one_send.at[image], one_recv.at[image])

    def weight_copies():
        return [
            to_partner(ref.at[me_t], ref.at[me_t], weight_send.at[number], weight_recv.at[number])
            for number, ref in enumerate((out_low, gate_up_low, down_low, inner_all))
        ]

    def pair_copies(image):
        block = keys_values.at[image, me_s]
        return [
            to_seq(block, block, pair_send.at[image, step], pair_recv.at[image, step], step)
            for step in range(1, ns)
        ]

    def att_copy(image):
        return to_partner(
            attended_send.at[image], attended_in.at[me_t, image], att_send.at[image], att_recv.at[image]
        )

    def datt_copy(image):
        return to_partner(
            grad_attended_send.at[image], grad_attended.at[me_t, image], datt_send.at[image], datt_recv.at[image]
        )

    def row_copies(image):
        moves = (
            (normed_two.at[me_t, image], normed_two),
            (grad_middle_low.at[me_t, image], grad_middle_low),
            (normed_three_send.at[image], normed_three),
            (grad_gate_send.at[image], grad_gate),
            (grad_up_send.at[image], grad_up),
        )
        return [
            to_partner(source, target.at[me_t, image], rows_send.at[image, number], rows_recv.at[image, number])
            for number, (source, target) in enumerate(moves)
        ]

    def back_copies(image):
        return [
            to_seq(
                pairs_send.at[image, lax.rem(me_s + step, ns)], pairs_recv.at[image, step],
                back_send.at[image, step], back_recv.at[image, step], step,
            )
            for step in range(1, ns)
        ]

    def final_copy(image):
        return to_partner(
            grad_one.at[image, other_rows], grad_one_recv.at[image], final_send.at[image], final_recv.at[image]
        )

    def inner_copy():
        return to_partner(
            inner_sums.at[other], inner_recv, final_send.at[images], final_recv.at[images]
        )

    gain_one, bias_one = norm_pack[0:1], norm_pack[1:2]
    gain_two, bias_two = norm_pack[2:3], norm_pack[3:4]

    for image in range(images):
        normed, _, _ = norm_parts(tokens[image].astype(F32), gain_one, bias_one)
        normed_one[me_t, image] = normed.astype(BF)
    greet((("tensor", nt), ("seq", ns)), pltpu.get_barrier_semaphore())
    for image in range(images):
        one_copy(image).start()

    narrow = heads * DH
    pad = jnp.zeros((256 - narrow, width), BF)
    query_low[...] = jnp.concatenate([w_qkv[0].astype(BF), pad], 0)
    key_value_low[0:narrow] = w_qkv[1].astype(BF)
    key_value_low[narrow : 2 * narrow] = w_qkv[2].astype(BF)

    def project(image, carry):
        one_copy(image).wait_recv()
        blocks = [normed_one[half, image] for half in range(2)]
        pairs = jnp.concatenate([dot(block, key_value_low[...], NT) for block in blocks], 0)
        pairs = pairs * cosine[...] + swap_quarters(pairs) * sine[...]
        keys_values[image, me_s] = pairs.astype(BF)
        for copy in pair_copies(image):
            copy.start()
        raw = jnp.concatenate([dot(block, query_low[...], NT) for block in blocks], 0)
        raw = raw * cosine[:, 0:256] + swap_quarters(raw) * sine[:, 0:256]
        raw = raw * (DH ** (-0.5))
        lane = lax.broadcasted_iota(jnp.int32, (1, 128), 1)
        for head in range(heads):
            tile = raw[:, head // 2 * 128 : head // 2 * 128 + 128]
            queries[image * heads + head] = jnp.where(lax.div(lane, DH) == head % 2, tile, 0.0).astype(BF)
        normed_one_all[image] = jnp.concatenate([block.astype(F32) for block in blocks], 0).astype(BF)
        return carry

    lax.fori_loop(0, images, project, 0)

    for load in loads[0:3]:
        load.wait()
    out_low[me_t] = jnp.concatenate([pad, w_out[...].astype(BF)], 0)
    for index in range(2):
        gate_up_low[me_t, index] = w_gate_up[index].astype(BF)
    down_low[me_t] = w_down[...].astype(BF)
    inner_all[me_t] = jnp.zeros_like(inner_all[me_t])
    inner_all[me_t, 0:2] = inner_pack[...]
    for copy in weight_copies():
        copy.start()
    loads[3].wait()
    extra[...] = jnp.zeros_like(extra)
    inner_sums[...] = jnp.zeros_like(inner_sums)

    def half_mask(half):
        lane = lax.broadcasted_iota(jnp.int32, (1, 128), 1)
        return lax.div(lane, DH) == half

    def tile_of(index):
        return pl.ds(pl.multiple_of(index * 128, 128), 128)

    def key_tile(image, index):
        return keys_values[image, :, :, tile_of(index)].reshape(slots, 128)

    def attend(image):
        for copy in pair_copies(image):
            copy.wait_recv()
        bias = jnp.where(keep[pl.ds(image, 1), :] > 0, 0.0, -1e30)
        attended[...] = jnp.zeros_like(attended)

        def head_step(head, carry):
            scores[...] = dot(queries[image * heads + head], key_tile(image, lax.div(head, 2)), NT)
            for start in range(0, seq_rows, CHUNK):
                rows = slice(start, start + CHUNK)
                part = scores[rows] + bias
                part = jnp.exp(part - jnp.max(part, -1, keepdims=True))
                part = part * (1.0 / jnp.sum(part, -1, keepdims=True))
                probs[image * heads + head, rows] = part.astype(BF)
            place = lax.div(head + 1, 2)
            mixed = dot(probs[image * heads + head], key_tile(image, place + 1), NN)
            attended[:, tile_of(place)] += jnp.where(half_mask(lax.rem(head + 1, 2)), mixed, 0.0)
            return carry

        lax.fori_loop(0, heads, head_step, 0)
        attended_low[image] = attended[...].astype(BF)
        attended_in[me_t, image] = attended[own_rows].astype(BF)
        attended_send[image] = attended[other_rows].astype(BF)
        att_copy(image).start()

    def feed(image):
        att_copy(image).wait_recv()
        inputs = tokens[image].astype(F32)
        branch = sum(dot(attended_in[half, image], out_low[half], NN) for half in range(2))
        middle = inputs + branch
        extra[4:5] += column_sums(branch * branch)
        normed, hat_two, inverse_two = norm_parts(middle, gain_two, bias_two)
        rows_two = normed.astype(BF)
        normed_two[me_t, image] = rows_two
        halves = (me_t, other)
        gates = [dot(rows_two, gate_up_low[half, 0], NN) for half in halves]
        ups = [dot(rows_two, gate_up_low[half, 1], NN) for half in halves]
        sigmoids = [1.0 / (1.0 + jnp.exp(-gate)) for gate in gates]
        hiddens = [gate * sigmoid * up for gate, sigmoid, up in zip(gates, sigmoids, ups)]
        mean = sum(jnp.sum(hidden, -1, keepdims=True) for hidden in hiddens) / hidden_all
        centres = [hidden - mean for hidden in hiddens]
        spread = sum(jnp.sum(centre * centre, -1, keepdims=True) for centre in centres) / hidden_all
        inverse_three = lax.rsqrt(spread + EPSILON)
        hats = [centre * inverse_three for centre in centres]
        lows = [
            (hat * inner_all[half, 0:1] + inner_all[half, 1:2]).astype(BF)
            for hat, half in zip(hats, halves)
        ]
        branch = sum(dot(low, down_low[half], NN) for low, half in zip(lows, halves))
        extra[5:6] += column_sums(branch * branch)
        residual[image] = middle + branch
        cotangent = out_grad[image, own_rows] * mask[image, own_rows]
        grad_branch = cotangent.astype(BF)
        grads = [dot(grad_branch, down_low[half], NT) for half in halves]
        for half, grad, hat in zip(halves, grads, hats):
            inner_sums[half, 0:1] += column_sums(grad * hat)
            inner_sums[half, 1:2] += column_sums(grad)
        scaled = [grad * inner_all[half, 0:1] for grad, half in zip(grads, halves)]
        first = sum(jnp.sum(value, -1, keepdims=True) for value in scaled) / hidden_all
        second = (
            sum(jnp.sum(value * hat, -1, keepdims=True) for value, hat in zip(scaled, hats)) / hidden_all
        )
        grad_hiddens = [
            inverse_three * (value - first - hat * second) for value, hat in zip(scaled, hats)
        ]
        gate_rows = [
            (grad * up * (sigmoid + gate * sigmoid * (1.0 - sigmoid))).astype(BF)
            for grad, up, sigmoid, gate in zip(grad_hiddens, ups, sigmoids, gates)
        ]
        up_rows = [
            (grad * gate * sigmoid).astype(BF)
            for grad, gate, sigmoid in zip(grad_hiddens, gates, sigmoids)
        ]
        normed_three[me_t, image] = lows[0]
        normed_three_send[image] = lows[1]
        grad_gate[me_t, image] = gate_rows[0]
        grad_gate_send[image] = gate_rows[1]
        grad_up[me_t, image] = up_rows[0]
        grad_up_send[image] = up_rows[1]
        grad_two = sum(
            dot(gate_row, gate_up_low[half, 0], NT) + dot(up_row, gate_up_low[half, 1], NT)
            for gate_row, up_row, half in zip(gate_rows, up_rows, halves)
        )
        extra[2:3] += column_sums(grad_two * hat_two)
        extra[3:4] += column_sums(grad_two)
        back = cotangent + norm_back(grad_two, hat_two, inverse_two, gain_two)
        grad_middle[image] = back
        low = back.astype(BF)
        grad_middle_low[me_t, image] = low
        grad_attended[me_t, image] = dot(low, out_low[me_t], NT).astype(BF)
        grad_attended_send[image] = dot(low, out_low[other], NT).astype(BF)
        datt_copy(image).start()
        for copy in row_copies(image):
            copy.start()

    def attend_back(image):
        datt_copy(image).wait_recv()
        grad_attended_all[...] = jnp.concatenate(
            [grad_attended[half, image].astype(F32) for half in range(2)], 0
        )
        grad_query[...] = jnp.zeros_like(grad_query)
        grad_pairs[...] = jnp.zeros_like(grad_pairs)

        def head_step(head, carry):
            place = lax.div(head + 1, 2)
            at_key, at_value = lax.div(head, 2), place + 1
            key_half, value_half = half_mask(lax.rem(head, 2)), half_mask(lax.rem(head + 1, 2))
            wide = jnp.where(value_half, grad_attended_all[:, tile_of(place)], 0.0)
            low = wide.astype(BF)
            scores[...] = dot(low, key_tile(image, at_value), NT)
            delta = jnp.sum(wide * attended_low[image, :, tile_of(place)].astype(F32), -1, keepdims=True)
            for start in range(0, seq_rows, CHUNK):
                rows = slice(start, start + CHUNK)
                chance = probs[image * heads + head, rows].astype(F32)
                grad_scores[rows] = (chance * (scores[rows] - delta[rows])).astype(BF)
            grad_query[:, tile_of(at_key)] += jnp.where(
                key_half, dot(grad_scores[...], key_tile(image, at_key), NN), 0.0
            )
            query_t = jnp.transpose(queries[image * heads + head].astype(F32)).astype(BF)
            grad_pairs[tile_of(at_key)] += dot(query_t, grad_scores[...], NN)
            grad_pairs[tile_of(at_value)] += dot(
                jnp.transpose(wide).astype(BF), probs[image * heads + head], NN
            )
            return carry

        lax.fori_loop(0, heads, head_step, 0)
        pairs = jnp.transpose(grad_pairs[...])
        pairs_send[image] = pairs.astype(BF).reshape(ns, seq_rows, width)
        for copy in back_copies(image):
            copy.start()
        raw = grad_query[...] * (DH ** (-0.5))
        raw = raw * cosine[:, 0:256] - swap_quarters(raw) * sine[:, 0:256]
        grad_query_low[image] = raw.astype(BF)

    def stage(step, carry):
        @pl.when(step < images)
        def _():
            attend(step)

        @pl.when(step >= 1)
        def _():
            attend_back(step - 1)

        @pl.when(step == 0)
        def _():
            for copy in weight_copies():
                copy.wait_recv()

        @pl.when(step < images)
        def _():
            feed(step)

        return carry

    lax.fori_loop(0, images + 1, stage, 0)
    inner_copy().start()

    full_out[...] = jnp.zeros_like(full_out)
    full_gate_up[...] = jnp.zeros_like(full_gate_up)
    full_down[...] = jnp.zeros_like(full_down)

    def weights(image, carry):
        for copy in row_copies(image):
            copy.wait_recv()
        for half in range(2):
            place = slice(half * own, half * own + own)
            grad_branch = (out_grad[image, place] * mask[image, place]).astype(BF)
            full_down[...] += dot(normed_three[half, image], grad_branch, TN)
            rows_two = normed_two[half, image]
            full_gate_up[0] += dot(rows_two, grad_gate[half, image], TN)
            full_gate_up[1] += dot(rows_two, grad_up[half, image], TN)
            mixed = attended_low[image].astype(F32)[place].astype(BF)
            full_out[...] += dot(mixed, grad_middle_low[half, image], TN)[256 - narrow :]
        return carry

    lax.fori_loop(0, images, weights, 0)
    for load in loads[4:8]:
        load.wait()
    full_out[...] = full_out[...] * scale + error_out[...]
    full_gate_up[...] = full_gate_up[...] * scale + error_gate_up[...]
    full_down[...] = full_down[...] * scale + error_down[...]

    sum_query[...] = jnp.zeros_like(sum_query)
    sum_pairs[...] = jnp.zeros_like(sum_pairs)

    def finish_pairs(image, carry):
        for copy in back_copies(image):
            copy.wait_recv()
        pairs = pairs_send[image, me_s].astype(F32)
        for step in range(1, ns):
            pairs = pairs + pairs_recv[image, step].astype(F32)
        pairs = pairs * cosine[...] - swap_quarters(pairs) * sine[...]
        pairs = pairs.astype(BF)
        query = grad_query_low[image]
        grad_one[image] = dot(query, query_low[...], NN) + dot(pairs, key_value_low[...], NN)
        final_copy(image).start()
        sum_query[...] += dot(query, normed_one_all[image], TN)
        sum_pairs[...] += dot(pairs, normed_one_all[image], TN)
        return carry

    lax.fori_loop(0, images, finish_pairs, 0)
    full_qkv[0] = sum_query[0:narrow] * scale + error_qkv[0]
    full_qkv[1] = sum_pairs[0:narrow] * scale + error_qkv[1]
    full_qkv[2] = sum_pairs[narrow : 2 * narrow] * scale + error_qkv[2]

    def finish(image, carry):
        final_copy(image).wait_recv()
        grad = grad_one[image, own_rows] + grad_one_recv[image]
        _, hat_one, inverse_one = norm_parts(tokens[image].astype(F32), gain_one, bias_one)
        input_grad[image] = grad_middle[image] + norm_back(grad, hat_one, inverse_one, gain_one)
        extra[0:1] += column_sums(grad * hat_one)
        extra[1:2] += column_sums(grad)
        return carry

    lax.fori_loop(0, images, finish, 0)
    extra[0:4] = extra[0:4] * scale
    inner_copy().wait_recv()
    inner[...] = (inner_sums[me_t] + inner_recv[...]) * scale

    for image in range(images):
        for copy in (
            one_copy(image), *pair_copies(image), att_copy(image), datt_copy(image),
            *row_copies(image), *back_copies(image), final_copy(image),
        ):
            copy.wait_send()
    for copy in (*weight_copies(), inner_copy()):
        copy.wait_send()


def block(mesh_sizes, tokens, keep, mask, cosine, sine, norm_pack, inner_pack, w_qkv, hbm):
    nd, ns, nt = mesh_sizes
    images, own, width = tokens.shape
    seq_rows = 2 * own
    slots = ns * seq_rows
    narrow = w_qkv.shape[1]
    heads = narrow // DH
    wide = inner_pack.shape[1]
    shape = jax.ShapeDtypeStruct
    outs = (
        shape((images, own, width), F32),
        shape((images, own, width), F32),
        shape((3, narrow, width), F32),
        shape((narrow, width), F32),
        shape((2, width, wide), F32),
        shape((wide, width), F32),
        shape((8, width), F32),
        shape((8, wide), F32),
    )
    vmem = pl.BlockSpec(memory_space=pltpu.VMEM)
    hbm_spec = pl.BlockSpec(memory_space=pl.ANY)
    dma = pltpu.SemaphoreType.DMA
    scratch = [
        pltpu.VMEM((2, images, own, width), BF),
        pltpu.VMEM((images, seq_rows, width), BF),
        pltpu.VMEM((images, ns, seq_rows, width), BF),
        pltpu.VMEM((images * heads, seq_rows, 128), BF),
        pltpu.VMEM((images * heads, seq_rows, slots), BF),
        pltpu.VMEM((seq_rows, slots), F32),
        pltpu.VMEM((seq_rows, slots), BF),
        pltpu.VMEM((seq_rows, 256), F32),
        pltpu.VMEM((images, seq_rows, 256), BF),
        pltpu.VMEM((2, images, own, 256), BF),
        pltpu.VMEM((images, own, 256), BF),
        pltpu.VMEM((2, 256, width), BF),
        pltpu.VMEM((2, 2, width, wide), BF),
        pltpu.VMEM((2, wide, width), BF),
        pltpu.VMEM((2, 8, wide), F32),
        pltpu.VMEM((256, width), BF),
        pltpu.VMEM((2 * narrow, width), BF),
        pltpu.VMEM((2, images, own, width), BF),
        pltpu.VMEM((2, images, own, width), BF),
        pltpu.VMEM((images, own, width), F32),
        *[pltpu.VMEM((2, images, own, wide), BF)] * 3,
        *[pltpu.VMEM((images, own, wide), BF)] * 3,
        pltpu.VMEM((2, images, own, 256), BF),
        pltpu.VMEM((images, own, 256), BF),
        pltpu.VMEM((seq_rows, 256), F32),
        pltpu.VMEM((seq_rows, 256), F32),
        pltpu.VMEM((images, seq_rows, 256), BF),
        pltpu.VMEM((width, slots), F32),
        pltpu.VMEM((images, ns, seq_rows, width), BF),
        pltpu.VMEM((images, ns, seq_rows, width), BF),
        pltpu.VMEM((images, seq_rows, width), F32),
        pltpu.VMEM((images, own, width), F32),
        pltpu.VMEM((256, width), F32),
        pltpu.VMEM((2 * narrow, width), F32),
        pltpu.VMEM((2, 8, wide), F32),
        pltpu.VMEM((8, wide), F32),
        *[pltpu.VMEM(array.shape, F32) for array in hbm],
        dma((8,)),
        *[dma((images,))] * 2,
        *[dma((4,))] * 2,
        *[dma((images, ns))] * 2,
        *[dma((images,))] * 4,
        *[dma((images, 5))] * 2,
        *[dma((images, ns))] * 2,
        *[dma((images + 1,))] * 2,
    ]
    return pl.pallas_call(
        functools.partial(block_kernel, mesh_sizes, images),
        out_shape=outs,
        in_specs=[vmem] * 8 + [hbm_spec] * len(hbm),
        out_specs=[vmem] * len(outs),
        scratch_shapes=scratch,
        compiler_params=pltpu.CompilerParams(
            collective_id=1, has_side_effects=True, vmem_limit_bytes=62 * 2**20
        ),
        name="block",
    )(tokens, keep, mask, cosine, sine, norm_pack, inner_pack, w_qkv, *hbm)


def rope_tables(first_slot, count):
    slot_ids = first_slot + jnp.arange(count, dtype=jnp.int32)
    inside = jnp.logical_and(slot_ids >= 1, slot_ids <= GRID * GRID)
    patch = jnp.where(inside, slot_ids - 1, 0)
    row_pos = (patch // GRID).astype(jnp.float32)
    col_pos = (patch % GRID).astype(jnp.float32)
    quarter = DH // 4
    freqs = 10000.0 ** (-jnp.arange(quarter, dtype=jnp.float32) / quarter)
    angles = jnp.concatenate([row_pos[:, None] * freqs, col_pos[:, None] * freqs], -1) * (
        16.0 / GRID
    )
    return (jnp.cos(angles), jnp.sin(angles))


def quarter_lanes(first, second, narrow, rest):
    pairs = jnp.stack(
        [first[:, :QUARTER], second[:, :QUARTER], first[:, QUARTER:], second[:, QUARTER:]], 1
    )
    head = pairs.reshape(first.shape[0], DH)
    keys = jnp.tile(head, (1, narrow // DH))
    return jnp.concatenate([keys, jnp.full_like(keys, rest)], -1)


def per_device(
    tokens,
    out_grad,
    keep_mask,
    w_qkv,
    w_out,
    w_gate_up,
    w_down,
    norm_pack,
    inner_pack,
    moment_qkv,
    moment_out,
    moment_gate_up,
    moment_down,
    moment_norm,
    moment_inner,
    error_qkv,
    error_out,
    error_gate_up,
    error_down,
    basis_qkv,
    basis_out,
    basis_gate_up,
    basis_down,
):
    own_rows, images, width = tokens.shape
    seq_rows = out_grad.shape[0]
    slot_count = keep_mask.shape[0]
    narrow = w_out.shape[0]
    sizes = tuple(lax.axis_size(axis) for axis in ("dp", "seq", "tensor"))
    block_start = lax.axis_index("seq") * seq_rows
    mask = lax.dynamic_slice_in_dim(keep_mask, block_start, seq_rows, 0)
    mask = jnp.transpose(mask).astype(F32)[:, :, None]
    cosine_table, sine_table = rope_tables(block_start, seq_rows)
    cosine = quarter_lanes(cosine_table, cosine_table, narrow, 1.0)
    sine = quarter_lanes(-sine_table, sine_table, narrow, 0.0)

    def turn(array):
        return jnp.swapaxes(array, -1, -2)

    residual, input_grad, *fulls, extra, inner = block(
        sizes,
        jnp.swapaxes(tokens, 0, 1), jnp.transpose(keep_mask), mask, cosine, sine, norm_pack, inner_pack, turn(w_qkv),
        (
            w_out, w_gate_up, w_down, jnp.swapaxes(out_grad, 0, 1),
            turn(error_qkv[0]), error_out[0], error_gate_up[0], error_down[0],
        ),
    )
    bases = tuple(turn(basis) for basis in (basis_qkv, basis_out, basis_gate_up, basis_down))
    parts = factors(sizes, fulls, bases, extra, inner)
    (
        factor_left, factor_qkv, factor_out, factor_gate_up, factor_down,
        new_error_qkv, new_error_out, new_error_gate_up, new_error_down,
        new_moment_qkv, new_moment_out, new_moment_gate_up, new_moment_down, new_moment_norm, new_moment_inner,
        new_w_qkv, new_w_out, new_w_gate_up, new_w_down, new_norm_pack, new_inner_pack,
    ) = update(
        fulls,
        (turn(moment_qkv), moment_out, moment_gate_up, moment_down),
        (turn(w_qkv), w_out, w_gate_up, w_down),
        parts,
        (norm_pack, moment_norm, inner_pack, moment_inner),
    )
    squares = jnp.sum(parts[3][4:6], -1)
    branch_rms = jnp.sqrt(squares / (slot_count * images * lax.axis_size("dp") * width))
    return (
        jnp.swapaxes(residual, 0, 1), jnp.swapaxes(input_grad, 0, 1),
        *(turn(factor) for factor in (factor_left, factor_qkv, factor_out, factor_gate_up, factor_down)),
        turn(new_error_qkv)[None], new_error_out[None], new_error_gate_up[None], new_error_down[None],
        turn(new_moment_qkv), new_moment_out, new_moment_gate_up, new_moment_down, new_moment_norm, new_moment_inner,
        turn(new_w_qkv), new_w_out, new_w_gate_up, new_w_down, new_norm_pack, new_inner_pack,
        branch_rms,
    )


def solution(mesh):
    placed = (
        P(("seq", "tensor"), "dp", None),
        P("seq", "dp", None),
        P(None, "dp"),
        P(None, None, "tensor"),
        P("tensor", None),
        P(None, None, "tensor"),
        P("tensor", None),
        P(),
        P(None, "tensor"),
        P(None, None, "tensor"),
        P("tensor", None),
        P(None, None, "tensor"),
        P("tensor", None),
        P(),
        P(None, "tensor"),
        P(("dp", "seq"), None, None, "tensor"),
        P(("dp", "seq"), "tensor", None),
        P(("dp", "seq"), None, None, "tensor"),
        P(("dp", "seq"), "tensor", None),
        P(None, "tensor", None),
        P("tensor", None),
        P(None, "tensor", None),
        P("tensor", None),
    )
    return jax.shard_map(
        per_device,
        mesh=mesh,
        in_specs=placed,
        out_specs=(
            P(("seq", "tensor"), "dp", None),
            P(("seq", "tensor"), "dp", None),
            P(),
            P(None, "tensor", None),
            P("tensor", None),
            P(None, "tensor", None),
            P("tensor", None),
            P(("dp", "seq"), None, None, "tensor"),
            P(("dp", "seq"), "tensor", None),
            P(("dp", "seq"), None, None, "tensor"),
            P(("dp", "seq"), "tensor", None),
            P(None, None, "tensor"),
            P("tensor", None),
            P(None, None, "tensor"),
            P("tensor", None),
            P(),
            P(None, "tensor"),
            P(None, None, "tensor"),
            P("tensor", None),
            P(None, None, "tensor"),
            P("tensor", None),
            P(),
            P(None, "tensor"),
            P(),
        ),
        check_vma=False,
    )
```

profile of v0, /device:TPU:0, one launch (start us, length us, event | category | flops | bytes accessed | tf_op | source)
XLA Modules:
  0.0 125.8 jit_solution(17001640090032412820)
XLA Ops:
  0.7 0.8 convert_bitcast_fusion
  1.4 1.0 copy.53.refs_2_
  2.4 0.1 broadcast_multiply_fusion.1
  2.5 0.2 fusion.9
  2.8 0.1 copy.51
  2.9 0.8 concatenate.10.refs_3_
  3.8 0.1 copy.52
  3.9 0.8 concatenate.11.refs_4_
  4.7 0.0 copy-start.9
  4.7 70.1 %block.1 = (f32[3,136,384]{2,1,0:T(8,128)}, f32[3,136,384]{2,1,0:T(8,128)}, f32[3,192,384]{2,1,0:T(8,128)}, f32[192,384]{1,0:T(8,128)}, f32[2,384,512]{2,1,0:T(8...) custom-call(bf16[3,136,384]{2,1,0:T(8,128)(2,1)} %bitcast.67, s32[3,1088]{1,0:T(4,128)} %bitcast.69, ...), custom_call_target="tpu_custom_call" | custom-call | tf_op jit(solution)/shard_map/block/pallas_call | solution.py:822
  74.9 1.4 %copy-done = f32[2,384,512]{2,1,0:T(8,128)S(1)} copy-done((f32[2,384,512]{2,1,0:T(8,128)S(1)}, f32[2,384,512]{2,1,0:T(8,128)}, u32[]{:S(2)}) %copy-start) | copy-done | bytes 1572888
  76.3 1.2 copy-done.1
  77.5 1.1 copy-done.4
  78.6 1.0 copy-done.7
  79.6 0.7 copy-done.16
  80.3 0.7 copy-done.18
  81.0 0.0 copy-start.11
  81.0 0.0 copy-start.20
  81.1 34.8 %factors.1 = (f32[5,8,384]{2,1,0:T(8,128)S(1)}, bf16[5,24,384]{2,1,0:T(8,128)(2,1)S(1)}, bf16[2,384,24]{2,1,0:T(8,128)(2,1)S(1)}, f32[8,384]{1,0:T(8,128)S(1)}, ...) custom-call(f32[3,192,384]{2,1,0:T(8,128)S(1)} %copy-done.1, ...), custom_call_target="tpu_custom_call" | custom-call | tf_op jit(solution)/shard_map/factors/pallas_call | solution.py:192
  116.0 7.4 %update.1 = (f32[5,8,384]{2,1,0:T(8,128)}, f32[3,8,192]{2,1,0:T(8,128)}, f32[8,192]{1,0:T(8,128)}, f32[2,8,512]{2,1,0:T(8,128)}, f32[8,512]{1,0:T(8,128)}, /*ind...) custom-call(f32[3,192,384]{2,1,0:T(8,128)S(1)} %copy-done.2, ...), custom_call_target="tpu_custom_call" | custom-call | tf_op jit(solution)/shard_map/update/pallas_call | solution.py:298
  123.5 0.1 slice_reduce_fusion
  123.6 0.5 multiply_sqrt_fusion
  124.1 0.8 copy.56
  124.9 0.8 copy.57
  (48 shorter events, 0.2 us)
Async XLA Ops:
  4.7 70.2 %copy-start.12 = (f32[2,512,8]{1,2,0:T(8,128)S(1)}, f32[2,512,8]{1,2,0:T(8,128)}, u32[]{:S(2)}) copy-start(f32[2,512,8]{1,2,0:T(8,128)} %param.44) | copy-start | bytes 98308
  4.7 70.2 %copy-start.13 = (f32[3,192,8]{1,2,0:T(8,128)S(1)}, f32[3,192,8]{1,2,0:T(8,128)}, u32[]{:S(2)}) copy-start(f32[3,192,8]{1,2,0:T(8,128)} %param.42) | copy-start | bytes 55300
  4.7 70.2 %copy-start.15 = (f32[512,8]{0,1:T(8,128)S(1)}, f32[512,8]{0,1:T(8,128)}, u32[]{:S(2)}) copy-start(f32[512,8]{0,1:T(8,128)} %param.45) | copy-start | bytes 49156
  4.7 70.2 %copy-start.19 = (f32[192,8]{0,1:T(8,128)S(1)}, f32[192,8]{0,1:T(8,128)}, u32[]{:S(2)}) copy-start(f32[192,8]{0,1:T(8,128)} %param.43) | copy-start | bytes 18436
  4.7 111.2 %copy-start.9 = (f32[3,384,192]{1,2,0:T(8,128)S(1)}, f32[3,384,192]{1,2,0:T(8,128)}, u32[]{:S(2)}) copy-start(f32[3,384,192]{1,2,0:T(8,128)} %param.32) | copy-start | bytes 2654212
  4.7 111.2 %copy-start.10 = (f32[512,384]{1,0:T(8,128)S(1)}, f32[512,384]{1,0:T(8,128)}, u32[]{:S(2)}) copy-start(f32[512,384]{1,0:T(8,128)} %refs_7_.1) | copy-start | bytes 2359300
  74.9 1.4 %copy-start = (f32[2,384,512]{2,1,0:T(8,128)S(1)}, f32[2,384,512]{2,1,0:T(8,128)}, u32[]{:S(2)}) copy-start(f32[2,384,512]{2,1,0:T(8,128)} %get-tuple-element.67.refs_2_) | copy-start | bytes 4718596
  76.3 1.2 copy-start.1
  77.5 1.1 copy-start.4
  78.6 1.0 copy-start.7
  79.5 0.7 copy-start.16
  80.3 0.7 copy-start.18
  81.0 34.9 %copy-start.2 = (f32[3,192,384]{2,1,0:T(8,128)S(1)}, f32[3,192,384]{2,1,0:T(8,128)}, u32[]{:S(2)}) copy-start(f32[3,192,384]{2,1,0:T(8,128)} %get-tuple-element.65.refs_0_) | copy-start | bytes 2654212
  81.0 34.9 %copy-start.3 = (f32[512,384]{1,0:T(8,128)S(1)}, f32[512,384]{1,0:T(8,128)}, u32[]{:S(2)}) copy-start(f32[512,384]{1,0:T(8,128)} %refs_11_.1) | copy-start | bytes 2359300
  81.0 34.9 %copy-start.5 = (f32[512,384]{1,0:T(8,128)S(1)}, f32[512,384]{1,0:T(8,128)}, u32[]{:S(2)}) copy-start(f32[512,384]{1,0:T(8,128)} %get-tuple-element.68.refs_3_) | copy-start | bytes 2359300
  81.0 34.9 %copy-start.6 = (f32[192,384]{1,0:T(8,128)S(1)}, f32[192,384]{1,0:T(8,128)}, u32[]{:S(2)}) copy-start(f32[192,384]{1,0:T(8,128)} %refs_9_.3) | copy-start | bytes 884740
  81.0 34.9 %copy-start.8 = (f32[192,384]{1,0:T(8,128)S(1)}, f32[192,384]{1,0:T(8,128)}, u32[]{:S(2)}) copy-start(f32[192,384]{1,0:T(8,128)} %get-tuple-element.66.refs_1_) | copy-start | bytes 884740
  81.0 34.9 %copy-start.11 = (f32[192,384]{1,0:T(8,128)S(1)}, f32[192,384]{1,0:T(8,128)}, u32[]{:S(2)}) copy-start(f32[192,384]{1,0:T(8,128)} %refs_5_.3) | copy-start | bytes 884740
  81.0 34.9 %copy-start.14 = (f32[4,384]{1,0:T(4,128)S(1)}, f32[4,384]{1,0:T(4,128)}, u32[]{:S(2)}) copy-start(f32[4,384]{1,0:T(4,128)} %refs_22_.1) | copy-start | bytes 18436
  81.0 34.9 %copy-start.17 = (f32[2,512]{1,0:T(2,128)S(1)}, f32[2,512]{1,0:T(2,128)}, u32[]{:S(2)}) copy-start(f32[2,512]{1,0:T(2,128)} %refs_24_.1) | copy-start | bytes 12292
  81.0 34.9 %copy-start.20 = (f32[4,384]{1,0:T(4,128)S(1)}, f32[4,384]{1,0:T(4,128)}, u32[]{:S(2)}) copy-start(f32[4,384]{1,0:T(4,128)} %refs_23_.1) | copy-start | bytes 18436
  81.0 34.9 %copy-start.21 = (f32[2,512]{1,0:T(2,128)S(1)}, f32[2,512]{1,0:T(2,128)}, u32[]{:S(2)}) copy-start(f32[2,512]{1,0:T(2,128)} %refs_25_.1) | copy-start | bytes 12292
  116.0 8.1 %copy-start.23 = (f32[3,136,384]{2,1,0:T(8,128)S(1)}, f32[3,136,384]{2,1,0:T(8,128)}, u32[]{:S(2)}) copy-start(f32[3,136,384]{2,1,0:T(8,128)} %get-tuple-element.63) | copy-start | bytes 1880068
  123.5 1.5 %copy-start.22 = (f32[3,136,384]{2,1,0:T(8,128)S(1)}, f32[3,136,384]{2,1,0:T(8,128)}, u32[]{:S(2)}) copy-start(f32[3,136,384]{2,1,0:T(8,128)} %get-tuple-element.64) | copy-start | bytes 1880068
where the time goes:
time: 126 us
  Pallas kernels  112 us (89%)
  local copies, waits for them, and re-layouts  10.7 us (8%)
  other arithmetic  1.73 us (1%)
    pallas_call x1, Pallas kernels, block(): pl.pallas_call(functools.partial(block_kernel, mesh_sizes, images), out_s...  70.1 us
    pallas_call x1, Pallas kernels, factors(): pl.pallas_call(functools.partial(factor_kernel, mesh_sizes), out_shape=ou...  34.8 us
    unnamed x50, local copies, waits for them, and re-layouts  7.82 us
    pallas_call x1, Pallas kernels, update(): pl.pallas_call(update_kernel, grid=(steps,), out_shape=[*small, *like, *l...  7.44 us

commit v1 on v0

--- a/solution.py
+++ b/solution.py
@@ -1,4 +1,5 @@
 import functools
+import math
 
 import jax
 import jax.numpy as jnp
@@ -13,6 +14,7 @@
 RANK = 8
 QUARTER = DH // 4
 CHUNK = 16
+LIMIT = 62
 
 
 EPSILON = 1e-06
@@ -75,6 +77,10 @@
             )
             copy.start()
             copies.append(copy)
+    return copies
+
+
+def arrive(copies):
     for copy in copies:
         copy.wait()
 
@@ -87,128 +93,22 @@
 
 
 def greet(axes, barrier):
-    count = 0
     for axis, size in axes:
         me = lax.axis_index(axis)
         for step in range(1, size):
             pl.semaphore_signal(
                 barrier, inc=1, device_id={axis: lax.rem(me + step, size)}, device_id_type=MESH
             )
-            count += 1
-    pl.semaphore_wait(barrier, count)
-
-
-def factor_kernel(sizes, *refs):
-    (
-        full_qkv, full_out, full_gate_up, full_down,
-        basis_qkv, basis_out, basis_gate_up, basis_down, extra, inner,
-        left_rows, left_rows_fine, left_cols_fine, extra_sum,
-        narrow_rows, narrow_cols_fine, wide_rows, wide_rows_fine, down_cols_fine, inner_sum,
-        sum_t, sum_s, sum_d, narrow_s, narrow_d, wide_s, wide_d,
-        send_t, recv_t, send_s, recv_s, send_d, recv_d, send_ns, recv_ns, send_nd, recv_nd,
-    ) = refs
-    nd, ns, nt = sizes
-    greet((("tensor", nt), ("seq", ns), ("dp", nd)), pltpu.get_barrier_semaphore())
-    me_t, me_s, me_d = (lax.axis_index(axis) for axis in ("tensor", "seq", "dp"))
-    own = sum_t.at[me_t]
-    own[0:8] = sum(fine_dot(basis_qkv[index], full_qkv[index], NN) for index in range(3))
-    own[8:16] = fine_dot(basis_out[...], full_out[...], NN)
-    for index in range(2):
-        own[16 + 8 * index : 24 + 8 * index] = fine_dot(
-            basis_gate_up[index], full_gate_up[index], NT
-        )
-    own[32:40] = fine_dot(basis_down[...], full_down[...], NN)
-    own[40:48] = extra[...]
-    exchange("tensor", nt, (sum_t,), send_t, recv_t)
-    sum_s[me_s] = total(sum_t, nt)
-    exchange("seq", ns, (sum_s,), send_s, recv_s)
-    sum_d[me_d] = total(sum_s, ns)
-    exchange("dp", nd, (sum_d,), send_d, recv_d)
-    summed = total(sum_d, nd)
-    share = 1.0 / (ns * nd)
-    extra_sum[0:4] = summed[40:44] * share
-    extra_sum[4:8] = summed[44:48]
-    left = gram_schmidt(summed[0:40].reshape(5, RANK, summed.shape[-1]))
-    for index in range(5):
-        left_rows[index] = left[index]
-        high, low = split(left[index])
-        triple = jnp.concatenate([high.astype(F32), high.astype(F32), low.astype(F32)], 0)
-        left_rows_fine[index] = triple.astype(BF)
-        if index in (2, 3):
-            left_cols_fine[index - 2] = jnp.transpose(triple).astype(BF)
-    for index in range(3):
-        narrow_s[me_s, 8 * index : 8 * index + 8] = fine_dot(left[0], full_qkv[index], NT)
-    narrow_s[me_s, 24:32] = fine_dot(left[1], full_out[...], NT)
-    for index in range(2):
-        wide_s[me_s, 8 * index : 8 * index + 8] = fine_dot(left[2 + index], full_gate_up[index], NN)
-    wide_s[me_s, 16:24] = fine_dot(left[4], full_down[...], NT)
-    wide_s[me_s, 24:32] = inner[...]
-    exchange("seq", ns, (narrow_s, wide_s), send_ns, recv_ns)
-    narrow_d[me_d] = total(narrow_s, ns)
-    wide_d[me_d] = total(wide_s, ns)
-    exchange("dp", nd, (narrow_d, wide_d), send_nd, recv_nd)
-    narrow = total(narrow_d, nd) * share
-    wide = total(wide_d, nd) * share
-    inner_sum[...] = wide[24:32]
-
-    def triple_of(rows):
-        high, low = split(rows)
-        return jnp.concatenate([high.astype(F32), low.astype(F32), high.astype(F32)], 0)
-
-    for index in range(4):
-        part = narrow[8 * index : 8 * index + 8]
-        narrow_rows[index] = part
-        narrow_cols_fine[index] = jnp.transpose(triple_of(part)).astype(BF)
-    for index in range(3):
-        part = wide[8 * index : 8 * index + 8]
-        wide_rows[index] = part
-        if index < 2:
-            wide_rows_fine[index] = triple_of(part).astype(BF)
-        else:
-            down_cols_fine[...] = jnp.transpose(triple_of(part)).astype(BF)
-
-
-def factors(mesh_sizes, fulls, bases, extra, inner):
-    nd, ns, nt = mesh_sizes
-    _, narrow, width = fulls[0].shape
-    wide = fulls[2].shape[-1]
-    shape = jax.ShapeDtypeStruct
-    outs = (
-        shape((5, RANK, width), F32),
-        shape((5, 3 * RANK, width), BF),
-        shape((2, width, 3 * RANK), BF),
-        shape((8, width), F32),
-        shape((4, RANK, narrow), F32),
-        shape((4, narrow, 3 * RANK), BF),
-        shape((3, RANK, wide), F32),
-        shape((2, 3 * RANK, wide), BF),
-        shape((wide, 3 * RANK), BF),
-        shape((8, wide), F32),
-    )
-    sems = []
-    for count, size in ((1, nt), (1, ns), (1, nd), (2, ns), (2, nd)):
-        sems += [pltpu.SemaphoreType.DMA((count, size))] * 2
-    vmem = pl.BlockSpec(memory_space=pltpu.VMEM)
-    return pl.pallas_call(
-        functools.partial(factor_kernel, mesh_sizes),
-        out_shape=outs,
-        in_specs=[vmem] * 10,
-        out_specs=[vmem] * len(outs),
-        scratch_shapes=[
-            pltpu.VMEM((nt, 48, width), F32),
-            pltpu.VMEM((ns, 48, width), F32),
-            pltpu.VMEM((nd, 48, width), F32),
-            pltpu.VMEM((ns, 32, narrow), F32),
-            pltpu.VMEM((nd, 32, narrow), F32),
-            pltpu.VMEM((ns, 32, wide), F32),
-            pltpu.VMEM((nd, 32, wide), F32),
-            *sems,
-        ],
-        compiler_params=pltpu.CompilerParams(
-            collective_id=0, has_side_effects=True, vmem_limit_bytes=24 * 2**20
-        ),
-        name="factors",
-    )(*fulls, *bases, extra, inner)
+
+
+def triple_first(rows):
+    high, low = split(rows)
+    return jnp.concatenate([high.astype(F32), high.astype(F32), low.astype(F32)], 0)
+
+
+def triple_second(rows):
+    high, low = split(rows)
+    return jnp.concatenate([high.astype(F32), low.astype(F32), high.astype(F32)], 0)
 
 
 def update_kernel(*refs):
@@ -309,21 +209,41 @@
             whole(norm),
             whole(inner),
         ],
-        compiler_params=pltpu.CompilerParams(vmem_limit_bytes=48 * 2**20),
+        compiler_params=pltpu.CompilerParams(vmem_limit_bytes=LIMIT * 2**20),
         name="update",
     )(*fulls, *moments, *weights, *parts, *norms)
 
 
-def swap_quarters(value):
+def swap_quarters(tile):
     lane = lax.broadcasted_iota(jnp.int32, (1, 128), 1)
     low = lax.rem(lax.div(lane, QUARTER), 2) == 0
-    tiles = []
-    for start in range(0, value.shape[-1], 128):
-        tile = value[:, start : start + 128]
-        tiles.append(
-            jnp.where(low, pltpu.roll(tile, 128 - QUARTER, 1), pltpu.roll(tile, QUARTER, 1))
-        )
-    return jnp.concatenate(tiles, -1)
+    return jnp.where(low, pltpu.roll(tile, 128 - QUARTER, 1), pltpu.roll(tile, QUARTER, 1))
+
+
+def turn_pairs(pairs, cosine, sine):
+    keys = lax.broadcasted_iota(jnp.int32, (1, 128), 1) < DH
+    first, second, third = (pairs[:, start : start + 128] for start in (0, 128, 256))
+    first = first * cosine + swap_quarters(first) * sine
+    second = jnp.where(keys, second * cosine + swap_quarters(second) * sine, second)
+    return jnp.concatenate([first, second, third], -1)
+
+
+def turn_queries(raw, cosine, sine):
+    tiles = (raw[:, start : start + 128] for start in (0, 128))
+    return jnp.concatenate([tile * cosine + swap_quarters(tile) * sine for tile in tiles], -1)
+
+
+def angle_tables(first_slot, count):
+    slots = first_slot + lax.broadcasted_iota(jnp.int32, (count, 128), 0)
+    place = lax.rem(lax.broadcasted_iota(jnp.int32, (count, 128), 1), DH)
+    inside = jnp.logical_and(slots >= 1, slots <= GRID * GRID)
+    patch = jnp.where(inside, slots - 1, 0)
+    quarter = lax.div(place, QUARTER)
+    position = jnp.where(quarter < 2, lax.div(patch, GRID), lax.rem(patch, GRID)).astype(F32)
+    power = lax.rem(place, QUARTER).astype(F32)
+    angles = position * jnp.exp(power * (-math.log(10000.0) / QUARTER)) * (16.0 / GRID)
+    sine = jnp.sin(angles)
+    return jnp.cos(angles), jnp.where(lax.rem(quarter, 2) == 0, -sine, sine)
 
 
 def norm_parts(values, gain, bias):
@@ -349,10 +269,12 @@
 
 def block_kernel(sizes, images, *refs):
     (
-        tokens, keep, mask, cosine, sine, norm_pack, inner_pack, w_qkv,
-        w_out_hbm, w_gate_up_hbm, w_down_hbm, out_grad_hbm,
+        keep, norm_pack, inner_pack, basis_qkv, basis_out, basis_gate_up, basis_down,
+        tokens_hbm, w_qkv_hbm, w_out_hbm, w_gate_up_hbm, w_down_hbm, out_grad_hbm,
         error_qkv_hbm, error_out_hbm, error_gate_up_hbm, error_down_hbm,
-        residual, input_grad, full_qkv, full_out, full_gate_up, full_down, extra, inner,
+        residual, input_grad, full_qkv, full_out, full_gate_up, full_down,
+        left_rows, left_rows_fine, left_cols_fine, extra_sum,
+        narrow_rows, narrow_cols_fine, wide_rows, wide_rows_fine, down_cols_fine, inner_sum,
         normed_one, normed_one_all, keys_values, queries, probs, scores, grad_scores,
         attended, attended_low, attended_in, attended_send,
         out_low, gate_up_low, down_low, inner_all, query_low, key_value_low,
@@ -360,14 +282,17 @@
         normed_three_send, grad_gate_send, grad_up_send,
         grad_attended, grad_attended_send, grad_attended_all, grad_query, grad_query_low, grad_pairs,
         pairs_send, pairs_recv, grad_one, grad_one_recv, sum_query, sum_pairs, inner_sums, inner_recv,
-        w_out, w_gate_up, w_down, out_grad, error_qkv, error_out, error_gate_up, error_down,
+        tokens, w_qkv, w_out, w_gate_up, w_down, out_grad, mask, cosine, sine, extra, kept_rows,
+        early_t, early_d, early_s, late_t, late_s, late_d, norm_t, norm_s, norm_d,
+        thin_d, thin_s, broad_d, broad_s, slim_s, slim_d,
         local_sems, one_send, one_recv, weight_send, weight_recv, pair_send, pair_recv,
         att_send, att_recv, datt_send, datt_recv, rows_send, rows_recv, back_send, back_recv,
-        final_send, final_recv,
+        final_send, final_recv, low_send, low_recv,
     ) = refs
     nd, ns, nt = sizes
     me_t, me_s = lax.axis_index("tensor"), lax.axis_index("seq")
     other = 1 - me_t
+    me_d = lax.axis_index("dp")
     own, width = tokens.shape[1], tokens.shape[2]
     seq_rows = 2 * own
     slots = ns * seq_rows
@@ -377,13 +302,16 @@
     own_rows = pl.ds(pl.multiple_of(me_t * own, 8), own)
     other_rows = pl.ds(pl.multiple_of(other * own, 8), own)
 
+    barrier = pltpu.get_barrier_semaphore()
+    greet((("tensor", nt), ("seq", ns), ("dp", nd)), barrier)
     loads = [
         pltpu.make_async_copy(source, target, local_sems.at[number])
         for number, (source, target) in enumerate(
             (
+                (tokens_hbm, tokens), (w_qkv_hbm, w_qkv),
                 (w_out_hbm, w_out), (w_gate_up_hbm, w_gate_up), (w_down_hbm, w_down), (out_grad_hbm, out_grad),
-                (error_qkv_hbm, error_qkv), (error_out_hbm, error_out),
-                (error_gate_up_hbm, error_gate_up), (error_down_hbm, error_down),
+                (error_qkv_hbm, full_qkv), (error_out_hbm, full_out),
+                (error_gate_up_hbm, full_gate_up), (error_down_hbm, full_down),
             )
         )
     ]
@@ -464,12 +392,20 @@
     gain_one, bias_one = norm_pack[0:1], norm_pack[1:2]
     gain_two, bias_two = norm_pack[2:3], norm_pack[3:4]
 
+    cosine[...], sine[...] = angle_tables(me_s * seq_rows, seq_rows)
+    kept = jnp.concatenate([keep[...].astype(F32), jnp.zeros((8 - images, slots), F32)], 0)
+    kept_rows[...] = jnp.transpose(kept)
+    kept = kept_rows[pl.ds(pl.multiple_of(me_s * seq_rows, 8), seq_rows)]
+    for image in range(images):
+        mask[image] = kept[:, image : image + 1]
+    loads[0].wait()
     for image in range(images):
         normed, _, _ = norm_parts(tokens[image].astype(F32), gain_one, bias_one)
         normed_one[me_t, image] = normed.astype(BF)
-    greet((("tensor", nt), ("seq", ns)), pltpu.get_barrier_semaphore())
+    pl.semaphore_wait(barrier, (nt - 1) + (ns - 1) + (nd - 1))
     for image in range(images):
         one_copy(image).start()
+    loads[1].wait()
 
     narrow = heads * DH
     pad = jnp.zeros((256 - narrow, width), BF)
@@ -481,13 +417,12 @@
         one_copy(image).wait_recv()
         blocks = [normed_one[half, image] for half in range(2)]
         pairs = jnp.concatenate([dot(block, key_value_low[...], NT) for block in blocks], 0)
-        pairs = pairs * cosine[...] + swap_quarters(pairs) * sine[...]
+        pairs = turn_pairs(pairs, cosine[...], sine[...])
         keys_values[image, me_s] = pairs.astype(BF)
         for copy in pair_copies(image):
             copy.start()
         raw = jnp.concatenate([dot(block, query_low[...], NT) for block in blocks], 0)
-        raw = raw * cosine[:, 0:256] + swap_quarters(raw) * sine[:, 0:256]
-        raw = raw * (DH ** (-0.5))
+        raw = turn_queries(raw, cosine[...], sine[...]) * (DH ** (-0.5))
         lane = lax.broadcasted_iota(jnp.int32, (1, 128), 1)
         for head in range(heads):
             tile = raw[:, head // 2 * 128 : head // 2 * 128 + 128]
@@ -497,7 +432,7 @@
 
     lax.fori_loop(0, images, project, 0)
 
-    for load in loads[0:3]:
+    for load in loads[2:5]:
         load.wait()
     out_low[me_t] = jnp.concatenate([pad, w_out[...].astype(BF)], 0)
     for index in range(2):
@@ -507,7 +442,7 @@
     inner_all[me_t, 0:2] = inner_pack[...]
     for copy in weight_copies():
         copy.start()
-    loads[3].wait()
+    loads[5].wait()
     extra[...] = jnp.zeros_like(extra)
     inner_sums[...] = jnp.zeros_like(inner_sums)
 
@@ -652,7 +587,7 @@
         for copy in back_copies(image):
             copy.start()
         raw = grad_query[...] * (DH ** (-0.5))
-        raw = raw * cosine[:, 0:256] - swap_quarters(raw) * sine[:, 0:256]
+        raw = turn_queries(raw, cosine[...], -sine[...])
         grad_query_low[image] = raw.astype(BF)
 
     def stage(step, carry):
@@ -678,9 +613,8 @@
     lax.fori_loop(0, images + 1, stage, 0)
     inner_copy().start()
 
-    full_out[...] = jnp.zeros_like(full_out)
-    full_gate_up[...] = jnp.zeros_like(full_gate_up)
-    full_down[...] = jnp.zeros_like(full_down)
+    for load in loads[7:10]:
+        load.wait()
 
     def weights(image, carry):
         for copy in row_copies(image):
@@ -688,57 +622,144 @@
         for half in range(2):
             place = slice(half * own, half * own + own)
             grad_branch = (out_grad[image, place] * mask[image, place]).astype(BF)
-            full_down[...] += dot(normed_three[half, image], grad_branch, TN)
+            full_down[...] += dot(normed_three[half, image], grad_branch, TN) * scale
             rows_two = normed_two[half, image]
-            full_gate_up[0] += dot(rows_two, grad_gate[half, image], TN)
-            full_gate_up[1] += dot(rows_two, grad_up[half, image], TN)
+            full_gate_up[0] += dot(rows_two, grad_gate[half, image], TN) * scale
+            full_gate_up[1] += dot(rows_two, grad_up[half, image], TN) * scale
             mixed = attended_low[image].astype(F32)[place].astype(BF)
-            full_out[...] += dot(mixed, grad_middle_low[half, image], TN)[256 - narrow :]
+            full_out[...] += dot(mixed, grad_middle_low[half, image], TN)[256 - narrow :] * scale
         return carry
 
     lax.fori_loop(0, images, weights, 0)
-    for load in loads[4:8]:
-        load.wait()
-    full_out[...] = full_out[...] * scale + error_out[...]
-    full_gate_up[...] = full_gate_up[...] * scale + error_gate_up[...]
-    full_down[...] = full_down[...] * scale + error_down[...]
+
+    def low_exchange(axis, size, buffers, number):
+        return exchange(axis, size, buffers, low_send.at[number], low_recv.at[number])
+
+    share = 1.0 / (ns * nd)
+    early = early_t.at[me_t]
+    early[0:8] = fine_dot(basis_out[...], full_out[...], NN)
+    for index in range(2):
+        early[8 + 8 * index : 16 + 8 * index] = fine_dot(
+            basis_gate_up[index], full_gate_up[index], NT
+        )
+    early[24:32] = fine_dot(basis_down[...], full_down[...], NN)
+    early[32:40] = extra[...]
+    moves = low_exchange("tensor", nt, (early_t,), 0)
 
     sum_query[...] = jnp.zeros_like(sum_query)
     sum_pairs[...] = jnp.zeros_like(sum_pairs)
 
-    def finish_pairs(image, carry):
+    def finish_pairs(image):
         for copy in back_copies(image):
             copy.wait_recv()
         pairs = pairs_send[image, me_s].astype(F32)
         for step in range(1, ns):
             pairs = pairs + pairs_recv[image, step].astype(F32)
-        pairs = pairs * cosine[...] - swap_quarters(pairs) * sine[...]
-        pairs = pairs.astype(BF)
+        pairs = turn_pairs(pairs, cosine[...], -sine[...]).astype(BF)
         query = grad_query_low[image]
         grad_one[image] = dot(query, query_low[...], NN) + dot(pairs, key_value_low[...], NN)
         final_copy(image).start()
         sum_query[...] += dot(query, normed_one_all[image], TN)
         sum_pairs[...] += dot(pairs, normed_one_all[image], TN)
+
+    finish_pairs(0)
+    arrive(moves)
+    early_d[me_d] = total(early_t, nt)
+    early_moves = low_exchange("dp", nd, (early_d,), 1)
+
+    def rest_pairs(image, carry):
+        finish_pairs(image)
         return carry
 
-    lax.fori_loop(0, images, finish_pairs, 0)
-    full_qkv[0] = sum_query[0:narrow] * scale + error_qkv[0]
-    full_qkv[1] = sum_pairs[0:narrow] * scale + error_qkv[1]
-    full_qkv[2] = sum_pairs[narrow : 2 * narrow] * scale + error_qkv[2]
+    lax.fori_loop(1, images, rest_pairs, 0)
+    loads[6].wait()
+    full_qkv[0] += sum_query[0:narrow] * scale
+    full_qkv[1] += sum_pairs[0:narrow] * scale
+    full_qkv[2] += sum_pairs[narrow : 2 * narrow] * scale
+    late_t[me_t] = sum(fine_dot(basis_qkv[index], full_qkv[index], NN) for index in range(3))
+    late_moves = low_exchange("tensor", nt, (late_t,), 2)
+
+    norm_t[me_t] = jnp.zeros_like(norm_t[me_t])
 
     def finish(image, carry):
         final_copy(image).wait_recv()
         grad = grad_one[image, own_rows] + grad_one_recv[image]
         _, hat_one, inverse_one = norm_parts(tokens[image].astype(F32), gain_one, bias_one)
         input_grad[image] = grad_middle[image] + norm_back(grad, hat_one, inverse_one, gain_one)
-        extra[0:1] += column_sums(grad * hat_one)
-        extra[1:2] += column_sums(grad)
+        norm_t[me_t, 0:1] += column_sums(grad * hat_one)
+        norm_t[me_t, 1:2] += column_sums(grad)
         return carry
 
+    def finalize_left(index, rows):
+        left_rows[index] = rows
+        triple = triple_first(rows)
+        left_rows_fine[index] = triple.astype(BF)
+        if index in (2, 3):
+            left_cols_fine[index - 2] = jnp.transpose(triple).astype(BF)
+
+    arrive(late_moves)
+    late_s[me_s] = total(late_t, nt)
+    late_moves = low_exchange("seq", ns, (late_s,), 3)
     lax.fori_loop(0, images, finish, 0)
-    extra[0:4] = extra[0:4] * scale
+    norm_moves = low_exchange("tensor", nt, (norm_t,), 4)
+    arrive(early_moves)
+    early_s[me_s] = total(early_d, nd)
+    early_moves = low_exchange("seq", ns, (early_s,), 5)
+    arrive(late_moves)
+    late_d[me_d] = total(late_s, ns)
+    late_moves = low_exchange("dp", nd, (late_d,), 6)
+    arrive(early_moves)
+    summed = total(early_s, ns)
+    extra_sum[2:4] = summed[34:36] * (share * scale)
+    extra_sum[4:6] = summed[36:38]
+    extra_sum[6:8] = jnp.zeros_like(extra_sum[6:8])
+    left = gram_schmidt(summed[0:32].reshape(4, RANK, width))
+    for index in range(4):
+        finalize_left(index + 1, left[index])
+    thin_d[me_d] = fine_dot(left[0], full_out[...], NT)
+    for index in range(2):
+        broad_d[me_d, 8 * index : 8 * index + 8] = fine_dot(left[1 + index], full_gate_up[index], NN)
+    broad_d[me_d, 16:24] = fine_dot(left[3], full_down[...], NT)
     inner_copy().wait_recv()
-    inner[...] = (inner_sums[me_t] + inner_recv[...]) * scale
+    broad_d[me_d, 24:32] = (inner_sums[me_t] + inner_recv[...]) * scale
+    early_moves = low_exchange("dp", nd, (thin_d, broad_d), 7)
+    arrive(norm_moves)
+    norm_s[me_s] = total(norm_t, nt) * scale
+    arrive(late_moves)
+    left = gram_schmidt(total(late_d, nd).reshape(1, RANK, width))[0]
+    for index in range(3):
+        slim_s[me_s, 8 * index : 8 * index + 8] = fine_dot(left, full_qkv[index], NT)
+    late_moves = low_exchange("seq", ns, (slim_s, norm_s), 8)
+    finalize_left(0, left)
+    arrive(early_moves)
+    thin_s[me_s] = total(thin_d, nd)
+    broad_s[me_s] = total(broad_d, nd)
+    early_moves = low_exchange("seq", ns, (thin_s, broad_s), 9)
+    arrive(late_moves)
+    slim_d[me_d] = total(slim_s, ns)
+    norm_d[me_d] = total(norm_s, ns)
+    late_moves = low_exchange("dp", nd, (slim_d, norm_d), 10)
+
+    def finalize_narrow(index, rows):
+        narrow_rows[index] = rows
+        narrow_cols_fine[index] = jnp.transpose(triple_second(rows)).astype(BF)
+
+    arrive(early_moves)
+    finalize_narrow(3, total(thin_s, ns) * share)
+    broad = total(broad_s, ns) * share
+    inner_sum[...] = broad[24:32]
+    for index in range(3):
+        part = broad[8 * index : 8 * index + 8]
+        wide_rows[index] = part
+        if index < 2:
+            wide_rows_fine[index] = triple_second(part).astype(BF)
+        else:
+            down_cols_fine[...] = jnp.transpose(triple_second(part)).astype(BF)
+    arrive(late_moves)
+    slim = total(slim_d, nd) * share
+    for index in range(3):
+        finalize_narrow(index, slim[8 * index : 8 * index + 8])
+    extra_sum[0:2] = total(norm_d, nd)[0:2] * share
 
     for image in range(images):
         for copy in (
@@ -750,14 +771,14 @@
         copy.wait_send()
 
 
-def block(mesh_sizes, tokens, keep, mask, cosine, sine, norm_pack, inner_pack, w_qkv, hbm):
+def block(mesh_sizes, small, hbm):
     nd, ns, nt = mesh_sizes
-    images, own, width = tokens.shape
+    images, own, width = hbm[0].shape
     seq_rows = 2 * own
     slots = ns * seq_rows
-    narrow = w_qkv.shape[1]
+    narrow = hbm[1].shape[1]
     heads = narrow // DH
-    wide = inner_pack.shape[1]
+    wide = small[2].shape[1]
     shape = jax.ShapeDtypeStruct
     outs = (
         shape((images, own, width), F32),
@@ -766,7 +787,15 @@
         shape((narrow, width), F32),
         shape((2, width, wide), F32),
         shape((wide, width), F32),
+        shape((5, RANK, width), F32),
+        shape((5, 3 * RANK, width), BF),
+        shape((2, width, 3 * RANK), BF),
         shape((8, width), F32),
+        shape((4, RANK, narrow), F32),
+        shape((4, narrow, 3 * RANK), BF),
+        shape((3, RANK, wide), F32),
+        shape((2, 3 * RANK, wide), BF),
+        shape((wide, 3 * RANK), BF),
         shape((8, wide), F32),
     )
     vmem = pl.BlockSpec(memory_space=pltpu.VMEM)
@@ -809,8 +838,19 @@
         pltpu.VMEM((2 * narrow, width), F32),
         pltpu.VMEM((2, 8, wide), F32),
         pltpu.VMEM((8, wide), F32),
-        *[pltpu.VMEM(array.shape, F32) for array in hbm],
-        dma((8,)),
+        *[pltpu.VMEM(array.shape, array.dtype) for array in hbm[0:6]],
+        pltpu.VMEM((images, seq_rows, 1), F32),
+        pltpu.VMEM((seq_rows, 128), F32),
+        pltpu.VMEM((seq_rows, 128), F32),
+        pltpu.VMEM((8, width), F32),
+        pltpu.VMEM((slots, 8), F32),
+        *[pltpu.VMEM((size, 40, width), F32) for size in (nt, nd, ns)],
+        *[pltpu.VMEM((size, 8, width), F32) for size in (nt, ns, nd)],
+        *[pltpu.VMEM((size, 8, width), F32) for size in (nt, ns, nd)],
+        *[pltpu.VMEM((size, 8, narrow), F32) for size in (nd, ns)],
+        *[pltpu.VMEM((size, 32, wide), F32) for size in (nd, ns)],
+        *[pltpu.VMEM((size, 24, narrow), F32) for size in (ns, nd)],
+        dma((10,)),
         *[dma((images,))] * 2,
         *[dma((4,))] * 2,
         *[dma((images, ns))] * 2,
@@ -818,41 +858,19 @@
         *[dma((images, 5))] * 2,
         *[dma((images, ns))] * 2,
         *[dma((images + 1,))] * 2,
+        *[dma((11, 2, max(mesh_sizes)))] * 2,
     ]
     return pl.pallas_call(
         functools.partial(block_kernel, mesh_sizes, images),
         out_shape=outs,
-        in_specs=[vmem] * 8 + [hbm_spec] * len(hbm),
+        in_specs=[vmem] * len(small) + [hbm_spec] * len(hbm),
         out_specs=[vmem] * len(outs),
         scratch_shapes=scratch,
         compiler_params=pltpu.CompilerParams(
-            collective_id=1, has_side_effects=True, vmem_limit_bytes=62 * 2**20
+            collective_id=0, has_side_effects=True, vmem_limit_bytes=LIMIT * 2**20
         ),
         name="block",
-    )(tokens, keep, mask, cosine, sine, norm_pack, inner_pack, w_qkv, *hbm)
-
-
-def rope_tables(first_slot, count):
-    slot_ids = first_slot + jnp.arange(count, dtype=jnp.int32)
-    inside = jnp.logical_and(slot_ids >= 1, slot_ids <= GRID * GRID)
-    patch = jnp.where(inside, slot_ids - 1, 0)
-    row_pos = (patch // GRID).astype(jnp.float32)
-    col_pos = (patch % GRID).astype(jnp.float32)
-    quarter = DH // 4
-    freqs = 10000.0 ** (-jnp.arange(quarter, dtype=jnp.float32) / quarter)
-    angles = jnp.concatenate([row_pos[:, None] * freqs, col_pos[:, None] * freqs], -1) * (
-        16.0 / GRID
-    )
-    return (jnp.cos(angles), jnp.sin(angles))
-
-
-def quarter_lanes(first, second, narrow, rest):
-    pairs = jnp.stack(
-        [first[:, :QUARTER], second[:, :QUARTER], first[:, QUARTER:], second[:, QUARTER:]], 1
-    )
-    head = pairs.reshape(first.shape[0], DH)
-    keys = jnp.tile(head, (1, narrow // DH))
-    return jnp.concatenate([keys, jnp.full_like(keys, rest)], -1)
+    )(*small, *hbm)
 
 
 def per_device(
@@ -881,30 +899,24 @@
     basis_down,
 ):
     own_rows, images, width = tokens.shape
-    seq_rows = out_grad.shape[0]
     slot_count = keep_mask.shape[0]
-    narrow = w_out.shape[0]
     sizes = tuple(lax.axis_size(axis) for axis in ("dp", "seq", "tensor"))
-    block_start = lax.axis_index("seq") * seq_rows
-    mask = lax.dynamic_slice_in_dim(keep_mask, block_start, seq_rows, 0)
-    mask = jnp.transpose(mask).astype(F32)[:, :, None]
-    cosine_table, sine_table = rope_tables(block_start, seq_rows)
-    cosine = quarter_lanes(cosine_table, cosine_table, narrow, 1.0)
-    sine = quarter_lanes(-sine_table, sine_table, narrow, 0.0)
 
     def turn(array):
         return jnp.swapaxes(array, -1, -2)
 
-    residual, input_grad, *fulls, extra, inner = block(
+    residual, input_grad, *rest = block(
         sizes,
-        jnp.swapaxes(tokens, 0, 1), jnp.transpose(keep_mask), mask, cosine, sine, norm_pack, inner_pack, turn(w_qkv),
         (
-            w_out, w_gate_up, w_down, jnp.swapaxes(out_grad, 0, 1),
+            jnp.transpose(keep_mask), norm_pack, inner_pack,
+            *(turn(basis) for basis in (basis_qkv, basis_out, basis_gate_up, basis_down)),
+        ),
+        (
+            jnp.swapaxes(tokens, 0, 1), turn(w_qkv), w_out, w_gate_up, w_down, jnp.swapaxes(out_grad, 0, 1),
             turn(error_qkv[0]), error_out[0], error_gate_up[0], error_down[0],
         ),
     )
-    bases = tuple(turn(basis) for basis in (basis_qkv, basis_out, basis_gate_up, basis_down))
-    parts = factors(sizes, fulls, bases, extra, inner)
+    fulls, parts = rest[0:4], rest[4:]
     (
         factor_left, factor_qkv, factor_out, factor_gate_up, factor_down,
         new_error_qkv, new_error_out, new_error_gate_up, new_error_down,

time: 126 us -> 106 us (0.84)
  Pallas kernels: 112 us -> 102 us
  local copies, waits for them, and re-layouts: 10.7 us -> 1.66 us
    pallas_call x1 -> x0, Pallas kernels: 34.8 us -> none  [factors(): pl.pallas_call(functools.partial(factor_kernel, mesh_sizes), out_shape=ou...]
    pallas_call x1, Pallas kernels: 70.1 us -> 93.3 us  [block(): pl.pallas_call(functools.partial(block_kernel, mesh_sizes, images), out_s...]
    unnamed x50 -> x6, local copies, waits for them, and re-layouts: 7.82 us -> 1.66 us
    concatenate x2 -> x0, local copies, waits for them, and re-layouts: 1.57 us -> none  [quarter_lanes(): return jnp.concatenate([keys, jnp.full_like(keys, rest)], -1)]
    pallas_call x1, Pallas kernels: 7.44 us -> 8.86 us  [update(): pl.pallas_call(update_kernel, grid=(steps,), out_shape=[*small, *like, *l...]
where the time goes in v1:
time: 106 us
  Pallas kernels  102 us (96%)
  local copies, waits for them, and re-layouts  1.66 us (2%)
  other arithmetic  1.41 us (1%)
    pallas_call x1, Pallas kernels, block(): pl.pallas_call(functools.partial(block_kernel, mesh_sizes, images), out_s...  93.3 us
    pallas_call x1, Pallas kernels, update(): pl.pallas_call(update_kernel, grid=(steps,), out_shape=[*small, *like, *l...  8.86 us

profile of v1, /device:TPU:0, one launch (start us, length us, event | category | flops | bytes accessed | tf_op | source)
XLA Modules:
  0.0 105.9 jit_solution(12979408650156699068)
XLA Ops:
  0.7 93.3 %block.1 = (f32[3,136,384]{2,1,0:T(8,128)}, f32[3,136,384]{2,1,0:T(8,128)}, f32[3,192,384]{2,1,0:T(8,128)}, f32[192,384]{1,0:T(8,128)}, f32[2,384,512]{2,1,0:T(8...) custom-call(s32[3,1088]{1,0:T(4,128)} %bitcast.43, ...), custom_call_target="tpu_custom_call" | custom-call | tf_op jit(solution)/shard_map/block/pallas_call | solution.py:863
  94.0 0.0 copy-start.1
  94.0 8.9 %update.1 = (f32[5,8,384]{2,1,0:T(8,128)}, f32[3,8,192]{2,1,0:T(8,128)}, f32[8,192]{1,0:T(8,128)}, f32[2,8,512]{2,1,0:T(8,128)}, f32[8,512]{1,0:T(8,128)}, /*ind...) custom-call(f32[3,192,384]{2,1,0:T(8,128)} %get-tuple-element.63.ref, ...), custom_call_target="tpu_custom_call" | custom-call | tf_op jit(solution)/shard_map/update/pallas_call | solution.py:198
  102.8 0.0 copy-start
  102.9 0.9 slice_reduce_fusion
  103.7 0.5 multiply_sqrt_fusion
  104.3 0.0 copy-done.1
  104.3 0.8 copy.49
  105.1 0.0 copy-done
  105.1 0.8 copy.50
Async XLA Ops:
  94.0 10.3 %copy-start.1 = (f32[3,136,384]{2,1,0:T(8,128)S(1)}, f32[3,136,384]{2,1,0:T(8,128)}, u32[]{:S(2)}) copy-start(f32[3,136,384]{2,1,0:T(8,128)} %get-tuple-element.61) | copy-start | bytes 1880068
  102.8 2.3 %copy-start = (f32[3,136,384]{2,1,0:T(8,128)S(1)}, f32[3,136,384]{2,1,0:T(8,128)}, u32[]{:S(2)}) copy-start(f32[3,136,384]{2,1,0:T(8,128)} %get-tuple-element.62) | copy-start | bytes 1880068

commit v2 on v1

--- a/solution.py
+++ b/solution.py
@@ -14,7 +14,7 @@
 RANK = 8
 QUARTER = DH // 4
 CHUNK = 16
-LIMIT = 62
+LIMIT = 43
 
 
 EPSILON = 1e-06
@@ -42,11 +42,9 @@
 def fine_dot(left, right, dims):
     left_high, left_low = split(left)
     right_high, right_low = split(right)
-    return (
-        dot(left_high, right_high, dims)
-        + dot(left_high, right_low, dims)
-        + dot(left_low, right_high, dims)
-    )
+    both = jnp.concatenate([left_high.astype(F32), left_low.astype(F32)], 0).astype(BF)
+    rows = dot(both, right_high, dims)
+    return rows[0:RANK] + rows[RANK:] + dot(left_high, right_low, dims)
 
 
 def gram_schmidt(stack):
@@ -80,6 +78,25 @@
     return copies
 
 
+def scatter(axis, size, pieces, inbox, sends, receives):
+    me = lax.axis_index(axis)
+    inbox[me] = pieces[me]
+    copies = []
+    for step in range(1, size):
+        peer = lax.rem(me + step, size)
+        copy = pltpu.make_async_remote_copy(
+            src_ref=pieces.at[peer],
+            dst_ref=inbox.at[me],
+            send_sem=sends.at[0, step],
+            recv_sem=receives.at[0, step],
+            device_id={axis: peer},
+            device_id_type=MESH,
+        )
+        copy.start()
+        copies.append(copy)
+    return copies
+
+
 def arrive(copies):
     for copy in copies:
         copy.wait()
@@ -111,107 +128,34 @@
     return jnp.concatenate([high.astype(F32), low.astype(F32), high.astype(F32)], 0)
 
 
-def update_kernel(*refs):
-    (
-        full_qkv, full_out, full_gate_up, full_down,
-        moment_qkv, moment_out, moment_gate_up, moment_down,
-        w_qkv, w_out, w_gate_up, w_down,
-        left_rows, left_rows_fine, left_cols_fine, extra_sum,
-        narrow_rows, narrow_cols_fine, wide_rows, wide_rows_fine, down_cols_fine, inner_sum,
-        norm_pack, moment_norm, inner_pack, moment_inner,
-        factor_left, factor_qkv, factor_out, factor_gate_up, factor_down,
-        error_qkv, error_out, error_gate_up, error_down,
-        new_moment_qkv, new_moment_out, new_moment_gate_up, new_moment_down, new_moment_norm, new_moment_inner,
-        new_w_qkv, new_w_out, new_w_gate_up, new_w_down, new_norm_pack, new_inner_pack,
-    ) = refs
-
-    def put(approx, full, moment, weight, error, new_moment, new_weight):
-        error[...] = full[...] - approx
-        fresh = MOMENTUM * moment[...] + approx
-        new_moment[...] = fresh
-        new_weight[...] = weight[...] - STEP_RATE * fresh
-
-    for index in range(3):
-        put(
-            dot(narrow_cols_fine[index], left_rows_fine[0], NN),
-            *(ref.at[index] for ref in (full_qkv, moment_qkv, w_qkv, error_qkv, new_moment_qkv, new_w_qkv)),
-        )
-    put(
-        dot(narrow_cols_fine[3], left_rows_fine[1], NN),
-        full_out, moment_out, w_out, error_out, new_moment_out, new_w_out,
-    )
+def store_kernel(count, total_rows, *refs):
+    sources, squares = refs[:count], refs[count]
+    targets, branch_rms, sems = refs[count + 1 : 2 * count + 1], refs[2 * count + 1], refs[2 * count + 2]
+    copies = [
+        pltpu.make_async_copy(source, target, sems.at[number])
+        for number, (source, target) in enumerate(zip(sources, targets))
+    ]
+    for copy in copies:
+        copy.start()
+    roots = jnp.sqrt(jnp.sum(squares[...], -1, keepdims=True) / total_rows)
     for index in range(2):
-        put(
-            dot(left_cols_fine[index], wide_rows_fine[index], NN),
-            *(ref.at[index] for ref in (full_gate_up, moment_gate_up, w_gate_up, error_gate_up, new_moment_gate_up, new_w_gate_up)),
-        )
-    put(
-        dot(down_cols_fine[...], left_rows_fine[4], NN),
-        full_down, moment_down, w_down, error_down, new_moment_down, new_w_down,
-    )
-
-    @pl.when(pl.program_id(0) == 0)
-    def _():
-        factor_left[...] = left_rows[...]
-        factor_qkv[...] = narrow_rows[0:3]
-        factor_out[...] = narrow_rows[3]
-        factor_gate_up[...] = wide_rows[0:2]
-        factor_down[...] = wide_rows[2]
-        fresh = MOMENTUM * moment_norm[...] + extra_sum[0:4]
-        new_moment_norm[...] = fresh
-        new_norm_pack[...] = norm_pack[...] - STEP_RATE * fresh
-        fresh = MOMENTUM * moment_inner[...] + inner_sum[0:2]
-        new_moment_inner[...] = fresh
-        new_inner_pack[...] = inner_pack[...] - STEP_RATE * fresh
-
-
-def update(fulls, moments, weights, parts, norms):
-    steps = 4
-    _, narrow, width = fulls[0].shape
-    wide = fulls[2].shape[-1]
-    part = width // steps
-
-    def whole(array):
-        zeros = (0,) * array.ndim
-        return pl.BlockSpec(array.shape, lambda step, zeros=zeros: zeros)
-
-    matrices = [
-        pl.BlockSpec((3, narrow // steps, width), lambda step: (0, step, 0)),
-        pl.BlockSpec((narrow // steps, width), lambda step: (step, 0)),
-        pl.BlockSpec((2, part, wide), lambda step: (0, step, 0)),
-        pl.BlockSpec((wide // steps, width), lambda step: (step, 0)),
-    ]
-    specs = [whole(array) for array in parts]
-    specs[2] = pl.BlockSpec((2, part, 3 * RANK), lambda step: (0, step, 0))
-    specs[5] = pl.BlockSpec((4, narrow // steps, 3 * RANK), lambda step: (0, step, 0))
-    specs[8] = pl.BlockSpec((wide // steps, 3 * RANK), lambda step: (step, 0))
-    shape = jax.ShapeDtypeStruct
-    small = [
-        shape((5, RANK, width), F32),
-        shape((3, RANK, narrow), F32),
-        shape((RANK, narrow), F32),
-        shape((2, RANK, wide), F32),
-        shape((RANK, wide), F32),
-    ]
-    like = [shape(array.shape, F32) for array in fulls]
-    norm, inner = shape((4, width), F32), shape((2, wide), F32)
+        branch_rms[index] = roots[index, 0]
+    for copy in copies:
+        copy.wait()
+
+
+def store(arrays, squares, total_rows):
+    vmem = pl.BlockSpec(memory_space=pltpu.VMEM)
+    count = len(arrays)
     return pl.pallas_call(
-        update_kernel,
-        grid=(steps,),
-        out_shape=[*small, *like, *like, norm, inner, *like, norm, inner],
-        in_specs=[*matrices * 3, *specs, *(whole(array) for array in norms)],
-        out_specs=[
-            *(whole(array) for array in small),
-            *matrices * 2,
-            whole(norm),
-            whole(inner),
-            *matrices,
-            whole(norm),
-            whole(inner),
-        ],
-        compiler_params=pltpu.CompilerParams(vmem_limit_bytes=LIMIT * 2**20),
-        name="update",
-    )(*fulls, *moments, *weights, *parts, *norms)
+        functools.partial(store_kernel, count, total_rows),
+        out_shape=[*(jax.ShapeDtypeStruct(array.shape, F32) for array in arrays), jax.ShapeDtypeStruct((2,), F32)],
+        in_specs=[vmem] * (count + 1),
+        out_specs=[*[pl.BlockSpec(memory_space=pltpu.HBM)] * count, pl.BlockSpec(memory_space=pltpu.SMEM)],
+        scratch_shapes=[pltpu.SemaphoreType.DMA((count,))],
+        compiler_params=pltpu.CompilerParams(vmem_limit_bytes=2**20),
+        name="store",
+    )(*arrays, squares)
 
 
 def swap_quarters(tile):
@@ -269,22 +213,24 @@
 
 def block_kernel(sizes, images, *refs):
     (
-        keep, norm_pack, inner_pack, basis_qkv, basis_out, basis_gate_up, basis_down,
+        keep, norm_pack, inner_pack, moment_norm, moment_inner, basis_qkv, basis_out, basis_gate_up, basis_down,
         tokens_hbm, w_qkv_hbm, w_out_hbm, w_gate_up_hbm, w_down_hbm, out_grad_hbm,
         error_qkv_hbm, error_out_hbm, error_gate_up_hbm, error_down_hbm,
-        residual, input_grad, full_qkv, full_out, full_gate_up, full_down,
-        left_rows, left_rows_fine, left_cols_fine, extra_sum,
-        narrow_rows, narrow_cols_fine, wide_rows, wide_rows_fine, down_cols_fine, inner_sum,
+        moment_qkv_hbm, moment_out_hbm, moment_gate_up_hbm, moment_down_hbm,
+        residual, input_grad, factor_left, factor_qkv, factor_out, factor_gate_up, factor_down,
+        full_qkv, full_out, full_gate_up, full_down,
+        moment_qkv, moment_out, moment_gate_up, moment_down, new_moment_norm, new_moment_inner,
+        w_qkv, w_out, w_gate_up, w_down, new_norm_pack, new_inner_pack, squares,
         normed_one, normed_one_all, keys_values, queries, probs, scores, grad_scores,
         attended, attended_low, attended_in, attended_send,
         out_low, gate_up_low, down_low, inner_all, query_low, key_value_low,
         normed_two, grad_middle_low, grad_middle, normed_three, grad_gate, grad_up,
         normed_three_send, grad_gate_send, grad_up_send,
         grad_attended, grad_attended_send, grad_attended_all, grad_query, grad_query_low, grad_pairs,
-        pairs_send, pairs_recv, grad_one, grad_one_recv, sum_query, sum_pairs, inner_sums, inner_recv,
-        tokens, w_qkv, w_out, w_gate_up, w_down, out_grad, mask, cosine, sine, extra, kept_rows,
-        early_t, early_d, early_s, late_t, late_s, late_d, norm_t, norm_s, norm_d,
-        thin_d, thin_s, broad_d, broad_s, slim_s, slim_d,
+        pairs_send, pairs_x, pairs_y, relay_x, relay_y, grad_one, grad_one_recv, sum_query, sum_pairs, inner_sums, inner_recv,
+        tokens, out_grad, mask, cosine, sine, extra, kept_rows,
+        early_t, early_all, early_in, early_d, early_left, late_t, late_s, late_d, norm_t, norm_s, norm_d,
+        right_all, right_in, right_d, right_sum, slim_s, slim_d, thin_s, thin_d,
         local_sems, one_send, one_recv, weight_send, weight_recv, pair_send, pair_recv,
         att_send, att_recv, datt_send, datt_recv, rows_send, rows_recv, back_send, back_recv,
         final_send, final_recv, low_send, low_recv,
@@ -292,13 +238,19 @@
     nd, ns, nt = sizes
     me_t, me_s = lax.axis_index("tensor"), lax.axis_index("seq")
     other = 1 - me_t
+    near_x = me_s + 1 - 2 * lax.rem(me_s, 2)
+    near_y = lax.rem(me_s + 2, 4)
+    far = 3 - me_s
     me_d = lax.axis_index("dp")
     own, width = tokens.shape[1], tokens.shape[2]
     seq_rows = 2 * own
     slots = ns * seq_rows
     heads = w_qkv.shape[1] // DH
-    hidden_all = 2 * w_down.shape[0]
+    wide = w_down.shape[0]
+    hidden_all = 2 * wide
     scale = (images * seq_rows) ** (-0.5)
+    top = (own + 15) // 16 * 16
+    upper, lower = slice(0, top), slice(top, seq_rows)
     own_rows = pl.ds(pl.multiple_of(me_t * own, 8), own)
     other_rows = pl.ds(pl.multiple_of(other * own, 8), own)
 
@@ -312,6 +264,8 @@
                 (w_out_hbm, w_out), (w_gate_up_hbm, w_gate_up), (w_down_hbm, w_down), (out_grad_hbm, out_grad),
                 (error_qkv_hbm, full_qkv), (error_out_hbm, full_out),
                 (error_gate_up_hbm, full_gate_up), (error_down_hbm, full_down),
+                (moment_qkv_hbm, moment_qkv), (moment_out_hbm, moment_out),
+                (moment_gate_up_hbm, moment_gate_up), (moment_down_hbm, moment_down),
             )
         )
     ]
@@ -324,10 +278,10 @@
             device_id={"tensor": other}, device_id_type=MESH,
         )
 
-    def to_seq(source, target, send, receive, step):
+    def to_seq(source, target, send, receive, peer):
         return pltpu.make_async_remote_copy(
             src_ref=source, dst_ref=target, send_sem=send, recv_sem=receive,
-            device_id={"seq": lax.rem(me_s + step, ns)}, device_id_type=MESH,
+            device_id={"seq": peer}, device_id_type=MESH,
         )
 
     def one_copy(image):
@@ -340,12 +294,25 @@
             for number, ref in enumerate((out_low, gate_up_low, down_low, inner_all))
         ]
 
-    def pair_copies(image):
-        block = keys_values.at[image, me_s]
-        return [
-            to_seq(block, block, pair_send.at[image, step], pair_recv.at[image, step], step)
-            for step in range(1, ns)
-        ]
+    def pair_copy(image, tile, kind):
+        place, peer = ((me_s, near_x), (me_s, near_y), (near_x, near_y), (near_y, near_x))[kind]
+        block = keys_values.at[image, tile, place]
+        if kind >= 2:
+            block = block.at[(upper, lower)[kind - 2]]
+        return to_seq(block, block, pair_send.at[image, tile, kind], pair_recv.at[image, tile, kind], peer)
+
+    def send_pairs(image, tile):
+        for kind in range(2):
+            pair_copy(image, tile, kind).start()
+
+    def forward_pairs(image, tile):
+        for kind in range(2):
+            pair_copy(image, tile, kind).wait_recv()
+            pair_copy(image, tile, 2 + kind).start()
+
+    def await_pairs(image, tile):
+        for kind in range(2, 4):
+            pair_copy(image, tile, kind).wait_recv()
 
     def att_copy(image):
         return to_partner(
@@ -370,14 +337,26 @@
             for number, (source, target) in enumerate(moves)
         ]
 
-    def back_copies(image):
-        return [
-            to_seq(
-                pairs_send.at[image, lax.rem(me_s + step, ns)], pairs_recv.at[image, step],
-                back_send.at[image, step], back_recv.at[image, step], step,
-            )
-            for step in range(1, ns)
-        ]
+    def back_copy(image, kind):
+        place, rows, target, there, peer = (
+            (far, upper, relay_x, slice(0, top), near_x),
+            (far, lower, relay_y, slice(0, seq_rows - top), near_y),
+            (near_x, upper, pairs_x, upper, near_x),
+            (near_y, lower, pairs_y, lower, near_y),
+            (near_x, lower, pairs_x, lower, near_x),
+            (near_y, upper, pairs_y, upper, near_y),
+        )[kind]
+        return to_seq(
+            pairs_send.at[image, place, rows], target.at[image, there],
+            back_send.at[image, kind], back_recv.at[image, kind], peer,
+        )
+
+    def relay_back(image):
+        for place, rows, inbox, arrival, onward in ((near_y, upper, relay_x, 0, 5), (near_x, lower, relay_y, 1, 4)):
+            back_copy(image, arrival).wait_recv()
+            value = pairs_send[image, place, rows].astype(F32) + inbox[image].astype(F32)
+            pairs_send[image, place, rows] = value.astype(BF)
+            back_copy(image, onward).start()
 
     def final_copy(image):
         return to_partner(
@@ -418,9 +397,14 @@
         blocks = [normed_one[half, image] for half in range(2)]
         pairs = jnp.concatenate([dot(block, key_value_low[...], NT) for block in blocks], 0)
         pairs = turn_pairs(pairs, cosine[...], sine[...])
-        keys_values[image, me_s] = pairs.astype(BF)
-        for copy in pair_copies(image):
-            copy.start()
+        for tile in range(3):
+            keys_values[image, tile, me_s] = pairs[:, 128 * tile : 128 * tile + 128].astype(BF)
+
+        @pl.when(image == 0)
+        def _():
+            for tile in range(3):
+                send_pairs(image, tile)
+
         raw = jnp.concatenate([dot(block, query_low[...], NT) for block in blocks], 0)
         raw = turn_queries(raw, cosine[...], sine[...]) * (DH ** (-0.5))
         lane = lax.broadcasted_iota(jnp.int32, (1, 128), 1)
@@ -446,40 +430,73 @@
     extra[...] = jnp.zeros_like(extra)
     inner_sums[...] = jnp.zeros_like(inner_sums)
 
-    def half_mask(half):
+    def halves_of(lower, upper):
         lane = lax.broadcasted_iota(jnp.int32, (1, 128), 1)
-        return lax.div(lane, DH) == half
-
-    def tile_of(index):
-        return pl.ds(pl.multiple_of(index * 128, 128), 128)
+        return jnp.where(lane < DH, lower, upper)
+
+    def half_of(value, half):
+        return halves_of(value, 0.0) if half == 0 else halves_of(0.0, value)
 
     def key_tile(image, index):
-        return keys_values[image, :, :, tile_of(index)].reshape(slots, 128)
+        return keys_values[image, index].reshape(slots, 128)
 
     def attend(image):
-        for copy in pair_copies(image):
-            copy.wait_recv()
+        @pl.when(image == 0)
+        def _():
+            forward_pairs(0, 0)
+            forward_pairs(0, 1)
+            send_pairs(1, 0)
+            forward_pairs(0, 2)
+            send_pairs(1, 1)
+            send_pairs(1, 2)
+
         bias = jnp.where(keep[pl.ds(image, 1), :] > 0, 0.0, -1e30)
-        attended[...] = jnp.zeros_like(attended)
-
-        def head_step(head, carry):
-            scores[...] = dot(queries[image * heads + head], key_tile(image, lax.div(head, 2)), NT)
+
+        def score(head):
+            scores[head % 2] = dot(queries[image * heads + head], key_tile(image, head // 2), NT)
+
+        def chances(head):
             for start in range(0, seq_rows, CHUNK):
                 rows = slice(start, start + CHUNK)
-                part = scores[rows] + bias
+                part = scores[head % 2, rows] + bias
                 part = jnp.exp(part - jnp.max(part, -1, keepdims=True))
                 part = part * (1.0 / jnp.sum(part, -1, keepdims=True))
                 probs[image * heads + head, rows] = part.astype(BF)
-            place = lax.div(head + 1, 2)
-            mixed = dot(probs[image * heads + head], key_tile(image, place + 1), NN)
-            attended[:, tile_of(place)] += jnp.where(half_mask(lax.rem(head + 1, 2)), mixed, 0.0)
-            return carry
-
-        lax.fori_loop(0, heads, head_step, 0)
+
+        def mix(head):
+            return dot(probs[image * heads + head], key_tile(image, 1 + (head + 1) // 2), NN)
+
+        await_pairs(image, 0)
+        score(0)
+        score(1)
+        chances(0)
+        await_pairs(image, 1)
+        score(2)
+        mixed = [mix(0)]
+        chances(1)
+        await_pairs(image, 2)
+        mixed.append(mix(1))
+        chances(2)
+        mixed.append(mix(2))
+        attended[:, 0:128] = half_of(mixed[0], 1)
+        attended[:, 128:256] = halves_of(mixed[1], mixed[2])
         attended_low[image] = attended[...].astype(BF)
         attended_in[me_t, image] = attended[own_rows].astype(BF)
         attended_send[image] = attended[other_rows].astype(BF)
         att_copy(image).start()
+
+        @pl.when(image == 0)
+        def _():
+            forward_pairs(1, 0)
+            forward_pairs(1, 1)
+
+        @pl.when(image == 1)
+        def _():
+            forward_pairs(2, 0)
+
+        @pl.when(image == 2)
+        def _():
+            relay_back(0)
 
     def feed(image):
         att_copy(image).wait_recv()
@@ -507,6 +524,13 @@
         branch = sum(dot(low, down_low[half], NN) for low, half in zip(lows, halves))
         extra[5:6] += column_sums(branch * branch)
         residual[image] = middle + branch
+
+        @pl.when(image == 0)
+        def _():
+            forward_pairs(1, 2)
+            for tile in range(3):
+                send_pairs(2, tile)
+
         cotangent = out_grad[image, own_rows] * mask[image, own_rows]
         grad_branch = cotangent.astype(BF)
         grads = [dot(grad_branch, down_low[half], NT) for half in halves]
@@ -556,67 +580,70 @@
         grad_attended_all[...] = jnp.concatenate(
             [grad_attended[half, image].astype(F32) for half in range(2)], 0
         )
-        grad_query[...] = jnp.zeros_like(grad_query)
-        grad_pairs[...] = jnp.zeros_like(grad_pairs)
-
-        def head_step(head, carry):
-            place = lax.div(head + 1, 2)
-            at_key, at_value = lax.div(head, 2), place + 1
-            key_half, value_half = half_mask(lax.rem(head, 2)), half_mask(lax.rem(head + 1, 2))
-            wide = jnp.where(value_half, grad_attended_all[:, tile_of(place)], 0.0)
-            low = wide.astype(BF)
-            scores[...] = dot(low, key_tile(image, at_value), NT)
-            delta = jnp.sum(wide * attended_low[image, :, tile_of(place)].astype(F32), -1, keepdims=True)
+        wides = [half_of(grad_attended_all[:, 0:128], 1)]
+        wides += [half_of(grad_attended_all[:, 128:256], half) for half in range(2)]
+        lows = [wide.astype(BF) for wide in wides]
+        mixed = attended_low[image].astype(F32)
+        deltas = [
+            jnp.sum(wide * mixed[:, tile * 128 : tile * 128 + 128], -1, keepdims=True)
+            for wide, tile in zip(wides, (0, 1, 1))
+        ]
+
+        def grad_chance(head):
+            scores[head % 2] = dot(lows[head], key_tile(image, 1 + (head + 1) // 2), NT)
+
+        def grad_score(head):
             for start in range(0, seq_rows, CHUNK):
                 rows = slice(start, start + CHUNK)
                 chance = probs[image * heads + head, rows].astype(F32)
-                grad_scores[rows] = (chance * (scores[rows] - delta[rows])).astype(BF)
-            grad_query[:, tile_of(at_key)] += jnp.where(
-                key_half, dot(grad_scores[...], key_tile(image, at_key), NN), 0.0
-            )
-            query_t = jnp.transpose(queries[image * heads + head].astype(F32)).astype(BF)
-            grad_pairs[tile_of(at_key)] += dot(query_t, grad_scores[...], NN)
-            grad_pairs[tile_of(at_value)] += dot(
-                jnp.transpose(wide).astype(BF), probs[image * heads + head], NN
-            )
-            return carry
-
-        lax.fori_loop(0, heads, head_step, 0)
+                grad_scores[head, rows] = (chance * (scores[head % 2, rows] - deltas[head][rows])).astype(BF)
+
+        def pair_rows(place, wide, half, right):
+            rows = jnp.transpose(wide)[half * DH : half * DH + DH].astype(BF)
+            grad_pairs[place * DH : place * DH + DH] = dot(rows, right, NN)
+
+        def value_grad(head):
+            pair_rows(heads + head, wides[head], (head + 1) % 2, probs[image * heads + head])
+
+        def key_grad(head):
+            wide = queries[image * heads + head].astype(F32)
+            pair_rows(head, wide, head % 2, grad_scores[head])
+
+        def query_grad(head):
+            return dot(grad_scores[head], key_tile(image, head // 2), NN)
+
+        grad_chance(0)
+        grad_chance(1)
+        value_grad(0)
+        grad_score(0)
+        grad_chance(2)
+        value_grad(1)
+        grad_score(1)
+        query_grads = [query_grad(0)]
+        key_grad(0)
+        value_grad(2)
+        grad_score(2)
+        query_grads.append(query_grad(1))
+        key_grad(1)
+        query_grads.append(query_grad(2))
+        key_grad(2)
+        grad_query[:, 0:128] = halves_of(query_grads[0], query_grads[1])
+        grad_query[:, 128:256] = half_of(query_grads[2], 0)
         pairs = jnp.transpose(grad_pairs[...])
         pairs_send[image] = pairs.astype(BF).reshape(ns, seq_rows, width)
-        for copy in back_copies(image):
-            copy.start()
+
+        @pl.when(image == 0)
+        def _():
+            forward_pairs(2, 1)
+            forward_pairs(2, 2)
+
+        for kind in range(4):
+            back_copy(image, kind).start()
         raw = grad_query[...] * (DH ** (-0.5))
         raw = turn_queries(raw, cosine[...], -sine[...])
         grad_query_low[image] = raw.astype(BF)
 
-    def stage(step, carry):
-        @pl.when(step < images)
-        def _():
-            attend(step)
-
-        @pl.when(step >= 1)
-        def _():
-            attend_back(step - 1)
-
-        @pl.when(step == 0)
-        def _():
-            for copy in weight_copies():
-                copy.wait_recv()
-
-        @pl.when(step < images)
-        def _():
-            feed(step)
-
-        return carry
-
-    lax.fori_loop(0, images + 1, stage, 0)
-    inner_copy().start()
-
-    for load in loads[7:10]:
-        load.wait()
-
-    def weights(image, carry):
+    def weights(image):
         for copy in row_copies(image):
             copy.wait_recv()
         for half in range(2):
@@ -628,33 +655,61 @@
             full_gate_up[1] += dot(rows_two, grad_up[half, image], TN) * scale
             mixed = attended_low[image].astype(F32)[place].astype(BF)
             full_out[...] += dot(mixed, grad_middle_low[half, image], TN)[256 - narrow :] * scale
+
+    def stage(step, carry):
+        @pl.when(step < images)
+        def _():
+            attend(step)
+
+        @pl.when(step == images)
+        def _():
+            for load in loads[7:10]:
+                load.wait()
+            lax.fori_loop(0, images - 1, lambda image, rest: weights(image) or rest, 0)
+            relay_back(1)
+
+        @pl.when(step >= 1)
+        def _():
+            attend_back(step - 1)
+
+        @pl.when(step == 0)
+        def _():
+            for copy in weight_copies():
+                copy.wait_recv()
+
+        @pl.when(step < images)
+        def _():
+            feed(step)
+
         return carry
 
-    lax.fori_loop(0, images, weights, 0)
+    lax.fori_loop(0, images + 1, stage, 0)
+    inner_copy().start()
+
+    weights(images - 1)
 
     def low_exchange(axis, size, buffers, number):
         return exchange(axis, size, buffers, low_send.at[number], low_recv.at[number])
 
+    def low_scatter(pieces, inbox, number):
+        return scatter("seq", ns, pieces, inbox, low_send.at[number], low_recv.at[number])
+
     share = 1.0 / (ns * nd)
     early = early_t.at[me_t]
-    early[0:8] = fine_dot(basis_out[...], full_out[...], NN)
+    early[0] = fine_dot(basis_out[...], full_out[...], NN)
     for index in range(2):
-        early[8 + 8 * index : 16 + 8 * index] = fine_dot(
-            basis_gate_up[index], full_gate_up[index], NT
-        )
-    early[24:32] = fine_dot(basis_down[...], full_down[...], NN)
-    early[32:40] = extra[...]
-    moves = low_exchange("tensor", nt, (early_t,), 0)
+        early[1 + index] = fine_dot(basis_gate_up[index], full_gate_up[index], NT)
+    early[3] = fine_dot(basis_down[...], full_down[...], NN)
+    early_moves = low_exchange("tensor", nt, (early_t,), 0)
 
     sum_query[...] = jnp.zeros_like(sum_query)
     sum_pairs[...] = jnp.zeros_like(sum_pairs)
 
     def finish_pairs(image):
-        for copy in back_copies(image):
-            copy.wait_recv()
+        for kind in range(2, 6):
+            back_copy(image, kind).wait_recv()
         pairs = pairs_send[image, me_s].astype(F32)
-        for step in range(1, ns):
-            pairs = pairs + pairs_recv[image, step].astype(F32)
+        pairs = pairs + pairs_x[image].astype(F32) + pairs_y[image].astype(F32)
         pairs = turn_pairs(pairs, cosine[...], -sine[...]).astype(BF)
         query = grad_query_low[image]
         grad_one[image] = dot(query, query_low[...], NN) + dot(pairs, key_value_low[...], NN)
@@ -663,23 +718,23 @@
         sum_pairs[...] += dot(pairs, normed_one_all[image], TN)
 
     finish_pairs(0)
-    arrive(moves)
-    early_d[me_d] = total(early_t, nt)
-    early_moves = low_exchange("dp", nd, (early_d,), 1)
-
-    def rest_pairs(image, carry):
-        finish_pairs(image)
-        return carry
-
-    lax.fori_loop(1, images, rest_pairs, 0)
+    arrive(early_moves)
+    early_all[...] = total(early_t, nt)
+    early_moves = low_scatter(early_all, early_in, 1)
+    relay_back(images - 1)
+    finish_pairs(1)
+    arrive(early_moves)
+    early_d[me_d] = total(early_in, ns)
+    early_moves = low_exchange("dp", nd, (early_d,), 2)
+    finish_pairs(2)
     loads[6].wait()
     full_qkv[0] += sum_query[0:narrow] * scale
     full_qkv[1] += sum_pairs[0:narrow] * scale
     full_qkv[2] += sum_pairs[narrow : 2 * narrow] * scale
     late_t[me_t] = sum(fine_dot(basis_qkv[index], full_qkv[index], NN) for index in range(3))
-    late_moves = low_exchange("tensor", nt, (late_t,), 2)
-
-    norm_t[me_t] = jnp.zeros_like(norm_t[me_t])
+    late_moves = low_exchange("tensor", nt, (late_t,), 3)
+
+    norm_t[me_t] = extra[...]
 
     def finish(image, carry):
         final_copy(image).wait_recv()
@@ -690,81 +745,94 @@
         norm_t[me_t, 1:2] += column_sums(grad)
         return carry
 
-    def finalize_left(index, rows):
-        left_rows[index] = rows
-        triple = triple_first(rows)
-        left_rows_fine[index] = triple.astype(BF)
-        if index in (2, 3):
-            left_cols_fine[index - 2] = jnp.transpose(triple).astype(BF)
+    def settle(left, right, full, moment, weight):
+        approx = dot(triple_second(right).astype(BF), triple_first(left).astype(BF), TN)
+        full[...] = full[...] - approx
+        fresh = MOMENTUM * moment[...] + approx
+        moment[...] = fresh
+        weight[...] = weight[...] - STEP_RATE * fresh
+
+    def orthonormal(rows):
+        return gram_schmidt(rows.reshape(1, RANK, width))[0]
 
     arrive(late_moves)
     late_s[me_s] = total(late_t, nt)
-    late_moves = low_exchange("seq", ns, (late_s,), 3)
+    late_moves = low_exchange("seq", ns, (late_s,), 4)
+    arrive(early_moves)
+    early_left[me_s] = orthonormal(total(early_d, nd))
+    early_moves = low_exchange("seq", ns, (early_left,), 5)
     lax.fori_loop(0, images, finish, 0)
-    norm_moves = low_exchange("tensor", nt, (norm_t,), 4)
-    arrive(early_moves)
-    early_s[me_s] = total(early_d, nd)
-    early_moves = low_exchange("seq", ns, (early_s,), 5)
+    norm_moves = low_exchange("tensor", nt, (norm_t,), 6)
     arrive(late_moves)
     late_d[me_d] = total(late_s, ns)
-    late_moves = low_exchange("dp", nd, (late_d,), 6)
+    late_moves = low_exchange("dp", nd, (late_d,), 7)
     arrive(early_moves)
-    summed = total(early_s, ns)
-    extra_sum[2:4] = summed[34:36] * (share * scale)
-    extra_sum[4:6] = summed[36:38]
-    extra_sum[6:8] = jnp.zeros_like(extra_sum[6:8])
-    left = gram_schmidt(summed[0:32].reshape(4, RANK, width))
+    right_all[0, :, 0:narrow] = fine_dot(early_left[0], full_out[...], NT)
+    right_all[0, :, narrow:] = jnp.zeros((RANK, wide - narrow), F32)
+    for index in range(2):
+        right_all[1 + index] = fine_dot(early_left[1 + index], full_gate_up[index], NN)
+    right_all[3] = fine_dot(early_left[3], full_down[...], NT)
+    early_moves = low_scatter(right_all, right_in, 8)
     for index in range(4):
-        finalize_left(index + 1, left[index])
-    thin_d[me_d] = fine_dot(left[0], full_out[...], NT)
-    for index in range(2):
-        broad_d[me_d, 8 * index : 8 * index + 8] = fine_dot(left[1 + index], full_gate_up[index], NN)
-    broad_d[me_d, 16:24] = fine_dot(left[3], full_down[...], NT)
+        factor_left[1 + index] = early_left[index]
     inner_copy().wait_recv()
-    broad_d[me_d, 24:32] = (inner_sums[me_t] + inner_recv[...]) * scale
-    early_moves = low_exchange("dp", nd, (thin_d, broad_d), 7)
+    thin_s[me_s] = (inner_sums[me_t] + inner_recv[...]) * scale
     arrive(norm_moves)
-    norm_s[me_s] = total(norm_t, nt) * scale
+    norm_s[me_s] = total(norm_t, nt)
+    arrive(early_moves)
+    right_d[me_d] = total(right_in, ns)
+    early_moves = low_exchange("dp", nd, (right_d,), 9)
     arrive(late_moves)
-    left = gram_schmidt(total(late_d, nd).reshape(1, RANK, width))[0]
+    left = orthonormal(total(late_d, nd))
     for index in range(3):
         slim_s[me_s, 8 * index : 8 * index + 8] = fine_dot(left, full_qkv[index], NT)
-    late_moves = low_exchange("seq", ns, (slim_s, norm_s), 8)
-    finalize_left(0, left)
-    arrive(early_moves)
-    thin_s[me_s] = total(thin_d, nd)
-    broad_s[me_s] = total(broad_d, nd)
-    early_moves = low_exchange("seq", ns, (thin_s, broad_s), 9)
+    late_moves = low_exchange("seq", ns, (slim_s, norm_s, thin_s), 10)
+    factor_left[0] = left
+    for load in loads[10:14]:
+        load.wait()
     arrive(late_moves)
     slim_d[me_d] = total(slim_s, ns)
     norm_d[me_d] = total(norm_s, ns)
-    late_moves = low_exchange("dp", nd, (slim_d, norm_d), 10)
-
-    def finalize_narrow(index, rows):
-        narrow_rows[index] = rows
-        narrow_cols_fine[index] = jnp.transpose(triple_second(rows)).astype(BF)
-
+    thin_d[me_d] = total(thin_s, ns)
+    late_moves = low_exchange("dp", nd, (slim_d, norm_d, thin_d), 11)
     arrive(early_moves)
-    finalize_narrow(3, total(thin_s, ns) * share)
-    broad = total(broad_s, ns) * share
-    inner_sum[...] = broad[24:32]
-    for index in range(3):
-        part = broad[8 * index : 8 * index + 8]
-        wide_rows[index] = part
-        if index < 2:
-            wide_rows_fine[index] = triple_second(part).astype(BF)
-        else:
-            down_cols_fine[...] = jnp.transpose(triple_second(part)).astype(BF)
+    right_sum[me_s] = total(right_d, nd) * share
+    early_moves = low_exchange("seq", ns, (right_sum,), 12)
+    arrive(early_moves)
+    right = right_sum[0, :, 0:narrow]
+    factor_out[...] = right
+    settle(early_left[0], right, full_out, moment_out, w_out)
+    for index in range(2):
+        right = right_sum[1 + index]
+        factor_gate_up[index] = right
+        left_triple, right_triple = triple_first(early_left[1 + index]), triple_second(right)
+        approx = dot(left_triple.astype(BF), right_triple.astype(BF), TN)
+        full_gate_up[index] = full_gate_up[index] - approx
+        fresh = MOMENTUM * moment_gate_up[index] + approx
+        moment_gate_up[index] = fresh
+        w_gate_up[index] = w_gate_up[index] - STEP_RATE * fresh
+    factor_down[...] = right_sum[3]
+    settle(early_left[3], right_sum[3], full_down, moment_down, w_down)
     arrive(late_moves)
     slim = total(slim_d, nd) * share
     for index in range(3):
-        finalize_narrow(index, slim[8 * index : 8 * index + 8])
-    extra_sum[0:2] = total(norm_d, nd)[0:2] * share
+        right = slim[8 * index : 8 * index + 8]
+        factor_qkv[index] = right
+        settle(left, right, full_qkv.at[index], moment_qkv.at[index], w_qkv.at[index])
+    norms = total(norm_d, nd)
+    squares[...] = norms[4:6]
+    fresh = MOMENTUM * moment_norm[...] + norms[0:4] * (share * scale)
+    new_moment_norm[...] = fresh
+    new_norm_pack[...] = norm_pack[...] - STEP_RATE * fresh
+    fresh = MOMENTUM * moment_inner[...] + total(thin_d, nd)[0:2] * share
+    new_moment_inner[...] = fresh
+    new_inner_pack[...] = inner_pack[...] - STEP_RATE * fresh
 
     for image in range(images):
         for copy in (
-            one_copy(image), *pair_copies(image), att_copy(image), datt_copy(image),
-            *row_copies(image), *back_copies(image), final_copy(image),
+            one_copy(image), att_copy(image), datt_copy(image), *row_copies(image), final_copy(image),
+            *(pair_copy(image, tile, kind) for tile in range(3) for kind in range(4)),
+            *(back_copy(image, kind) for kind in range(6)),
         ):
             copy.wait_send()
     for copy in (*weight_copies(), inner_copy()):
@@ -776,39 +844,29 @@
     images, own, width = hbm[0].shape
     seq_rows = 2 * own
     slots = ns * seq_rows
+    top = (own + 15) // 16 * 16
     narrow = hbm[1].shape[1]
     heads = narrow // DH
     wide = small[2].shape[1]
     shape = jax.ShapeDtypeStruct
-    outs = (
-        shape((images, own, width), F32),
-        shape((images, own, width), F32),
-        shape((3, narrow, width), F32),
-        shape((narrow, width), F32),
-        shape((2, width, wide), F32),
-        shape((wide, width), F32),
-        shape((5, RANK, width), F32),
-        shape((5, 3 * RANK, width), BF),
-        shape((2, width, 3 * RANK), BF),
-        shape((8, width), F32),
-        shape((4, RANK, narrow), F32),
-        shape((4, narrow, 3 * RANK), BF),
-        shape((3, RANK, wide), F32),
-        shape((2, 3 * RANK, wide), BF),
-        shape((wide, 3 * RANK), BF),
-        shape((8, wide), F32),
+    matrices = ((3, narrow, width), (narrow, width), (2, width, wide), (wide, width))
+    shapes = (
+        (images, own, width), (images, own, width),
+        (5, RANK, width), (3, RANK, narrow), (RANK, narrow), (2, RANK, wide), (RANK, wide),
+        *matrices, *matrices, (4, width), (2, wide), *matrices, (4, width), (2, wide), (2, width),
     )
+    outs = [pltpu.VMEM(dims, F32) for dims in shapes]
     vmem = pl.BlockSpec(memory_space=pltpu.VMEM)
-    hbm_spec = pl.BlockSpec(memory_space=pl.ANY)
+    hbm_spec = pl.BlockSpec(memory_space=pltpu.HBM)
     dma = pltpu.SemaphoreType.DMA
     scratch = [
         pltpu.VMEM((2, images, own, width), BF),
         pltpu.VMEM((images, seq_rows, width), BF),
-        pltpu.VMEM((images, ns, seq_rows, width), BF),
+        pltpu.VMEM((images, 3, ns, seq_rows, 128), BF),
         pltpu.VMEM((images * heads, seq_rows, 128), BF),
         pltpu.VMEM((images * heads, seq_rows, slots), BF),
-        pltpu.VMEM((seq_rows, slots), F32),
-        pltpu.VMEM((seq_rows, slots), BF),
+        pltpu.VMEM((2, seq_rows, slots), F32),
+        pltpu.VMEM((heads, seq_rows, slots), BF),
         pltpu.VMEM((seq_rows, 256), F32),
         pltpu.VMEM((images, seq_rows, 256), BF),
         pltpu.VMEM((2, images, own, 256), BF),
@@ -831,34 +889,39 @@
         pltpu.VMEM((images, seq_rows, 256), BF),
         pltpu.VMEM((width, slots), F32),
         pltpu.VMEM((images, ns, seq_rows, width), BF),
-        pltpu.VMEM((images, ns, seq_rows, width), BF),
+        *[pltpu.VMEM((images, seq_rows, width), BF)] * 2,
+        pltpu.VMEM((images, top, width), BF),
+        pltpu.VMEM((images, seq_rows - top, width), BF),
         pltpu.VMEM((images, seq_rows, width), F32),
         pltpu.VMEM((images, own, width), F32),
         pltpu.VMEM((256, width), F32),
         pltpu.VMEM((2 * narrow, width), F32),
         pltpu.VMEM((2, 8, wide), F32),
         pltpu.VMEM((8, wide), F32),
-        *[pltpu.VMEM(array.shape, array.dtype) for array in hbm[0:6]],
+        pltpu.VMEM(hbm[0].shape, BF),
+        pltpu.VMEM(hbm[5].shape, F32),
         pltpu.VMEM((images, seq_rows, 1), F32),
         pltpu.VMEM((seq_rows, 128), F32),
         pltpu.VMEM((seq_rows, 128), F32),
         pltpu.VMEM((8, width), F32),
         pltpu.VMEM((slots, 8), F32),
-        *[pltpu.VMEM((size, 40, width), F32) for size in (nt, nd, ns)],
-        *[pltpu.VMEM((size, 8, width), F32) for size in (nt, ns, nd)],
-        *[pltpu.VMEM((size, 8, width), F32) for size in (nt, ns, nd)],
-        *[pltpu.VMEM((size, 8, narrow), F32) for size in (nd, ns)],
-        *[pltpu.VMEM((size, 32, wide), F32) for size in (nd, ns)],
-        *[pltpu.VMEM((size, 24, narrow), F32) for size in (ns, nd)],
-        dma((10,)),
+        pltpu.VMEM((nt, 4, RANK, width), F32),
+        pltpu.VMEM((4, RANK, width), F32),
+        *[pltpu.VMEM((size, RANK, width), F32) for size in (ns, nd, ns)],
+        *[pltpu.VMEM((size, RANK, width), F32) for size in (nt, ns, nd)],
+        *[pltpu.VMEM((size, RANK, width), F32) for size in (nt, ns, nd)],
+        *[pltpu.VMEM((size, RANK, wide), F32) for size in (4, ns, nd, ns)],
+        *[pltpu.VMEM((size, 3 * RANK, narrow), F32) for size in (ns, nd)],
+        *[pltpu.VMEM((size, RANK, wide), F32) for size in (ns, nd)],
+        dma((14,)),
         *[dma((images,))] * 2,
         *[dma((4,))] * 2,
-        *[dma((images, ns))] * 2,
+        *[dma((images, 3, 4))] * 2,
         *[dma((images,))] * 4,
         *[dma((images, 5))] * 2,
-        *[dma((images, ns))] * 2,
+        *[dma((images, 6))] * 2,
         *[dma((images + 1,))] * 2,
-        *[dma((11, 2, max(mesh_sizes)))] * 2,
+        *[dma((13, 3, max(mesh_sizes)))] * 2,
     ]
     return pl.pallas_call(
         functools.partial(block_kernel, mesh_sizes, images),
@@ -867,7 +930,7 @@
         out_specs=[vmem] * len(outs),
         scratch_shapes=scratch,
         compiler_params=pltpu.CompilerParams(
-            collective_id=0, has_side_effects=True, vmem_limit_bytes=LIMIT * 2**20
+            collective_id=0, has_side_effects=True, vmem_limit_bytes=(LIMIT + nd // 8) * 2**20
         ),
         name="block",
     )(*small, *hbm)
@@ -905,32 +968,25 @@
     def turn(array):
         return jnp.swapaxes(array, -1, -2)
 
-    residual, input_grad, *rest = block(
+    *arrays, squares = block(
         sizes,
         (
-            jnp.transpose(keep_mask), norm_pack, inner_pack,
+            jnp.transpose(keep_mask), norm_pack, inner_pack, moment_norm, moment_inner,
             *(turn(basis) for basis in (basis_qkv, basis_out, basis_gate_up, basis_down)),
         ),
         (
             jnp.swapaxes(tokens, 0, 1), turn(w_qkv), w_out, w_gate_up, w_down, jnp.swapaxes(out_grad, 0, 1),
             turn(error_qkv[0]), error_out[0], error_gate_up[0], error_down[0],
+            turn(moment_qkv), moment_out, moment_gate_up, moment_down,
         ),
     )
-    fulls, parts = rest[0:4], rest[4:]
     (
-        factor_left, factor_qkv, factor_out, factor_gate_up, factor_down,
+        residual, input_grad, factor_left, factor_qkv, factor_out, factor_gate_up, factor_down,
         new_error_qkv, new_error_out, new_error_gate_up, new_error_down,
         new_moment_qkv, new_moment_out, new_moment_gate_up, new_moment_down, new_moment_norm, new_moment_inner,
         new_w_qkv, new_w_out, new_w_gate_up, new_w_down, new_norm_pack, new_inner_pack,
-    ) = update(
-        fulls,
-        (turn(moment_qkv), moment_out, moment_gate_up, moment_down),
-        (turn(w_qkv), w_out, w_gate_up, w_down),
-        parts,
-        (norm_pack, moment_norm, inner_pack, moment_inner),
-    )
-    squares = jnp.sum(parts[3][4:6], -1)
-    branch_rms = jnp.sqrt(squares / (slot_count * images * lax.axis_size("dp") * width))
+        branch_rms,
+    ) = store(arrays, squares, float(slot_count * images * lax.axis_size("dp") * width))
     return (
         jnp.swapaxes(residual, 0, 1), jnp.swapaxes(input_grad, 0, 1),
         *(turn(factor) for factor in (factor_left, factor_qkv, factor_out, factor_gate_up, factor_down)),

time: 106 us -> 85.8 us (0.81)
  Pallas kernels: 102 us -> 84.8 us
  local copies, waits for them, and re-layouts: 1.66 us -> 0 us
  other arithmetic: 1.41 us -> 0 us
    pallas_call x1, Pallas kernels: 93.3 us -> 79.5 us  [block(): pl.pallas_call(functools.partial(block_kernel, mesh_sizes, images), out_s...]
    pallas_call x1, Pallas kernels: 8.86 us -> 5.2 us  [store(): pl.pallas_call(functools.partial(store_kernel, count, total_rows), out_sh...]
    unnamed x6 -> x0, local copies, waits for them, and re-layouts: 1.66 us -> none
where the time goes in v2:
time: 85.8 us; the launch traced here: 85.6 us
  Pallas kernels  84.8 us (99%)
    pallas_call x1, Pallas kernels, block(): pl.pallas_call(functools.partial(block_kernel, mesh_sizes, images), out_s...  79.5 us
    pallas_call x1, Pallas kernels, store(): pl.pallas_call(functools.partial(store_kernel, count, total_rows), out_sh...  5.2 us

profile of v2, /device:TPU:0, one launch (start us, length us, event | category | flops | bytes accessed | tf_op | source)
XLA Modules:
  0.0 85.6 jit_solution(638795767250942271)
XLA Ops:
  0.7 79.5 %block.1 = (f32[3,136,384]{2,1,0:T(8,128)S(1)}, f32[3,136,384]{2,1,0:T(8,128)S(1)}, f32[5,8,384]{2,1,0:T(8,128)S(1)}, f32[3,8,192]{2,1,0:T(8,128)S(1)}, f32[8,19...) custom-call(s32[3,1088]{1,0:T(4,128)} %bitcast.40, ...), custom_call_target="tpu_custom_call" | custom-call | tf_op jit(solution)/shard_map/block/pallas_call | solution.py:926
  80.2 5.2 %store.1 = (f32[3,136,384]{2,1,0:T(8,128)}, f32[3,136,384]{2,1,0:T(8,128)}, f32[5,8,384]{2,1,0:T(8,128)}, f32[3,8,192]{2,1,0:T(8,128)}, f32[8,192]{1,0:T(8,128)}...) custom-call(f32[3,136,384]{2,1,0:T(8,128)S(1)} %get-tuple-element.72, ...), custom_call_target="tpu_custom_call" | custom-call | tf_op jit(solution)/shard_map/store/pallas_call | solution.py:150

commit v3 on v2

--- a/solution.py
+++ b/solution.py
@@ -14,7 +14,7 @@
 RANK = 8
 QUARTER = DH // 4
 CHUNK = 16
-LIMIT = 43
+LIMIT = 46
 
 
 EPSILON = 1e-06
@@ -39,12 +39,18 @@
 TN = ((0,), (0,))
 
 
+def two_rows(rows):
+    high, low = split(rows)
+    return jnp.concatenate([high.astype(F32), low.astype(F32)], 0).astype(BF)
+
+
+def fold(rows):
+    return rows[0:RANK] + rows[RANK:]
+
+
 def fine_dot(left, right, dims):
-    left_high, left_low = split(left)
     right_high, right_low = split(right)
-    both = jnp.concatenate([left_high.astype(F32), left_low.astype(F32)], 0).astype(BF)
-    rows = dot(both, right_high, dims)
-    return rows[0:RANK] + rows[RANK:] + dot(left_high, right_low, dims)
+    return fold(dot(two_rows(left), right_high, dims)) + dot(left.astype(BF), right_low, dims)
 
 
 def gram_schmidt(stack):
@@ -59,17 +65,18 @@
     return stack
 
 
-def exchange(axis, size, buffers, sends, receives):
+def exchange(axis, size, buffers, sends, receives, base):
     me = lax.axis_index(axis)
     copies = []
     for step in range(1, size):
         peer = lax.rem(me + step, size)
-        for number, buffer in enumerate(buffers):
+        for buffer in buffers:
+            place = base + len(copies)
             copy = pltpu.make_async_remote_copy(
                 src_ref=buffer.at[me],
                 dst_ref=buffer.at[me],
-                send_sem=sends.at[number, step],
-                recv_sem=receives.at[number, step],
+                send_sem=sends.at[place],
+                recv_sem=receives.at[place],
                 device_id={axis: peer},
                 device_id_type=MESH,
             )
@@ -78,7 +85,7 @@
     return copies
 
 
-def scatter(axis, size, pieces, inbox, sends, receives):
+def scatter(axis, size, pieces, inbox, sends, receives, base):
     me = lax.axis_index(axis)
     inbox[me] = pieces[me]
     copies = []
@@ -87,8 +94,8 @@
         copy = pltpu.make_async_remote_copy(
             src_ref=pieces.at[peer],
             dst_ref=inbox.at[me],
-            send_sem=sends.at[0, step],
-            recv_sem=receives.at[0, step],
+            send_sem=sends.at[base + step - 1],
+            recv_sem=receives.at[base + step - 1],
             device_id={axis: peer},
             device_id_type=MESH,
         )
@@ -128,15 +135,42 @@
     return jnp.concatenate([high.astype(F32), low.astype(F32), high.astype(F32)], 0)
 
 
-def store_kernel(count, total_rows, *refs):
-    sources, squares = refs[:count], refs[count]
-    targets, branch_rms, sems = refs[count + 1 : 2 * count + 1], refs[2 * count + 1], refs[2 * count + 2]
+def store_kernel(total_rows, plain, *refs):
+    sources, rest = refs[:plain], refs[plain:]
+    squares, factor_left, factor_qkv, factor_out, factor_gate_up, factor_down = rest[:6]
+    fulls, moments, weights = rest[6:10], rest[10:14], rest[14:18]
+    targets, rest = rest[18 : 18 + plain], rest[18 + plain :]
+    results, branch_rms, fresh, sems = rest[:12], rest[12], rest[13:25], rest[25]
     copies = [
         pltpu.make_async_copy(source, target, sems.at[number])
         for number, (source, target) in enumerate(zip(sources, targets))
     ]
     for copy in copies:
         copy.start()
+
+    def settle(number, approx, pick):
+        full, moment, weight = (pick(group[number]) for group in (fulls, moments, weights))
+        places = (number, 4 + number, 8 + number)
+        error_to, moment_to, weight_to = (pick(fresh[place]) for place in places)
+        error_to[...] = full[...] - approx
+        momentum = MOMENTUM * moment[...] + approx
+        moment_to[...] = momentum
+        weight_to[...] = weight[...] - STEP_RATE * momentum
+        for place in places:
+            copy = pltpu.make_async_copy(pick(fresh[place]), pick(results[place]), sems.at[len(copies)])
+            copy.start()
+            copies.append(copy)
+
+    def product(rows, columns):
+        return dot(rows.astype(BF), columns.astype(BF), TN)
+
+    lefts = [triple_first(factor_left[index]) for index in range(5)]
+    for index in range(2):
+        settle(2, product(lefts[2 + index], triple_second(factor_gate_up[index])), lambda ref: ref.at[index])
+    settle(3, product(triple_second(factor_down[...]), lefts[4]), lambda ref: ref)
+    settle(1, product(triple_second(factor_out[...]), lefts[1]), lambda ref: ref)
+    for index in range(3):
+        settle(0, product(triple_second(factor_qkv[index]), lefts[0]), lambda ref: ref.at[index])
     roots = jnp.sqrt(jnp.sum(squares[...], -1, keepdims=True) / total_rows)
     for index in range(2):
         branch_rms[index] = roots[index, 0]
@@ -144,18 +178,23 @@
         copy.wait()
 
 
-def store(arrays, squares, total_rows):
+def store(plain, squares, factors, fulls, moments, weights, total_rows):
     vmem = pl.BlockSpec(memory_space=pltpu.VMEM)
-    count = len(arrays)
+    matrices = [*fulls, *moments, *weights]
+    shapes = [jax.ShapeDtypeStruct(array.shape, F32) for array in (*plain, *factors, *matrices)]
+    count = len(plain) + len(factors)
     return pl.pallas_call(
-        functools.partial(store_kernel, count, total_rows),
-        out_shape=[*(jax.ShapeDtypeStruct(array.shape, F32) for array in arrays), jax.ShapeDtypeStruct((2,), F32)],
-        in_specs=[vmem] * (count + 1),
-        out_specs=[*[pl.BlockSpec(memory_space=pltpu.HBM)] * count, pl.BlockSpec(memory_space=pltpu.SMEM)],
-        scratch_shapes=[pltpu.SemaphoreType.DMA((count,))],
-        compiler_params=pltpu.CompilerParams(vmem_limit_bytes=2**20),
+        functools.partial(store_kernel, total_rows, count),
+        out_shape=[*shapes, jax.ShapeDtypeStruct((2,), F32)],
+        in_specs=[vmem] * (count + 1 + len(factors) + 12),
+        out_specs=[*[pl.BlockSpec(memory_space=pltpu.HBM)] * len(shapes), pl.BlockSpec(memory_space=pltpu.SMEM)],
+        scratch_shapes=[
+            *[pltpu.VMEM(array.shape, F32) for array in matrices],
+            pltpu.SemaphoreType.DMA((count + 21,)),
+        ],
+        compiler_params=pltpu.CompilerParams(vmem_limit_bytes=24 * 2**20),
         name="store",
-    )(*arrays, squares)
+    )(*plain, *factors, squares, *factors, *matrices)
 
 
 def swap_quarters(tile):
@@ -224,17 +263,19 @@
         normed_one, normed_one_all, keys_values, queries, probs, scores, grad_scores,
         attended, attended_low, attended_in, attended_send,
         out_low, gate_up_low, down_low, inner_all, query_low, key_value_low,
-        normed_two, grad_middle_low, grad_middle, normed_three, grad_gate, grad_up,
-        normed_three_send, grad_gate_send, grad_up_send,
+        slim_rows, grad_middle, wide_rows, wide_rows_send, grad_down, queries_t,
         grad_attended, grad_attended_send, grad_attended_all, grad_query, grad_query_low, grad_pairs,
-        pairs_send, pairs_x, pairs_y, relay_x, relay_y, grad_one, grad_one_recv, sum_query, sum_pairs, inner_sums, inner_recv,
-        tokens, out_grad, mask, cosine, sine, extra, kept_rows,
+        *rest,
+    ) = refs
+    pairs_send, pairs_x, pairs_y, relay_x, relay_y = rest[0:5]
+    ( grad_one, grad_one_recv, sum_query, sum_pairs, inner_sums, inner_recv,
+        tokens, out_grad, mask, cosine, sine, extra, kept_rows, late_sum, thin_query, thin_pairs,
         early_t, early_all, early_in, early_d, early_left, late_t, late_s, late_d, norm_t, norm_s, norm_d,
-        right_all, right_in, right_d, right_sum, slim_s, slim_d, thin_s, thin_d,
+        right_all, right_in, right_d, right_sum, slim_s, slim_d, tiny_s, tiny_d,
         local_sems, one_send, one_recv, weight_send, weight_recv, pair_send, pair_recv,
         att_send, att_recv, datt_send, datt_recv, rows_send, rows_recv, back_send, back_recv,
         final_send, final_recv, low_send, low_recv,
-    ) = refs
+    ) = rest[5:]
     nd, ns, nt = sizes
     me_t, me_s = lax.axis_index("tensor"), lax.axis_index("seq")
     other = 1 - me_t
@@ -325,13 +366,7 @@
         )
 
     def row_copies(image):
-        moves = (
-            (normed_two.at[me_t, image], normed_two),
-            (grad_middle_low.at[me_t, image], grad_middle_low),
-            (normed_three_send.at[image], normed_three),
-            (grad_gate_send.at[image], grad_gate),
-            (grad_up_send.at[image], grad_up),
-        )
+        moves = ((slim_rows.at[me_t, image], slim_rows), (wide_rows_send.at[image], wide_rows))
         return [
             to_partner(source, target.at[me_t, image], rows_send.at[image, number], rows_recv.at[image, number])
             for number, (source, target) in enumerate(moves)
@@ -372,17 +407,12 @@
     gain_two, bias_two = norm_pack[2:3], norm_pack[3:4]
 
     cosine[...], sine[...] = angle_tables(me_s * seq_rows, seq_rows)
-    kept = jnp.concatenate([keep[...].astype(F32), jnp.zeros((8 - images, slots), F32)], 0)
-    kept_rows[...] = jnp.transpose(kept)
-    kept = kept_rows[pl.ds(pl.multiple_of(me_s * seq_rows, 8), seq_rows)]
-    for image in range(images):
-        mask[image] = kept[:, image : image + 1]
     loads[0].wait()
     for image in range(images):
         normed, _, _ = norm_parts(tokens[image].astype(F32), gain_one, bias_one)
         normed_one[me_t, image] = normed.astype(BF)
-    pl.semaphore_wait(barrier, (nt - 1) + (ns - 1) + (nd - 1))
-    for image in range(images):
+        if image == 0:
+            pl.semaphore_wait(barrier, (nt - 1) + (ns - 1) + (nd - 1))
         one_copy(image).start()
     loads[1].wait()
 
@@ -426,7 +456,17 @@
     inner_all[me_t, 0:2] = inner_pack[...]
     for copy in weight_copies():
         copy.start()
+    kept = jnp.concatenate([keep[...].astype(F32), jnp.zeros((8 - images, slots), F32)], 0)
+    kept_rows[...] = jnp.transpose(kept)
+    kept = kept_rows[pl.ds(pl.multiple_of(me_s * seq_rows, 8), seq_rows)]
+    for image in range(images):
+        mask[image] = kept[:, image : image + 1]
     loads[5].wait()
+    loads[6].wait()
+    late_sum[...] = sum(fine_dot(basis_qkv[index], full_qkv[index], NN) for index in range(3))
+    gap = jnp.zeros((RANK, 256 - narrow), F32)
+    thin_query[...] = two_rows(jnp.concatenate([basis_qkv[0], gap], -1))
+    thin_pairs[...] = two_rows(jnp.concatenate([basis_qkv[1], basis_qkv[2]], -1))
     extra[...] = jnp.zeros_like(extra)
     inner_sums[...] = jnp.zeros_like(inner_sums)
 
@@ -445,10 +485,23 @@
         def _():
             forward_pairs(0, 0)
             forward_pairs(0, 1)
-            send_pairs(1, 0)
             forward_pairs(0, 2)
-            send_pairs(1, 1)
-            send_pairs(1, 2)
+            for tile in range(3):
+                send_pairs(1, tile)
+            for copy in weight_copies():
+                copy.wait_recv()
+
+            def ahead(place, carry):
+                cotangent = out_grad[place, own_rows] * mask[place, own_rows]
+                for index, half in enumerate((me_t, other)):
+                    grad_down[place, index] = dot(cotangent.astype(BF), down_low[half], NT)
+                for head in range(heads):
+                    turned = jnp.transpose(queries[place * heads + head].astype(F32))
+                    start = head % 2 * DH
+                    queries_t[place * heads + head] = turned[start : start + DH].astype(BF)
+                return carry
+
+            lax.fori_loop(0, images, ahead, 0)
 
         bias = jnp.where(keep[pl.ds(image, 1), :] > 0, 0.0, -1e30)
 
@@ -488,7 +541,6 @@
         @pl.when(image == 0)
         def _():
             forward_pairs(1, 0)
-            forward_pairs(1, 1)
 
         @pl.when(image == 1)
         def _():
@@ -506,7 +558,7 @@
         extra[4:5] += column_sums(branch * branch)
         normed, hat_two, inverse_two = norm_parts(middle, gain_two, bias_two)
         rows_two = normed.astype(BF)
-        normed_two[me_t, image] = rows_two
+        slim_rows[me_t, image, :, 0:width] = rows_two
         halves = (me_t, other)
         gates = [dot(rows_two, gate_up_low[half, 0], NN) for half in halves]
         ups = [dot(rows_two, gate_up_low[half, 1], NN) for half in halves]
@@ -527,13 +579,13 @@
 
         @pl.when(image == 0)
         def _():
+            forward_pairs(1, 1)
             forward_pairs(1, 2)
             for tile in range(3):
                 send_pairs(2, tile)
 
         cotangent = out_grad[image, own_rows] * mask[image, own_rows]
-        grad_branch = cotangent.astype(BF)
-        grads = [dot(grad_branch, down_low[half], NT) for half in halves]
+        grads = [grad_down[image, index] for index in range(2)]
         for half, grad, hat in zip(halves, grads, hats):
             inner_sums[half, 0:1] += column_sums(grad * hat)
             inner_sums[half, 1:2] += column_sums(grad)
@@ -553,12 +605,9 @@
             (grad * gate * sigmoid).astype(BF)
             for grad, gate, sigmoid in zip(grad_hiddens, gates, sigmoids)
         ]
-        normed_three[me_t, image] = lows[0]
-        normed_three_send[image] = lows[1]
-        grad_gate[me_t, image] = gate_rows[0]
-        grad_gate_send[image] = gate_rows[1]
-        grad_up[me_t, image] = up_rows[0]
-        grad_up_send[image] = up_rows[1]
+        for number, pair in enumerate((lows, gate_rows, up_rows)):
+            wide_rows[me_t, image, :, number * wide : number * wide + wide] = pair[0]
+            wide_rows_send[image, :, number * wide : number * wide + wide] = pair[1]
         grad_two = sum(
             dot(gate_row, gate_up_low[half, 0], NT) + dot(up_row, gate_up_low[half, 1], NT)
             for gate_row, up_row, half in zip(gate_rows, up_rows, halves)
@@ -568,7 +617,7 @@
         back = cotangent + norm_back(grad_two, hat_two, inverse_two, gain_two)
         grad_middle[image] = back
         low = back.astype(BF)
-        grad_middle_low[me_t, image] = low
+        slim_rows[me_t, image, :, width:] = low
         grad_attended[me_t, image] = dot(low, out_low[me_t], NT).astype(BF)
         grad_attended_send[image] = dot(low, out_low[other], NT).astype(BF)
         datt_copy(image).start()
@@ -598,16 +647,15 @@
                 chance = probs[image * heads + head, rows].astype(F32)
                 grad_scores[head, rows] = (chance * (scores[head % 2, rows] - deltas[head][rows])).astype(BF)
 
-        def pair_rows(place, wide, half, right):
-            rows = jnp.transpose(wide)[half * DH : half * DH + DH].astype(BF)
-            grad_pairs[place * DH : place * DH + DH] = dot(rows, right, NN)
-
         def value_grad(head):
-            pair_rows(heads + head, wides[head], (head + 1) % 2, probs[image * heads + head])
+            start = (head + 1) % 2 * DH
+            rows = jnp.transpose(wides[head])[start : start + DH].astype(BF)
+            place = (heads + head) * DH
+            grad_pairs[place : place + DH] = dot(rows, probs[image * heads + head], NN)
 
         def key_grad(head):
-            wide = queries[image * heads + head].astype(F32)
-            pair_rows(head, wide, head % 2, grad_scores[head])
+            place = head * DH
+            grad_pairs[place : place + DH] = dot(queries_t[image * heads + head], grad_scores[head], NN)
 
         def query_grad(head):
             return dot(grad_scores[head], key_tile(image, head // 2), NN)
@@ -629,8 +677,8 @@
         key_grad(2)
         grad_query[:, 0:128] = halves_of(query_grads[0], query_grads[1])
         grad_query[:, 128:256] = half_of(query_grads[2], 0)
-        pairs = jnp.transpose(grad_pairs[...])
-        pairs_send[image] = pairs.astype(BF).reshape(ns, seq_rows, width)
+
+        pairs_send[image] = jnp.transpose(grad_pairs[...]).astype(BF).reshape(ns, seq_rows, width)
 
         @pl.when(image == 0)
         def _():
@@ -649,12 +697,15 @@
         for half in range(2):
             place = slice(half * own, half * own + own)
             grad_branch = (out_grad[image, place] * mask[image, place]).astype(BF)
-            full_down[...] += dot(normed_three[half, image], grad_branch, TN) * scale
-            rows_two = normed_two[half, image]
-            full_gate_up[0] += dot(rows_two, grad_gate[half, image], TN) * scale
-            full_gate_up[1] += dot(rows_two, grad_up[half, image], TN) * scale
+            normed_three, grad_gate, grad_up = (
+                wide_rows[half, image, :, number * wide : number * wide + wide] for number in range(3)
+            )
+            full_down[...] += dot(normed_three, grad_branch, TN) * scale
+            rows_two, low = slim_rows[half, image, :, 0:width], slim_rows[half, image, :, width:]
+            full_gate_up[0] += dot(rows_two, grad_gate, TN) * scale
+            full_gate_up[1] += dot(rows_two, grad_up, TN) * scale
             mixed = attended_low[image].astype(F32)[place].astype(BF)
-            full_out[...] += dot(mixed, grad_middle_low[half, image], TN)[256 - narrow :] * scale
+            full_out[...] += dot(mixed, low, TN)[256 - narrow :] * scale
 
     def stage(step, carry):
         @pl.when(step < images)
@@ -672,11 +723,6 @@
         def _():
             attend_back(step - 1)
 
-        @pl.when(step == 0)
-        def _():
-            for copy in weight_copies():
-                copy.wait_recv()
-
         @pl.when(step < images)
         def _():
             feed(step)
@@ -688,11 +734,18 @@
 
     weights(images - 1)
 
-    def low_exchange(axis, size, buffers, number):
-        return exchange(axis, size, buffers, low_send.at[number], low_recv.at[number])
-
-    def low_scatter(pieces, inbox, number):
-        return scatter("seq", ns, pieces, inbox, low_send.at[number], low_recv.at[number])
+    taken = []
+
+    def take(count):
+        taken.append(count)
+        return sum(taken) - count
+
+    def low_exchange(axis, size, buffers):
+        base = take((size - 1) * len(buffers))
+        return exchange(axis, size, buffers, low_send, low_recv, base)
+
+    def low_scatter(pieces, inbox):
+        return scatter("seq", ns, pieces, inbox, low_send, low_recv, take(ns - 1))
 
     share = 1.0 / (ns * nd)
     early = early_t.at[me_t]
@@ -700,41 +753,59 @@
     for index in range(2):
         early[1 + index] = fine_dot(basis_gate_up[index], full_gate_up[index], NT)
     early[3] = fine_dot(basis_down[...], full_down[...], NN)
-    early_moves = low_exchange("tensor", nt, (early_t,), 0)
+    early[4] = extra[...]
+    early_moves = low_exchange("tensor", nt, (early_t,))
 
     sum_query[...] = jnp.zeros_like(sum_query)
     sum_pairs[...] = jnp.zeros_like(sum_pairs)
 
-    def finish_pairs(image):
+    def pairs_of(image):
         for kind in range(2, 6):
             back_copy(image, kind).wait_recv()
         pairs = pairs_send[image, me_s].astype(F32)
         pairs = pairs + pairs_x[image].astype(F32) + pairs_y[image].astype(F32)
         pairs = turn_pairs(pairs, cosine[...], -sine[...]).astype(BF)
+        rows = dot(thin_query[...], grad_query_low[image], NT) + dot(thin_pairs[...], pairs, NT)
+        late_sum[...] += fold(dot(two_rows(fold(rows)), normed_one_all[image], NN)) * scale
+        return pairs
+
+    def finish_pairs(image, pairs):
         query = grad_query_low[image]
         grad_one[image] = dot(query, query_low[...], NN) + dot(pairs, key_value_low[...], NN)
         final_copy(image).start()
         sum_query[...] += dot(query, normed_one_all[image], TN)
         sum_pairs[...] += dot(pairs, normed_one_all[image], TN)
 
-    finish_pairs(0)
+    finish_pairs(0, pairs_of(0))
     arrive(early_moves)
-    early_all[...] = total(early_t, nt)
-    early_moves = low_scatter(early_all, early_in, 1)
+    summed = total(early_t, nt)
+    early_all[...] = summed[0:4]
+    early_moves = low_scatter(early_all, early_in)
+    inner_copy().wait_recv()
+    tiny_s[me_s] = jnp.zeros_like(tiny_s[me_s])
+    tiny_s[me_s, 0:2] = ((inner_sums[me_t] + inner_recv[...]) * scale)[0:2]
+    tiny_s[me_s, 2:6, 0:width] = summed[4, 2:6]
+    tiny_moves = low_exchange("seq", ns, (tiny_s,))
     relay_back(images - 1)
-    finish_pairs(1)
+    finish_pairs(1, pairs_of(1))
     arrive(early_moves)
     early_d[me_d] = total(early_in, ns)
-    early_moves = low_exchange("dp", nd, (early_d,), 2)
-    finish_pairs(2)
-    loads[6].wait()
+    early_moves = low_exchange("dp", nd, (early_d,))
+    arrive(tiny_moves)
+    tiny_d[me_d] = total(tiny_s, ns)
+    tiny_moves = low_exchange("dp", nd, (tiny_d,))
+    pairs = pairs_of(images - 1)
+    late_t[me_t] = late_sum[...]
+    late_moves = low_exchange("tensor", nt, (late_t,))
+    finish_pairs(images - 1, pairs)
+    arrive(late_moves)
+    late_s[me_s] = total(late_t, nt)
+    late_moves = low_exchange("seq", ns, (late_s,))
     full_qkv[0] += sum_query[0:narrow] * scale
     full_qkv[1] += sum_pairs[0:narrow] * scale
     full_qkv[2] += sum_pairs[narrow : 2 * narrow] * scale
-    late_t[me_t] = sum(fine_dot(basis_qkv[index], full_qkv[index], NN) for index in range(3))
-    late_moves = low_exchange("tensor", nt, (late_t,), 3)
-
-    norm_t[me_t] = extra[...]
+
+    norm_t[me_t] = jnp.zeros_like(norm_t[me_t])
 
     def finish(image, carry):
         final_copy(image).wait_recv()
@@ -745,88 +816,67 @@
         norm_t[me_t, 1:2] += column_sums(grad)
         return carry
 
-    def settle(left, right, full, moment, weight):
-        approx = dot(triple_second(right).astype(BF), triple_first(left).astype(BF), TN)
-        full[...] = full[...] - approx
-        fresh = MOMENTUM * moment[...] + approx
-        moment[...] = fresh
-        weight[...] = weight[...] - STEP_RATE * fresh
-
     def orthonormal(rows):
         return gram_schmidt(rows.reshape(1, RANK, width))[0]
 
-    arrive(late_moves)
-    late_s[me_s] = total(late_t, nt)
-    late_moves = low_exchange("seq", ns, (late_s,), 4)
     arrive(early_moves)
     early_left[me_s] = orthonormal(total(early_d, nd))
-    early_moves = low_exchange("seq", ns, (early_left,), 5)
-    lax.fori_loop(0, images, finish, 0)
-    norm_moves = low_exchange("tensor", nt, (norm_t,), 6)
+    early_moves = low_exchange("seq", ns, (early_left,))
     arrive(late_moves)
     late_d[me_d] = total(late_s, ns)
-    late_moves = low_exchange("dp", nd, (late_d,), 7)
+    late_moves = low_exchange("dp", nd, (late_d,))
+    lax.fori_loop(0, images, finish, 0)
+    norm_moves = low_exchange("tensor", nt, (norm_t,))
     arrive(early_moves)
     right_all[0, :, 0:narrow] = fine_dot(early_left[0], full_out[...], NT)
     right_all[0, :, narrow:] = jnp.zeros((RANK, wide - narrow), F32)
     for index in range(2):
         right_all[1 + index] = fine_dot(early_left[1 + index], full_gate_up[index], NN)
     right_all[3] = fine_dot(early_left[3], full_down[...], NT)
-    early_moves = low_scatter(right_all, right_in, 8)
+    early_moves = low_scatter(right_all, right_in)
     for index in range(4):
         factor_left[1 + index] = early_left[index]
-    inner_copy().wait_recv()
-    thin_s[me_s] = (inner_sums[me_t] + inner_recv[...]) * scale
     arrive(norm_moves)
-    norm_s[me_s] = total(norm_t, nt)
-    arrive(early_moves)
-    right_d[me_d] = total(right_in, ns)
-    early_moves = low_exchange("dp", nd, (right_d,), 9)
+    norm_s[me_s] = total(norm_t, nt)[0:2]
     arrive(late_moves)
     left = orthonormal(total(late_d, nd))
     for index in range(3):
         slim_s[me_s, 8 * index : 8 * index + 8] = fine_dot(left, full_qkv[index], NT)
-    late_moves = low_exchange("seq", ns, (slim_s, norm_s, thin_s), 10)
+    late_moves = low_exchange("seq", ns, (slim_s, norm_s))
     factor_left[0] = left
+    arrive(early_moves)
+    right_d[me_d] = total(right_in, ns)
+    early_moves = low_exchange("dp", nd, (right_d,))
     for load in loads[10:14]:
         load.wait()
+    arrive(tiny_moves)
+    tiny = total(tiny_d, nd)
+    squares[...] = tiny[4:6, 0:width]
     arrive(late_moves)
     slim_d[me_d] = total(slim_s, ns)
     norm_d[me_d] = total(norm_s, ns)
-    thin_d[me_d] = total(thin_s, ns)
-    late_moves = low_exchange("dp", nd, (slim_d, norm_d, thin_d), 11)
+    late_moves = low_exchange("dp", nd, (slim_d, norm_d))
+    fresh = MOMENTUM * moment_norm[2:4] + tiny[2:4, 0:width] * (share * scale)
+    new_moment_norm[2:4] = fresh
+    new_norm_pack[2:4] = norm_pack[2:4] - STEP_RATE * fresh
+    fresh = MOMENTUM * moment_inner[...] + tiny[0:2] * share
+    new_moment_inner[...] = fresh
+    new_inner_pack[...] = inner_pack[...] - STEP_RATE * fresh
     arrive(early_moves)
     right_sum[me_s] = total(right_d, nd) * share
-    early_moves = low_exchange("seq", ns, (right_sum,), 12)
+    early_moves = low_exchange("seq", ns, (right_sum,))
     arrive(early_moves)
-    right = right_sum[0, :, 0:narrow]
-    factor_out[...] = right
-    settle(early_left[0], right, full_out, moment_out, w_out)
+    factor_out[...] = right_sum[0, :, 0:narrow]
     for index in range(2):
-        right = right_sum[1 + index]
-        factor_gate_up[index] = right
-        left_triple, right_triple = triple_first(early_left[1 + index]), triple_second(right)
-        approx = dot(left_triple.astype(BF), right_triple.astype(BF), TN)
-        full_gate_up[index] = full_gate_up[index] - approx
-        fresh = MOMENTUM * moment_gate_up[index] + approx
-        moment_gate_up[index] = fresh
-        w_gate_up[index] = w_gate_up[index] - STEP_RATE * fresh
+        factor_gate_up[index] = right_sum[1 + index]
     factor_down[...] = right_sum[3]
-    settle(early_left[3], right_sum[3], full_down, moment_down, w_down)
     arrive(late_moves)
     slim = total(slim_d, nd) * share
     for index in range(3):
-        right = slim[8 * index : 8 * index + 8]
-        factor_qkv[index] = right
-        settle(left, right, full_qkv.at[index], moment_qkv.at[index], w_qkv.at[index])
-    norms = total(norm_d, nd)
-    squares[...] = norms[4:6]
-    fresh = MOMENTUM * moment_norm[...] + norms[0:4] * (share * scale)
-    new_moment_norm[...] = fresh
-    new_norm_pack[...] = norm_pack[...] - STEP_RATE * fresh
-    fresh = MOMENTUM * moment_inner[...] + total(thin_d, nd)[0:2] * share
-    new_moment_inner[...] = fresh
-    new_inner_pack[...] = inner_pack[...] - STEP_RATE * fresh
+        factor_qkv[index] = slim[8 * index : 8 * index + 8]
+    fresh = MOMENTUM * moment_norm[0:2] + total(norm_d, nd) * (share * scale)
+    new_moment_norm[0:2] = fresh
+    new_norm_pack[0:2] = norm_pack[0:2] - STEP_RATE * fresh
 
     for image in range(images):
         for copy in (
@@ -877,21 +927,22 @@
         pltpu.VMEM((2, 8, wide), F32),
         pltpu.VMEM((256, width), BF),
         pltpu.VMEM((2 * narrow, width), BF),
-        pltpu.VMEM((2, images, own, width), BF),
-        pltpu.VMEM((2, images, own, width), BF),
+        pltpu.VMEM((2, images, own, 2 * width), BF),
         pltpu.VMEM((images, own, width), F32),
-        *[pltpu.VMEM((2, images, own, wide), BF)] * 3,
-        *[pltpu.VMEM((images, own, wide), BF)] * 3,
+        pltpu.VMEM((2, images, own, 3 * wide), BF),
+        pltpu.VMEM((images, own, 3 * wide), BF),
+        pltpu.VMEM((images, 2, own, wide), F32),
+        pltpu.VMEM((images * heads, DH, seq_rows), BF),
         pltpu.VMEM((2, images, own, 256), BF),
         pltpu.VMEM((images, own, 256), BF),
         pltpu.VMEM((seq_rows, 256), F32),
         pltpu.VMEM((seq_rows, 256), F32),
         pltpu.VMEM((images, seq_rows, 256), BF),
         pltpu.VMEM((width, slots), F32),
-        pltpu.VMEM((images, ns, seq_rows, width), BF),
-        *[pltpu.VMEM((images, seq_rows, width), BF)] * 2,
-        pltpu.VMEM((images, top, width), BF),
-        pltpu.VMEM((images, seq_rows - top, width), BF),
+        *[
+            pltpu.VMEM((images, *rows, width), BF)
+            for rows in ((ns, seq_rows), (seq_rows,), (seq_rows,), (top,), (seq_rows - top,))
+        ],
         pltpu.VMEM((images, seq_rows, width), F32),
         pltpu.VMEM((images, own, width), F32),
         pltpu.VMEM((256, width), F32),
@@ -905,11 +956,15 @@
         pltpu.VMEM((seq_rows, 128), F32),
         pltpu.VMEM((8, width), F32),
         pltpu.VMEM((slots, 8), F32),
-        pltpu.VMEM((nt, 4, RANK, width), F32),
+        pltpu.VMEM((RANK, width), F32),
+        pltpu.VMEM((2 * RANK, 256), BF),
+        pltpu.VMEM((2 * RANK, 2 * narrow), BF),
+        pltpu.VMEM((nt, 5, RANK, width), F32),
         pltpu.VMEM((4, RANK, width), F32),
         *[pltpu.VMEM((size, RANK, width), F32) for size in (ns, nd, ns)],
         *[pltpu.VMEM((size, RANK, width), F32) for size in (nt, ns, nd)],
-        *[pltpu.VMEM((size, RANK, width), F32) for size in (nt, ns, nd)],
+        pltpu.VMEM((nt, RANK, width), F32),
+        *[pltpu.VMEM((size, 2, width), F32) for size in (ns, nd)],
         *[pltpu.VMEM((size, RANK, wide), F32) for size in (4, ns, nd, ns)],
         *[pltpu.VMEM((size, 3 * RANK, narrow), F32) for size in (ns, nd)],
         *[pltpu.VMEM((size, RANK, wide), F32) for size in (ns, nd)],
@@ -918,10 +973,10 @@
         *[dma((4,))] * 2,
         *[dma((images, 3, 4))] * 2,
         *[dma((images,))] * 4,
-        *[dma((images, 5))] * 2,
+        *[dma((images, 2))] * 2,
         *[dma((images, 6))] * 2,
         *[dma((images + 1,))] * 2,
-        *[dma((13, 3, max(mesh_sizes)))] * 2,
+        *[dma((3 * (nt - 1) + 8 * (ns - 1) + 6 * (nd - 1),))] * 2,
     ]
     return pl.pallas_call(
         functools.partial(block_kernel, mesh_sizes, images),
@@ -968,7 +1023,7 @@
     def turn(array):
         return jnp.swapaxes(array, -1, -2)
 
-    *arrays, squares = block(
+    results = block(
         sizes,
         (
             jnp.transpose(keep_mask), norm_pack, inner_pack, moment_norm, moment_inner,
@@ -980,13 +1035,18 @@
             turn(moment_qkv), moment_out, moment_gate_up, moment_down,
         ),
     )
+    grads, lows, fulls, moments = results[0:2], results[2:7], results[7:11], results[11:15]
     (
-        residual, input_grad, factor_left, factor_qkv, factor_out, factor_gate_up, factor_down,
+        residual, input_grad, new_moment_norm, new_moment_inner, new_norm_pack, new_inner_pack,
+        factor_left, factor_qkv, factor_out, factor_gate_up, factor_down,
         new_error_qkv, new_error_out, new_error_gate_up, new_error_down,
-        new_moment_qkv, new_moment_out, new_moment_gate_up, new_moment_down, new_moment_norm, new_moment_inner,
-        new_w_qkv, new_w_out, new_w_gate_up, new_w_down, new_norm_pack, new_inner_pack,
+        new_moment_qkv, new_moment_out, new_moment_gate_up, new_moment_down,
+        new_w_qkv, new_w_out, new_w_gate_up, new_w_down,
         branch_rms,
-    ) = store(arrays, squares, float(slot_count * images * lax.axis_size("dp") * width))
+    ) = store(
+        (*grads, *results[15:17], *results[21:23]), results[23], lows, fulls, moments, results[17:21],
+        float(slot_count * images * lax.axis_size("dp") * width),
+    )
     return (
         jnp.swapaxes(residual, 0, 1), jnp.swapaxes(input_grad, 0, 1),
         *(turn(factor) for factor in (factor_left, factor_qkv, factor_out, factor_gate_up, factor_down)),

time: 85.8 us -> 80.1 us (0.934)
  Pallas kernels: 84.8 us -> 79 us
    pallas_call x1, Pallas kernels: 79.5 us -> 73.8 us  [block(): pl.pallas_call(functools.partial(block_kernel, mesh_sizes, images), out_s...]
where the time goes in v3:
time: 80.1 us; the launch traced here: 79.9 us
  Pallas kernels  79 us (99%)
  between operations  0.84 us (1%)
    pallas_call x1, Pallas kernels, block(): pl.pallas_call(functools.partial(block_kernel, mesh_sizes, images), out_s...  73.8 us
    pallas_call x1, Pallas kernels, store(): pl.pallas_call(functools.partial(store_kernel, total_rows, count), out_sh...  5.26 us

profile of v3, /device:TPU:0, one launch (start us, length us, event | category | flops | bytes accessed | tf_op | source)
XLA Modules:
  0.0 79.9 jit_solution(858332742366406902)
XLA Ops:
  0.7 73.8 %block.1 = (f32[3,136,384]{2,1,0:T(8,128)S(1)}, f32[3,136,384]{2,1,0:T(8,128)S(1)}, f32[5,8,384]{2,1,0:T(8,128)S(1)}, f32[3,8,192]{2,1,0:T(8,128)S(1)}, f32[8,19...) custom-call(s32[3,1088]{1,0:T(4,128)} %bitcast.40, ...), custom_call_target="tpu_custom_call" | custom-call | tf_op jit(solution)/shard_map/block/pallas_call | solution.py:981
  74.4 5.3 %store.1 = (f32[3,136,384]{2,1,0:T(8,128)}, f32[3,136,384]{2,1,0:T(8,128)}, f32[4,384]{1,0:T(4,128)}, f32[2,512]{1,0:T(2,128)}, f32[4,384]{1,0:T(4,128)}, /*inde...) custom-call(f32[3,136,384]{2,1,0:T(8,128)S(1)} %get-tuple-element.72, ...), custom_call_target="tpu_custom_call" | custom-call | tf_op jit(solution)/shard_map/store/pallas_call | solution.py:186

commit v4 on v3

--- a/solution.py
+++ b/solution.py
@@ -65,54 +65,47 @@
     return stack
 
 
-def exchange(axis, size, buffers, sends, receives, base):
-    me = lax.axis_index(axis)
-    copies = []
-    for step in range(1, size):
-        peer = lax.rem(me + step, size)
-        for buffer in buffers:
-            place = base + len(copies)
-            copy = pltpu.make_async_remote_copy(
-                src_ref=buffer.at[me],
-                dst_ref=buffer.at[me],
-                send_sem=sends.at[place],
-                recv_sem=receives.at[place],
-                device_id={axis: peer},
-                device_id_type=MESH,
-            )
-            copy.start()
-            copies.append(copy)
-    return copies
-
-
-def scatter(axis, size, pieces, inbox, sends, receives, base):
-    me = lax.axis_index(axis)
-    inbox[me] = pieces[me]
-    copies = []
-    for step in range(1, size):
-        peer = lax.rem(me + step, size)
-        copy = pltpu.make_async_remote_copy(
-            src_ref=pieces.at[peer],
-            dst_ref=inbox.at[me],
-            send_sem=sends.at[base + step - 1],
-            recv_sem=receives.at[base + step - 1],
-            device_id={axis: peer},
+class Moves:
+    def __init__(self, span, send, receive, device):
+        self.whole = pltpu.make_async_remote_copy(
+            src_ref=span, dst_ref=span, send_sem=send, recv_sem=receive, device_id=device, device_id_type=MESH
+        )
+
+    def arrive(self):
+        self.whole.wait()
+
+
+def exchange(axes, sizes, buffer, send, receive, pieces=None):
+    count = math.prod(sizes)
+    place = 0
+    for axis, size in zip(axes, sizes):
+        place = place * size + lax.axis_index(axis)
+    for step in range(1, count):
+        peer = lax.rem(place + step, count)
+        device, rest = {}, peer
+        for axis, size in reversed(tuple(zip(axes, sizes))):
+            device[axis] = lax.rem(rest, size)
+            rest = lax.div(rest, size)
+        pltpu.make_async_remote_copy(
+            src_ref=buffer.at[place] if pieces is None else pieces.at[peer],
+            dst_ref=buffer.at[place],
+            send_sem=send,
+            recv_sem=receive,
+            device_id=device,
             device_id_type=MESH,
-        )
-        copy.start()
-        copies.append(copy)
-    return copies
-
-
-def arrive(copies):
-    for copy in copies:
-        copy.wait()
+        ).start()
+    return Moves(buffer.at[0 : count - 1], send, receive, device)
+
+
+def arrive(moves):
+    for move in moves:
+        move.arrive()
 
 
 def total(buffer, size):
-    value = buffer[0]
+    value = buffer[0].astype(F32)
     for index in range(1, size):
-        value = value + buffer[index]
+        value = value + buffer[index].astype(F32)
     return value
 
 
@@ -270,7 +263,7 @@
     pairs_send, pairs_x, pairs_y, relay_x, relay_y = rest[0:5]
     ( grad_one, grad_one_recv, sum_query, sum_pairs, inner_sums, inner_recv,
         tokens, out_grad, mask, cosine, sine, extra, kept_rows, late_sum, thin_query, thin_pairs,
-        early_t, early_all, early_in, early_d, early_left, late_t, late_s, late_d, norm_t, norm_s, norm_d,
+        early_t, early_all, early_in, early_d, early_left, late_s, late_d, norm_t, norm_s, norm_d,
         right_all, right_in, right_d, right_sum, slim_s, slim_d, tiny_s, tiny_d,
         local_sems, one_send, one_recv, weight_send, weight_recv, pair_send, pair_recv,
         att_send, att_recv, datt_send, datt_recv, rows_send, rows_recv, back_send, back_recv,
@@ -310,7 +303,7 @@
             )
         )
     ]
-    for load in loads:
+    for load in loads[0:2]:
         load.start()
 
     def to_partner(source, target, send, receive):
@@ -340,7 +333,7 @@
         block = keys_values.at[image, tile, place]
         if kind >= 2:
             block = block.at[(upper, lower)[kind - 2]]
-        return to_seq(block, block, pair_send.at[image, tile, kind], pair_recv.at[image, tile, kind], peer)
+        return to_seq(block, block, pair_send.at[image], pair_recv.at[image, tile, min(kind, 2)], peer)
 
     def send_pairs(image, tile):
         for kind in range(2):
@@ -352,8 +345,8 @@
             pair_copy(image, tile, 2 + kind).start()
 
     def await_pairs(image, tile):
-        for kind in range(2, 4):
-            pair_copy(image, tile, kind).wait_recv()
+        block = keys_values.at[image, tile, far]
+        to_seq(block, block, pair_send.at[image], pair_recv.at[image, tile, 2], far).wait_recv()
 
     def att_copy(image):
         return to_partner(
@@ -383,7 +376,7 @@
         )[kind]
         return to_seq(
             pairs_send.at[image, place, rows], target.at[image, there],
-            back_send.at[image, kind], back_recv.at[image, kind], peer,
+            back_send.at[image], back_recv.at[image, min(kind, 2)], peer,
         )
 
     def relay_back(image):
@@ -414,6 +407,8 @@
         if image == 0:
             pl.semaphore_wait(barrier, (nt - 1) + (ns - 1) + (nd - 1))
         one_copy(image).start()
+    for load in loads[2:]:
+        load.start()
     loads[1].wait()
 
     narrow = heads * DH
@@ -735,17 +730,23 @@
     weights(images - 1)
 
     taken = []
-
-    def take(count):
-        taken.append(count)
-        return sum(taken) - count
-
-    def low_exchange(axis, size, buffers):
-        base = take((size - 1) * len(buffers))
-        return exchange(axis, size, buffers, low_send, low_recv, base)
+    sizes_of = {"dp": nd, "seq": ns, "tensor": nt}
+
+    def low_exchange(axes, *buffers):
+        moves = []
+        for buffer in buffers:
+            place = len(taken)
+            taken.append(place)
+            moves.append(
+                exchange(axes, [sizes_of[axis] for axis in axes], buffer, low_send.at[place], low_recv.at[place])
+            )
+        return moves
 
     def low_scatter(pieces, inbox):
-        return scatter("seq", ns, pieces, inbox, low_send, low_recv, take(ns - 1))
+        place = len(taken)
+        taken.append(place)
+        inbox[me_s] = pieces[me_s]
+        return [exchange(("seq",), (ns,), inbox, low_send.at[place], low_recv.at[place], pieces)]
 
     share = 1.0 / (ns * nd)
     early = early_t.at[me_t]
@@ -754,14 +755,14 @@
         early[1 + index] = fine_dot(basis_gate_up[index], full_gate_up[index], NT)
     early[3] = fine_dot(basis_down[...], full_down[...], NN)
     early[4] = extra[...]
-    early_moves = low_exchange("tensor", nt, (early_t,))
+    early_moves = low_exchange(("tensor",), early_t)
 
     sum_query[...] = jnp.zeros_like(sum_query)
     sum_pairs[...] = jnp.zeros_like(sum_pairs)
 
     def pairs_of(image):
-        for kind in range(2, 6):
-            back_copy(image, kind).wait_recv()
+        both = pairs_send.at[image, 0:2]
+        to_seq(both, both, back_send.at[image], back_recv.at[image, 2], far).wait_recv()
         pairs = pairs_send[image, me_s].astype(F32)
         pairs = pairs + pairs_x[image].astype(F32) + pairs_y[image].astype(F32)
         pairs = turn_pairs(pairs, cosine[...], -sine[...]).astype(BF)
@@ -785,22 +786,19 @@
     tiny_s[me_s] = jnp.zeros_like(tiny_s[me_s])
     tiny_s[me_s, 0:2] = ((inner_sums[me_t] + inner_recv[...]) * scale)[0:2]
     tiny_s[me_s, 2:6, 0:width] = summed[4, 2:6]
-    tiny_moves = low_exchange("seq", ns, (tiny_s,))
+    tiny_moves = low_exchange(("seq",), tiny_s)
     relay_back(images - 1)
     finish_pairs(1, pairs_of(1))
     arrive(early_moves)
     early_d[me_d] = total(early_in, ns)
-    early_moves = low_exchange("dp", nd, (early_d,))
+    early_moves = low_exchange(("dp",), early_d)
     arrive(tiny_moves)
     tiny_d[me_d] = total(tiny_s, ns)
-    tiny_moves = low_exchange("dp", nd, (tiny_d,))
+    tiny_moves = low_exchange(("dp",), tiny_d)
     pairs = pairs_of(images - 1)
-    late_t[me_t] = late_sum[...]
-    late_moves = low_exchange("tensor", nt, (late_t,))
+    late_s[me_s * nt + me_t] = late_sum[...]
+    late_moves = low_exchange(("seq", "tensor"), late_s)
     finish_pairs(images - 1, pairs)
-    arrive(late_moves)
-    late_s[me_s] = total(late_t, nt)
-    late_moves = low_exchange("seq", ns, (late_s,))
     full_qkv[0] += sum_query[0:narrow] * scale
     full_qkv[1] += sum_pairs[0:narrow] * scale
     full_qkv[2] += sum_pairs[narrow : 2 * narrow] * scale
@@ -821,18 +819,18 @@
 
     arrive(early_moves)
     early_left[me_s] = orthonormal(total(early_d, nd))
-    early_moves = low_exchange("seq", ns, (early_left,))
+    early_moves = low_exchange(("seq",), early_left)
     arrive(late_moves)
-    late_d[me_d] = total(late_s, ns)
-    late_moves = low_exchange("dp", nd, (late_d,))
+    late_d[me_d] = total(late_s, ns * nt)
+    late_moves = low_exchange(("dp",), late_d)
     lax.fori_loop(0, images, finish, 0)
-    norm_moves = low_exchange("tensor", nt, (norm_t,))
+    norm_moves = low_exchange(("tensor",), norm_t)
     arrive(early_moves)
-    right_all[0, :, 0:narrow] = fine_dot(early_left[0], full_out[...], NT)
-    right_all[0, :, narrow:] = jnp.zeros((RANK, wide - narrow), F32)
+    right = fine_dot(early_left[0], full_out[...], NT)
+    right_all[0] = jnp.concatenate([right, jnp.zeros((RANK, wide - narrow), F32)], -1).astype(BF)
     for index in range(2):
-        right_all[1 + index] = fine_dot(early_left[1 + index], full_gate_up[index], NN)
-    right_all[3] = fine_dot(early_left[3], full_down[...], NT)
+        right_all[1 + index] = fine_dot(early_left[1 + index], full_gate_up[index], NN).astype(BF)
+    right_all[3] = fine_dot(early_left[3], full_down[...], NT).astype(BF)
     early_moves = low_scatter(right_all, right_in)
     for index in range(4):
         factor_left[1 + index] = early_left[index]
@@ -840,22 +838,24 @@
     norm_s[me_s] = total(norm_t, nt)[0:2]
     arrive(late_moves)
     left = orthonormal(total(late_d, nd))
+    rights = []
     for index in range(3):
-        slim_s[me_s, 8 * index : 8 * index + 8] = fine_dot(left, full_qkv[index], NT)
-    late_moves = low_exchange("seq", ns, (slim_s, norm_s))
+        rights.append(fine_dot(left, full_qkv[index], NT))
+    slim_s[me_s] = jnp.concatenate(rights, 0).astype(BF)
+    late_moves = low_exchange(("seq",), slim_s, norm_s)
     factor_left[0] = left
     arrive(early_moves)
-    right_d[me_d] = total(right_in, ns)
-    early_moves = low_exchange("dp", nd, (right_d,))
+    right_d[me_d] = total(right_in, ns).astype(BF)
+    early_moves = low_exchange(("dp",), right_d)
     for load in loads[10:14]:
         load.wait()
     arrive(tiny_moves)
     tiny = total(tiny_d, nd)
     squares[...] = tiny[4:6, 0:width]
     arrive(late_moves)
-    slim_d[me_d] = total(slim_s, ns)
+    slim_d[me_d] = total(slim_s, ns).astype(BF)
     norm_d[me_d] = total(norm_s, ns)
-    late_moves = low_exchange("dp", nd, (slim_d, norm_d))
+    late_moves = low_exchange(("dp",), slim_d, norm_d)
     fresh = MOMENTUM * moment_norm[2:4] + tiny[2:4, 0:width] * (share * scale)
     new_moment_norm[2:4] = fresh
     new_norm_pack[2:4] = norm_pack[2:4] - STEP_RATE * fresh
@@ -863,13 +863,13 @@
     new_moment_inner[...] = fresh
     new_inner_pack[...] = inner_pack[...] - STEP_RATE * fresh
     arrive(early_moves)
-    right_sum[me_s] = total(right_d, nd) * share
-    early_moves = low_exchange("seq", ns, (right_sum,))
+    right_sum[me_s] = (total(right_d, nd) * share).astype(BF)
+    early_moves = low_exchange(("seq",), right_sum)
     arrive(early_moves)
-    factor_out[...] = right_sum[0, :, 0:narrow]
+    factor_out[...] = right_sum[0].astype(F32)[:, 0:narrow]
     for index in range(2):
-        factor_gate_up[index] = right_sum[1 + index]
-    factor_down[...] = right_sum[3]
+        factor_gate_up[index] = right_sum[1 + index].astype(F32)
+    factor_down[...] = right_sum[3].astype(F32)
     arrive(late_moves)
     slim = total(slim_d, nd) * share
     for index in range(3):
@@ -881,8 +881,13 @@
     for image in range(images):
         for copy in (
             one_copy(image), att_copy(image), datt_copy(image), *row_copies(image), final_copy(image),
-            *(pair_copy(image, tile, kind) for tile in range(3) for kind in range(4)),
-            *(back_copy(image, kind) for kind in range(6)),
+            *(
+                to_seq(span, span, send, receive, far)
+                for span, send, receive in (
+                    (keys_values.at[image, :, 0:3], pair_send.at[image], pair_recv.at[image, 0, 2]),
+                    (pairs_send.at[image, 0:3], back_send.at[image], back_recv.at[image, 2]),
+                )
+            ),
         ):
             copy.wait_send()
     for copy in (*weight_copies(), inner_copy()):
@@ -962,21 +967,23 @@
         pltpu.VMEM((nt, 5, RANK, width), F32),
         pltpu.VMEM((4, RANK, width), F32),
         *[pltpu.VMEM((size, RANK, width), F32) for size in (ns, nd, ns)],
-        *[pltpu.VMEM((size, RANK, width), F32) for size in (nt, ns, nd)],
+        *[pltpu.VMEM((size, RANK, width), F32) for size in (ns * nt, nd)],
         pltpu.VMEM((nt, RANK, width), F32),
         *[pltpu.VMEM((size, 2, width), F32) for size in (ns, nd)],
-        *[pltpu.VMEM((size, RANK, wide), F32) for size in (4, ns, nd, ns)],
-        *[pltpu.VMEM((size, 3 * RANK, narrow), F32) for size in (ns, nd)],
+        *[pltpu.VMEM((size, RANK, wide), BF) for size in (4, ns, nd, ns)],
+        *[pltpu.VMEM((size, 3 * RANK, narrow), BF) for size in (ns, nd)],
         *[pltpu.VMEM((size, RANK, wide), F32) for size in (ns, nd)],
         dma((14,)),
         *[dma((images,))] * 2,
         *[dma((4,))] * 2,
-        *[dma((images, 3, 4))] * 2,
+        dma((images,)),
+        dma((images, 3, 3)),
         *[dma((images,))] * 4,
         *[dma((images, 2))] * 2,
-        *[dma((images, 6))] * 2,
+        dma((images,)),
+        dma((images, 3)),
         *[dma((images + 1,))] * 2,
-        *[dma((3 * (nt - 1) + 8 * (ns - 1) + 6 * (nd - 1),))] * 2,
+        *[dma((16,))] * 2,
     ]
     return pl.pallas_call(
         functools.partial(block_kernel, mesh_sizes, images),

time: 80.1 us -> 78.7 us (0.983)
  Pallas kernels: 79 us -> 77.6 us
    pallas_call x1, Pallas kernels: 73.8 us -> 72.3 us  [block(): pl.pallas_call(functools.partial(block_kernel, mesh_sizes, images), out_s...]
where the time goes in v4:
time: 78.7 us; the launch traced here: 78.4 us
  Pallas kernels  77.6 us (99%)
  between operations  0.84 us (1%)
    pallas_call x1, Pallas kernels, block(): pl.pallas_call(functools.partial(block_kernel, mesh_sizes, images), out_s...  72.3 us
    pallas_call x1, Pallas kernels, store(): pl.pallas_call(functools.partial(store_kernel, total_rows, count), out_sh...  5.26 us

profile of v4, /device:TPU:0, one launch (start us, length us, event | category | flops | bytes accessed | tf_op | source)
XLA Modules:
  0.0 78.4 jit_solution(1479382788915602793)
XLA Ops:
  0.7 72.3 %block.1 = (f32[3,136,384]{2,1,0:T(8,128)S(1)}, f32[3,136,384]{2,1,0:T(8,128)S(1)}, f32[5,8,384]{2,1,0:T(8,128)S(1)}, f32[3,8,192]{2,1,0:T(8,128)S(1)}, f32[8,19...) custom-call(s32[3,1088]{1,0:T(4,128)} %bitcast.40, ...), custom_call_target="tpu_custom_call" | custom-call | tf_op jit(solution)/shard_map/block/pallas_call | solution.py:988
  73.0 5.3 %store.1 = (f32[3,136,384]{2,1,0:T(8,128)}, f32[3,136,384]{2,1,0:T(8,128)}, f32[4,384]{1,0:T(4,128)}, f32[2,512]{1,0:T(2,128)}, f32[4,384]{1,0:T(4,128)}, /*inde...) custom-call(f32[3,136,384]{2,1,0:T(8,128)S(1)} %get-tuple-element.72, ...), custom_call_target="tpu_custom_call" | custom-call | tf_op jit(solution)/shard_map/store/pallas_call | solution.py:179

commit v5 on v4

--- a/solution.py
+++ b/solution.py
@@ -133,7 +133,7 @@
     squares, factor_left, factor_qkv, factor_out, factor_gate_up, factor_down = rest[:6]
     fulls, moments, weights = rest[6:10], rest[10:14], rest[14:18]
     targets, rest = rest[18 : 18 + plain], rest[18 + plain :]
-    results, branch_rms, fresh, sems = rest[:12], rest[12], rest[13:25], rest[25]
+    results, branch_rms, fresh, roots_kept, sems = rest[:12], rest[12], rest[13:25], rest[25], rest[26]
     copies = [
         pltpu.make_async_copy(source, target, sems.at[number])
         for number, (source, target) in enumerate(zip(sources, targets))
@@ -154,6 +154,12 @@
             copy.start()
             copies.append(copy)
 
+    roots = jnp.sqrt(jnp.sum(squares[...], -1, keepdims=True) / total_rows)
+    for index in range(2):
+        roots_kept[index] = roots[index, 0]
+    copies.append(pltpu.make_async_copy(roots_kept, branch_rms, sems.at[len(copies)]))
+    copies[-1].start()
+
     def product(rows, columns):
         return dot(rows.astype(BF), columns.astype(BF), TN)
 
@@ -164,9 +170,6 @@
     settle(1, product(triple_second(factor_out[...]), lefts[1]), lambda ref: ref)
     for index in range(3):
         settle(0, product(triple_second(factor_qkv[index]), lefts[0]), lambda ref: ref.at[index])
-    roots = jnp.sqrt(jnp.sum(squares[...], -1, keepdims=True) / total_rows)
-    for index in range(2):
-        branch_rms[index] = roots[index, 0]
     for copy in copies:
         copy.wait()
 
@@ -180,10 +183,11 @@
         functools.partial(store_kernel, total_rows, count),
         out_shape=[*shapes, jax.ShapeDtypeStruct((2,), F32)],
         in_specs=[vmem] * (count + 1 + len(factors) + 12),
-        out_specs=[*[pl.BlockSpec(memory_space=pltpu.HBM)] * len(shapes), pl.BlockSpec(memory_space=pltpu.SMEM)],
+        out_specs=[pl.BlockSpec(memory_space=pltpu.HBM)] * (len(shapes) + 1),
         scratch_shapes=[
             *[pltpu.VMEM(array.shape, F32) for array in matrices],
-            pltpu.SemaphoreType.DMA((count + 21,)),
+            pltpu.SMEM((2,), F32),
+            pltpu.SemaphoreType.DMA((count + 22,)),
         ],
         compiler_params=pltpu.CompilerParams(vmem_limit_bytes=24 * 2**20),
         name="store",
@@ -244,11 +248,13 @@
 
 
 def block_kernel(sizes, images, *refs):
+    smalls = refs[0:9]
     (
-        keep, norm_pack, inner_pack, moment_norm, moment_inner, basis_qkv, basis_out, basis_gate_up, basis_down,
         tokens_hbm, w_qkv_hbm, w_out_hbm, w_gate_up_hbm, w_down_hbm, out_grad_hbm,
         error_qkv_hbm, error_out_hbm, error_gate_up_hbm, error_down_hbm,
         moment_qkv_hbm, moment_out_hbm, moment_gate_up_hbm, moment_down_hbm,
+    ) = refs[9:23]
+    (
         residual, input_grad, factor_left, factor_qkv, factor_out, factor_gate_up, factor_down,
         full_qkv, full_out, full_gate_up, full_down,
         moment_qkv, moment_out, moment_gate_up, moment_down, new_moment_norm, new_moment_inner,
@@ -259,7 +265,7 @@
         slim_rows, grad_middle, wide_rows, wide_rows_send, grad_down, queries_t,
         grad_attended, grad_attended_send, grad_attended_all, grad_query, grad_query_low, grad_pairs,
         *rest,
-    ) = refs
+    ) = refs[23:]
     pairs_send, pairs_x, pairs_y, relay_x, relay_y = rest[0:5]
     ( grad_one, grad_one_recv, sum_query, sum_pairs, inner_sums, inner_recv,
         tokens, out_grad, mask, cosine, sine, extra, kept_rows, late_sum, thin_query, thin_pairs,
@@ -268,7 +274,9 @@
         local_sems, one_send, one_recv, weight_send, weight_recv, pair_send, pair_recv,
         att_send, att_recv, datt_send, datt_recv, rows_send, rows_recv, back_send, back_recv,
         final_send, final_recv, low_send, low_recv,
+        keep, norm_pack, inner_pack, moment_norm, moment_inner, basis_qkv, basis_out, basis_gate_up, basis_down,
     ) = rest[5:]
+    copied = (keep, norm_pack, inner_pack, moment_norm, moment_inner, basis_qkv, basis_out, basis_gate_up, basis_down)
     nd, ns, nt = sizes
     me_t, me_s = lax.axis_index("tensor"), lax.axis_index("seq")
     other = 1 - me_t
@@ -299,11 +307,11 @@
                 (error_qkv_hbm, full_qkv), (error_out_hbm, full_out),
                 (error_gate_up_hbm, full_gate_up), (error_down_hbm, full_down),
                 (moment_qkv_hbm, moment_qkv), (moment_out_hbm, moment_out),
-                (moment_gate_up_hbm, moment_gate_up), (moment_down_hbm, moment_down),
+                (moment_gate_up_hbm, moment_gate_up), (moment_down_hbm, moment_down), *zip(smalls, copied),
             )
         )
     ]
-    for load in loads[0:2]:
+    for load in (loads[15], loads[0], loads[1]):
         load.start()
 
     def to_partner(source, target, send, receive):
@@ -396,10 +404,11 @@
             inner_sums.at[other], inner_recv, final_send.at[images], final_recv.at[images]
         )
 
+
+    cosine[...], sine[...] = angle_tables(me_s * seq_rows, seq_rows)
+    loads[15].wait()
     gain_one, bias_one = norm_pack[0:1], norm_pack[1:2]
     gain_two, bias_two = norm_pack[2:3], norm_pack[3:4]
-
-    cosine[...], sine[...] = angle_tables(me_s * seq_rows, seq_rows)
     loads[0].wait()
     for image in range(images):
         normed, _, _ = norm_parts(tokens[image].astype(F32), gain_one, bias_one)
@@ -407,7 +416,7 @@
         if image == 0:
             pl.semaphore_wait(barrier, (nt - 1) + (ns - 1) + (nd - 1))
         one_copy(image).start()
-    for load in loads[2:]:
+    for load in (*loads[2:5], loads[14], *loads[16:23], *loads[5:14]):
         load.start()
     loads[1].wait()
 
@@ -441,6 +450,8 @@
 
     lax.fori_loop(0, images, project, 0)
 
+    for load in (loads[14], *loads[16:23]):
+        load.wait()
     for load in loads[2:5]:
         load.wait()
     out_low[me_t] = jnp.concatenate([pad, w_out[...].astype(BF)], 0)
@@ -522,9 +533,9 @@
         score(2)
         mixed = [mix(0)]
         chances(1)
+        chances(2)
         await_pairs(image, 2)
         mixed.append(mix(1))
-        chances(2)
         mixed.append(mix(2))
         attended[:, 0:128] = half_of(mixed[0], 1)
         attended[:, 128:256] = halves_of(mixed[1], mixed[2])
@@ -539,6 +550,9 @@
 
         @pl.when(image == 1)
         def _():
+            for load in loads[7:10]:
+                load.wait()
+            weights(0)
             forward_pairs(2, 0)
 
         @pl.when(image == 2)
@@ -575,9 +589,6 @@
         @pl.when(image == 0)
         def _():
             forward_pairs(1, 1)
-            forward_pairs(1, 2)
-            for tile in range(3):
-                send_pairs(2, tile)
 
         cotangent = out_grad[image, own_rows] * mask[image, own_rows]
         grads = [grad_down[image, index] for index in range(2)]
@@ -619,6 +630,12 @@
         for copy in row_copies(image):
             copy.start()
 
+        @pl.when(image == 0)
+        def _():
+            forward_pairs(1, 2)
+            for tile in range(3):
+                send_pairs(2, tile)
+
     def attend_back(image):
         datt_copy(image).wait_recv()
         grad_attended_all[...] = jnp.concatenate(
@@ -689,18 +706,21 @@
     def weights(image):
         for copy in row_copies(image):
             copy.wait_recv()
+        parts = []
         for half in range(2):
             place = slice(half * own, half * own + own)
             grad_branch = (out_grad[image, place] * mask[image, place]).astype(BF)
             normed_three, grad_gate, grad_up = (
                 wide_rows[half, image, :, number * wide : number * wide + wide] for number in range(3)
             )
-            full_down[...] += dot(normed_three, grad_branch, TN) * scale
             rows_two, low = slim_rows[half, image, :, 0:width], slim_rows[half, image, :, width:]
-            full_gate_up[0] += dot(rows_two, grad_gate, TN) * scale
-            full_gate_up[1] += dot(rows_two, grad_up, TN) * scale
             mixed = attended_low[image].astype(F32)[place].astype(BF)
-            full_out[...] += dot(mixed, low, TN)[256 - narrow :] * scale
+            parts.append(((normed_three, grad_branch), (rows_two, grad_gate), (rows_two, grad_up), (mixed, low)))
+        down, gate, up, out = (dot(*first, TN) + dot(*second, TN) for first, second in zip(*parts))
+        full_down[...] += down * scale
+        full_gate_up[0] += gate * scale
+        full_gate_up[1] += up * scale
+        full_out[...] += out[256 - narrow :] * scale
 
     def stage(step, carry):
         @pl.when(step < images)
@@ -709,9 +729,7 @@
 
         @pl.when(step == images)
         def _():
-            for load in loads[7:10]:
-                load.wait()
-            lax.fori_loop(0, images - 1, lambda image, rest: weights(image) or rest, 0)
+            weights(1)
             relay_back(1)
 
         @pl.when(step >= 1)
@@ -973,7 +991,7 @@
         *[pltpu.VMEM((size, RANK, wide), BF) for size in (4, ns, nd, ns)],
         *[pltpu.VMEM((size, 3 * RANK, narrow), BF) for size in (ns, nd)],
         *[pltpu.VMEM((size, RANK, wide), F32) for size in (ns, nd)],
-        dma((14,)),
+        dma((23,)),
         *[dma((images,))] * 2,
         *[dma((4,))] * 2,
         dma((images,)),
@@ -984,11 +1002,12 @@
         dma((images, 3)),
         *[dma((images + 1,))] * 2,
         *[dma((16,))] * 2,
+        *[pltpu.VMEM(array.shape, array.dtype) for array in small],
     ]
     return pl.pallas_call(
         functools.partial(block_kernel, mesh_sizes, images),
         out_shape=outs,
-        in_specs=[vmem] * len(small) + [hbm_spec] * len(hbm),
+        in_specs=[hbm_spec] * (len(small) + len(hbm)),
         out_specs=[vmem] * len(outs),
         scratch_shapes=scratch,
         compiler_params=pltpu.CompilerParams(

time: 78.7 us -> 77.6 us (0.986)
  Pallas kernels: 77.6 us -> 76.6 us
where the time goes in v5:
time: 77.6 us; the launch traced here: 77.4 us
  Pallas kernels  76.6 us (99%)
  between operations  0.84 us (1%)
    pallas_call x1, Pallas kernels, block(): pl.pallas_call(functools.partial(block_kernel, mesh_sizes, images), out_s...  71.9 us
    pallas_call x1, Pallas kernels, store(): pl.pallas_call(functools.partial(store_kernel, total_rows, count), out_sh...  4.71 us

profile of v5, /device:TPU:0, one launch (start us, length us, event | category | flops | bytes accessed | tf_op | source)
XLA Modules:
  0.0 77.4 jit_solution(1955665074362113370)
XLA Ops:
  0.7 71.9 %block.1 = (f32[3,136,384]{2,1,0:T(8,128)S(1)}, f32[3,136,384]{2,1,0:T(8,128)S(1)}, f32[5,8,384]{2,1,0:T(8,128)S(1)}, f32[3,8,192]{2,1,0:T(8,128)S(1)}, f32[8,19...) custom-call(s32[3,1088]{1,0:T(4,128)} %bitcast.40, ...), custom_call_target="tpu_custom_call" | custom-call | tf_op jit(solution)/shard_map/block/pallas_call | solution.py:1007
  72.6 4.7 %store.1 = (f32[3,136,384]{2,1,0:T(8,128)}, f32[3,136,384]{2,1,0:T(8,128)}, f32[4,384]{1,0:T(4,128)}, f32[2,512]{1,0:T(2,128)}, f32[4,384]{1,0:T(4,128)}, /*inde...) custom-call(f32[3,136,384]{2,1,0:T(8,128)S(1)} %get-tuple-element.72, ...), custom_call_target="tpu_custom_call" | custom-call | tf_op jit(solution)/shard_map/store/pallas_call | solution.py:182

commit v6 on v5

--- a/solution.py
+++ b/solution.py
@@ -75,26 +75,35 @@
         self.whole.wait()
 
 
+def peers_of(axis, size):
+    me = lax.axis_index(axis)
+    if size == 4 and axis == "dp":
+        upper = lax.div(me, 2)
+        return [3 - 3 * upper, 2 - upper, 1 - me + 4 * upper]
+    if size == 4 and axis == "seq":
+        return [3 - me, me + 1 - 2 * lax.rem(me, 2), lax.rem(me + 2, 4)]
+    return [lax.rem(me + step, size) for step in range(1, size)]
+
+
 def exchange(axes, sizes, buffer, send, receive, pieces=None):
-    count = math.prod(sizes)
-    place = 0
-    for axis, size in zip(axes, sizes):
-        place = place * size + lax.axis_index(axis)
-    for step in range(1, count):
-        peer = lax.rem(place + step, count)
-        device, rest = {}, peer
-        for axis, size in reversed(tuple(zip(axes, sizes))):
-            device[axis] = lax.rem(rest, size)
-            rest = lax.div(rest, size)
+    own = [lax.axis_index(axis) for axis in axes]
+    place = own[0]
+    devices = [{axes[0]: peer} for peer in peers_of(axes[0], sizes[0])]
+    if len(axes) == 2:
+        place = own[0] * sizes[1] + own[1]
+        others = peers_of(axes[1], sizes[1])
+        devices = [{**device, axes[1]: peer} for device in devices for peer in (own[1], *others)]
+        devices += [{axes[0]: own[0], axes[1]: peer} for peer in others]
+    for device in devices:
         pltpu.make_async_remote_copy(
-            src_ref=buffer.at[place] if pieces is None else pieces.at[peer],
+            src_ref=buffer.at[place] if pieces is None else pieces.at[device[axes[0]]],
             dst_ref=buffer.at[place],
             send_sem=send,
             recv_sem=receive,
             device_id=device,
             device_id_type=MESH,
         ).start()
-    return Moves(buffer.at[0 : count - 1], send, receive, device)
+    return Moves(buffer.at[0 : len(devices)], send, receive, devices[0])
 
 
 def arrive(moves):

time: 77.6 us -> 77 us (level)
  no operation moved by 1% of the time
where the time goes in v6:
time: 77 us; the launch traced here: 76.8 us
  Pallas kernels  75.9 us (99%)
  between operations  0.84 us (1%)
    pallas_call x1, Pallas kernels, block(): pl.pallas_call(functools.partial(block_kernel, mesh_sizes, images), out_s...  71.2 us
    pallas_call x1, Pallas kernels, store(): pl.pallas_call(functools.partial(store_kernel, total_rows, count), out_sh...  4.71 us

profile of v6, /device:TPU:0, one launch (start us, length us, event | category | flops | bytes accessed | tf_op | source)
XLA Modules:
  0.0 76.8 jit_solution(16742110728247668192)
XLA Ops:
  0.7 71.2 %block.1 = (f32[3,136,384]{2,1,0:T(8,128)S(1)}, f32[3,136,384]{2,1,0:T(8,128)S(1)}, f32[5,8,384]{2,1,0:T(8,128)S(1)}, f32[3,8,192]{2,1,0:T(8,128)S(1)}, f32[8,19...) custom-call(s32[3,1088]{1,0:T(4,128)} %bitcast.40, ...), custom_call_target="tpu_custom_call" | custom-call | tf_op jit(solution)/shard_map/block/pallas_call | solution.py:1016
  71.9 4.7 %store.1 = (f32[3,136,384]{2,1,0:T(8,128)}, f32[3,136,384]{2,1,0:T(8,128)}, f32[4,384]{1,0:T(4,128)}, f32[2,512]{1,0:T(2,128)}, f32[4,384]{1,0:T(4,128)}, /*inde...) custom-call(f32[3,136,384]{2,1,0:T(8,128)S(1)} %get-tuple-element.72, ...), custom_call_target="tpu_custom_call" | custom-call | tf_op jit(solution)/shard_map/store/pallas_call | solution.py:191
